TPU v7x, 32 devices: a whole 2x2x4 slice. The times are simulated.
32 devices in a mesh: seq: 8 (over z, y), tp: 4 (over x, core).
Axes of the slice: x: 2, y: 2, z: 4, core: 2. Of those that a mesh axis runs over, the one named last changes fastest.
Arguments:
- latents: bfloat16 [1024, 3072], P('seq', 'tp'), may hold values from -6 to 6
- lengths: int32 [2], replicated, may hold values from 1 to 768, 1024 in all
- t_index: int32 [2], replicated, may hold values from 0 to 6
- mod_scale: float32 [3072], replicated, may hold values from -2 to 2
- q_weight: bfloat16 [3072, 2048], P(None, 'tp'), may hold values from -0.109375 to 0.109375
- k_weight: bfloat16 [3072, 2048], P(None, 'tp'), may hold values from -0.109375 to 0.109375
- v_weight: bfloat16 [3072, 2048], P(None, 'tp'), may hold values from -0.109375 to 0.109375
- out_weight: bfloat16 [2048, 3072], P('tp'), may hold values from -0.1875 to 0.1875
- q_gain: float32 [128], replicated, may hold values from 0.6 to 2.4
- k_gain: float32 [128], replicated, may hold values from 0.6 to 2.4
- student_weight: bfloat16 [3072, 3072], P('tp'), may hold values from -0.15625 to 0.15625
Outputs:
- target: bfloat16 [1024, 3072], P('seq', 'tp')
- student_velocity: bfloat16 [1024, 3072], P('seq', 'tp')
- loss: float32 [], replicated
Inputs may be any that keep to these rules, and one draw needn't show every extreme that they name: lengths sum to 1024.
All inputs are finite; a program needn't handle non-finite values.
Results may differ from a plain program's by a relative error of at most 0.024.
Values may be sent and summed in bfloat16 or wider, within the bound.
No kernel may reach another device: no remote copies, remote signals or barrier semaphores. Data moves between devices by JAX's collectives and lax.ppermute only.
A program may use at most 64 MiB of HBM per device.

v0:
```python
import math

import jax
import jax.numpy as jnp
from jax import lax
from jax.sharding import PartitionSpec as P

TGRID = 8


epsilon = 1e-06
kinetic_weight = 0.1


def image_index(positions, image_ends):
    return jnp.sum((positions[:, None] >= image_ends[None, :]).astype(jnp.int32), axis=1)


def head_norm(projected, gain):
    shaped = projected.reshape(projected.shape[0], -1, gain.shape[0])
    normed = shaped * lax.rsqrt(jnp.mean(shaped * shaped, axis=-1, keepdims=True) + epsilon) * gain
    return normed.astype(jnp.bfloat16)


def teacher(
    state, times, query_image, image_ends, mod_scale, q_weight, k_weight, v_weight, q_gain, k_gain
):
    row_count = state.shape[0]
    head_dim = q_gain.shape[0]
    state32 = state.astype(jnp.float32)
    normed = state32 * lax.rsqrt(jnp.mean(state32 * state32, axis=1, keepdims=True) + epsilon)
    hidden = (normed * (1.0 + times[:, None] * mod_scale[None, :])).astype(jnp.bfloat16)
    queries = head_norm(jnp.dot(hidden, q_weight, preferred_element_type=jnp.float32), q_gain)
    key_rows = head_norm(jnp.dot(hidden, k_weight, preferred_element_type=jnp.float32), k_gain)
    key_rows = key_rows.reshape(row_count, -1)
    value_rows = jnp.dot(hidden, v_weight, preferred_element_type=jnp.float32).astype(jnp.bfloat16)
    heads_here = queries.shape[1]
    score_scale = 1.0 / math.sqrt(head_dim)

    def attend(carry, key_block, value_block):
        running_max, running_total, running_sum = carry
        count = key_block.shape[0]
        key_image = image_index(jnp.arange(count, dtype=jnp.int32), image_ends)
        key_heads = key_block.reshape(count, heads_here, head_dim)
        value_heads = value_block.reshape(count, heads_here, head_dim)
        same_image = (query_image[:, None] == key_image[None, :])[:, None, :]
        scores = (
            jnp.einsum("qhd,khd->qhk", queries, key_heads, preferred_element_type=jnp.float32)
            * score_scale
        )
        scores = jnp.where(same_image, scores, -1e30)
        new_max = jnp.maximum(running_max, jnp.max(scores, axis=2))
        weights = jnp.where(same_image, jnp.exp(scores - new_max[:, :, None]), 0.0)
        new_total = jnp.sum(weights, axis=2)
        product = jnp.einsum(
            "qhk,khd->qhd",
            weights.astype(jnp.bfloat16),
            value_heads,
            preferred_element_type=jnp.float32,
        )
        return (new_max, new_total, product)

    start_carry = (
        jnp.full((row_count, heads_here), -1e30, jnp.float32),
        jnp.zeros((row_count, heads_here), jnp.float32),
        jnp.zeros((row_count, heads_here, head_dim), jnp.float32),
    )
    offset = jnp.int32(0)
    key_block = lax.all_gather(key_rows, "seq", axis=0, tiled=True)
    value_block = lax.all_gather(value_rows, "seq", axis=0, tiled=True)
    count = key_block.shape[0]
    first_image = image_index(jnp.reshape(offset, (1,)), image_ends)[0]
    last_image = image_index(jnp.reshape(offset + count - 1, (1,)), image_ends)[0]
    touches = jnp.logical_and(first_image <= query_image[-1], last_image >= query_image[0])
    final_max, final_total, final_sum = lax.cond(
        touches,
        lambda inner: attend(inner, key_block, value_block),
        lambda inner: inner,
        start_carry,
    )
    mixed = (final_sum / final_total[:, :, None]).astype(jnp.bfloat16).reshape(row_count, -1)
    return (mixed, hidden)


def on_device(
    latents,
    lengths,
    t_index,
    mod_scale,
    q_weight,
    k_weight,
    v_weight,
    out_weight,
    q_gain,
    k_gain,
    student_weight,
):
    row_count, width_here = latents.shape
    tp_index = lax.axis_index("tp")
    image_ends = jnp.cumsum(lengths)
    row_offset = lax.axis_index("seq") * row_count
    query_image = image_index(row_offset + jnp.arange(row_count, dtype=jnp.int32), image_ends)
    one_hot = (
        query_image[:, None] == jnp.arange(lengths.shape[0], dtype=jnp.int32)[None, :]
    ).astype(jnp.float32)
    start_times = jnp.sum(one_hot * (t_index.astype(jnp.float32) / TGRID)[None, :], axis=1)
    step_size = 1.0 / TGRID
    whole_rows = lax.all_gather(latents, "tp", axis=1, tiled=True)
    velocities = []
    first_hidden = whole_rows
    state_shard = latents
    for euler_index in range(2):
        if euler_index == 1:
            whole_rows = lax.all_gather(state_shard, "tp", axis=1, tiled=True)
        mixed, hidden = teacher(
            whole_rows,
            start_times + euler_index * step_size,
            query_image,
            image_ends,
            mod_scale,
            q_weight,
            k_weight,
            v_weight,
            q_gain,
            k_gain,
        )
        if euler_index == 0:
            first_hidden = hidden
        partial_value = jnp.dot(mixed, out_weight, preferred_element_type=jnp.float32)
        velocity = lax.psum_scatter(
            partial_value.astype(jnp.bfloat16), "tp", scatter_dimension=1, tiled=True
        )
        velocities.append(velocity)
        state_shard = (
            latents.astype(jnp.float32) + step_size * velocity.astype(jnp.float32)
        ).astype(jnp.bfloat16)
    columns = lax.dynamic_slice_in_dim(first_hidden, tp_index * width_here, width_here, 1)
    student_terms = jnp.dot(columns, student_weight, preferred_element_type=jnp.float32)
    student_velocity = lax.psum_scatter(
        student_terms.astype(jnp.bfloat16), "tp", scatter_dimension=1, tiled=True
    )
    target = (0.5 * (velocities[0].astype(jnp.float32) + velocities[1].astype(jnp.float32))).astype(
        jnp.bfloat16
    )
    student32 = student_velocity.astype(jnp.float32)
    residual = student32 - target.astype(jnp.float32)
    per_token = jnp.sum(residual * residual, axis=1) + kinetic_weight * jnp.sum(
        student32 * student32, axis=1
    )
    image_part = jnp.sum(one_hot * per_token[:, None], axis=0)
    image_sum = lax.psum(image_part, ("seq", "tp"))
    loss = jnp.mean(image_sum / (lengths.astype(jnp.float32) * mod_scale.shape[0]))
    return (target, student_velocity, loss)


def solution(mesh):
    placed = (
        P("seq", "tp"),
        P(),
        P(),
        P(),
        P(None, "tp"),
        P(None, "tp"),
        P(None, "tp"),
        P("tp", None),
        P(),
        P(),
        P("tp", None),
    )
    return jax.shard_map(
        on_device,
        mesh=mesh,
        in_specs=placed,
        out_specs=(P("seq", "tp"), P("seq", "tp"), P()),
        check_vma=False,
    )
```

profile of v0, /device:TPU:0, one launch (start us, length us, event | category | flops | bytes accessed | tf_op | source)
XLA Modules:
  0.0 336.3 jit_solution(12734759485271382639)
XLA Ops:
  8.1 10.4 %all_gather.18 = bf16[128,3072]{1,0:T(8,128)(2,1)S(1)} all-gather(bf16[128,768]{1,0:T(8,128)(2,1)} %param.15), channel_id=1, replica_groups=mesh['seq'=8,'tp'=4] {'tp'}, dimensions={1}, use_global_device_ids=true | all-gather | bytes 983040 | tf_op jit(solution)/shard_map/all_gather | solution.py:108
  21.2 1.5 fusion.38
  23.6 3.1 convolution_convert_fusion.4
  26.8 3.4 %fusion.70 = (f32[128,512]{1,0:T(8,128)}, f32[128,512]{1,0:T(8,128)S(1)}) fusion(bf16[128,3072]{1,0:T(8,128)(2,1)} %copy-done.1, bf16[3072,512]{1,0:T(8,128)(2,1)} %param.20), kind=kOutput, calls=%fused_computation.115 | convolution fusion | flops 402718720 | bytes 4456448 | tf_op jit(solution)/shard_map/dot_general | solution.py:34
  30.2 1.8 mul.218
  32.0 1.2 reduce_sum.175
  38.0 2.7 fusion.72
  41.5 1.2 multiply_reduce_fusion.1
  42.9 25.1 %all-gather.7.cloned.1.call-done = bf16[1024,512]{1,0:T(8,128)(2,1)} async-done(((bf16[128,512]{1,0:T(8,128)(2,1)}), bf16[1024,512]{1,0:T(8,128)(2,1)}) %all-gather.7.cloned.1.call-update) | async-done | bytes 1048592 | tf_op jit(solution)/shard_map/all_gather | solution.py:70
  68.0 41.7 %all-gather.5.cloned.1.call-done = bf16[1024,512]{1,0:T(8,128)(2,1)} async-done(((bf16[128,512]{1,0:T(8,128)(2,1)}), bf16[1024,512]{1,0:T(8,128)(2,1)}) %all-gather.5.cloned.1.call-update) | async-done | bytes 1048592 | tf_op jit(solution)/shard_map/all_gather | solution.py:69
  109.7 6.0 %conditional.2 = (f32[128,4]{0,1:T(4,128)S(1)}, f32[128,4,128]{0,2,1:T(8,128)S(1)}) conditional(s32[]{:T(128)} %convert_element_type.124, () %tuple.24, (s32[128]{0:T(128)S(1)}, s32[2]{0:T(128)}, bf16[1024,512]{1,0:T(8,128)(2,1)}, bf16[128,4,128]{2,0,1:T(8,128)(2,1)S(1)}, bf16[1024,512]{1,0:T(8,128)(2,1)}) %tuple.59), branch_computations={%region_8.9_spmd, %region_9.13_spmd} | conditional | flops 275386880 | bytes 14045748 | solution.py:75
  110.7 1.7 fusion
  112.5 1.6 convolution_bitcast_fusion
  115.8 1.5 convolution_convert_fusion.1
  117.4 22.0 %reduce-scatter.4.cloned.1.call-done = bf16[128,768]{1,0:T(8,128)(2,1)} async-done(((bf16[128,3072]{1,0:T(8,128)(2,1)}), bf16[128,768]{1,0:T(8,128)(2,1)}) %reduce-scatter.4.cloned.1.call-update) | async-done | bytes 196624 | tf_op jit(solution)/shard_map/reduce_scatter | solution.py:130
  140.4 8.0 %all_gather.21 = bf16[128,3072]{1,0:T(8,128)(2,1)S(1)} all-gather(bf16[128,768]{1,0:T(8,128)(2,1)S(1)} %fusion.43), channel_id=1, replica_groups=mesh['seq'=8,'tp'=4] {'tp'}, dimensions={1}, use_global_device_ids=true | all-gather | bytes 983040 | tf_op jit(solution)/shard_map/all_gather | solution.py:114
  149.3 3.2 convolution_convert_fusion.3
  152.6 3.6 %fusion.71 = (f32[128,512]{1,0:T(8,128)}, f32[128,512]{1,0:T(8,128)}) fusion(bf16[3072,512]{1,0:T(8,128)(2,1)} %param.20, bf16[128,3072]{1,0:T(8,128)(2,1)} %copy-done.3, f32[128]{0:T(128)S(1)} %broadcast_add_fusion, f32[128]{0:T(128)S(1)} %add_rsqrt_fusion.4, f32[3072]{0:T(1024)S(1)} %copy-done.6), kind=kOutput, calls=%fused_computation.116 | convolution fusion | flops 405078016 | bytes 4469760 | tf_op jit(solution)/shard_map/dot_general | solution.py:34
  157.6 1.6 fusion.50
  159.4 4.2 %convolution_convert_fusion.2 = bf16[128,3072]{1,0:T(8,128)(2,1)} fusion(bf16[768,3072]{1,0:T(8,128)(2,1)} %param.25, bf16[128,3072]{1,0:T(8,128)(2,1)} %copy-done.1, s32[]{:T(128)S(6)} %select_n.16), kind=kOutput, calls=%fused_computation.48 | convolution fusion | flops 604372992 | bytes 5701636 | tf_op jit(solution)/shard_map/dot_general | solution.py:138
  163.7 3.5 %fusion.64 = f32[128,512]{1,0:T(8,128)} fusion(bf16[3072,512]{1,0:T(8,128)(2,1)} %param.19, bf16[128,3072]{1,0:T(8,128)(2,1)} %copy-done.3, f32[128]{0:T(128)S(1)} %broadcast_add_fusion, f32[128]{0:T(128)S(1)} %add_rsqrt_fusion.4, f32[3072]{0:T(1024)S(1)} %copy-done.6), kind=kOutput, calls=%fused_computation.112 | convolution fusion | flops 405012480 | bytes 4207616 | tf_op jit(solution)/shard_map/dot_general | solution.py:33
  168.5 1.1 fusion.54
  169.6 23.9 %all-gather.11.cloned.1.call-done = bf16[1024,512]{1,0:T(8,128)(2,1)} async-done(((bf16[128,512]{1,0:T(8,128)(2,1)}), bf16[1024,512]{1,0:T(8,128)(2,1)}) %all-gather.11.cloned.1.call-update) | async-done | bytes 1048592 | tf_op jit(solution)/shard_map/all_gather | solution.py:70
  193.5 41.6 %all-gather.9.cloned.1.call-done = bf16[1024,512]{1,0:T(8,128)(2,1)} async-done(((bf16[128,512]{1,0:T(8,128)(2,1)}), bf16[1024,512]{1,0:T(8,128)(2,1)}) %all-gather.9.cloned.1.call-update) | async-done | bytes 1048592 | tf_op jit(solution)/shard_map/all_gather | solution.py:69
  235.1 5.3 %conditional.3 = (f32[128,4]{0,1:T(4,128)S(1)}, f32[128,4,128]{0,2,1:T(8,128)S(1)}) conditional(s32[]{:T(128)} %convert_element_type.124, () %tuple.26, (s32[128]{0:T(128)S(1)}, s32[2]{0:T(128)S(1)}, bf16[1024,512]{1,0:T(8,128)(2,1)}, bf16[128,4,128]{2,0,1:T(8,128)(2,1)S(1)}, bf16[1024,512]{1,0:T(8,128)(2,1)}) %tuple.60), branch_computations={%region_17.18_spmd, %region_18.0_spmd} | conditional | flops 275386880 | bytes 14045748 | solution.py:75
  235.4 1.8 fusion.18
  237.2 1.6 convolution_bitcast_fusion.1
  240.4 1.5 convolution_convert_fusion
  242.0 18.1 %reduce-scatter.8.cloned.1.call-done = bf16[128,768]{1,0:T(8,128)(2,1)} async-done(((bf16[128,3072]{1,0:T(8,128)(2,1)}), bf16[128,768]{1,0:T(8,128)(2,1)}) %reduce-scatter.8.cloned.1.call-update) | async-done | bytes 196624 | tf_op jit(solution)/shard_map/reduce_scatter | solution.py:139
  260.0 25.8 %reduce-scatter.6.cloned.1.call-done = bf16[128,768]{1,0:T(8,128)(2,1)} async-done(((bf16[128,3072]{1,0:T(8,128)(2,1)}), bf16[128,768]{1,0:T(8,128)(2,1)}) %reduce-scatter.6.cloned.1.call-update) | async-done | bytes 196624 | tf_op jit(solution)/shard_map/reduce_scatter | solution.py:130
  285.8 1.8 fusion.48
  287.8 39.3 %psum.7 = f32[2]{0:T(128)S(1)} all-reduce(f32[2]{0:T(128)S(1)} %select_reduce_fusion), channel_id=1, replica_groups=mesh['seq'=8,'tp'=4] {'seq','tp'}, use_global_device_ids=true, to_apply=%region_27.28 | all-reduce | flops 2 | bytes 16 | tf_op jit(solution)/shard_map/psum | solution.py:151
  (90 shorter events, 18.1 us)
Async XLA Ops:
  7.2 108.6 %copy-start = (bf16[512,3072]{1,0:T(8,128)(2,1)S(1)}, bf16[512,3072]{1,0:T(8,128)(2,1)}, u32[]{:S(2)}) copy-start(bf16[512,3072]{1,0:T(8,128)(2,1)} %param.22) | copy-start | bytes 9437188
  7.2 60.8 %all-gather.7.cloned.1.call-start = ((), (), s32[]{:S(2)}) async-start(), calls=%async_computation.4 | async-start | bytes 1179648 | tf_op jit(solution)/shard_map/all_gather | solution.py:70
  18.5 0.9 copy-start.2
  20.4 14.4 %copy-start.8 = (s32[2,1]{0,1:T(1,128)}, s32[2,1]{0,1:T(1,128)S(1)}, u32[]{:S(2)}) copy-start(s32[2,1]{0,1:T(1,128)S(1)} %reduce-window.4) | copy-start | bytes 28
  20.6 0.6 copy-start.10
  22.7 0.9 copy-start.1
  26.7 6.4 %copy-start.12 = (f32[128]{0:T(128)S(1)}, f32[128]{0:T(128)}, u32[]{:S(2)}) copy-start(f32[128]{0:T(128)} %param.24) | copy-start | bytes 1540
  26.7 83.0 %all-gather.5.cloned.1.call-start = ((), (), s32[]{:S(2)}) async-start(), calls=%async_computation.3 | async-start | bytes 1179648 | tf_op jit(solution)/shard_map/all_gather | solution.py:69
  34.1 105.3 %reduce-scatter.4.cloned.1.call-start = ((), (), s32[]{:S(2)}) async-start(), calls=%async_computation.5 | async-start | bytes 983040 | tf_op jit(solution)/shard_map/reduce_scatter | solution.py:130
  38.0 4.8 %copy-start.7 = (f32[128]{0:T(128)S(1)}, f32[128]{0:T(128)}, u32[]{:S(2)}) copy-start(f32[128]{0:T(128)} %param.23) | copy-start | bytes 1540
  109.7 2.8 copy-start.14
  115.8 1.6 copy-start.11
  115.8 23.6 %copy-start.5 = (bf16[128,768]{1,0:T(8,128)(2,1)S(1)}, bf16[128,768]{1,0:T(8,128)(2,1)}, u32[]{:S(2)}) copy-start(bf16[128,768]{1,0:T(8,128)(2,1)} %param.15) | copy-start | bytes 589828
  117.3 32.0 %copy-start.6 = (f32[3072]{0:T(1024)S(1)}, f32[3072]{0:T(1024)}, u32[]{:S(2)}) copy-start(f32[3072]{0:T(1024)} %param.18) | copy-start | bytes 36868
  117.3 76.2 %all-gather.11.cloned.1.call-start = ((), (), s32[]{:S(2)}) async-start(), calls=%async_computation.7 | async-start | bytes 1179648 | tf_op jit(solution)/shard_map/all_gather | solution.py:70
  148.4 0.9 copy-start.3
  152.5 82.5 %all-gather.9.cloned.1.call-start = ((), (), s32[]{:S(2)}) async-start(), calls=%async_computation.6 | async-start | bytes 1179648 | tf_op jit(solution)/shard_map/all_gather | solution.py:69
  159.3 100.7 %reduce-scatter.8.cloned.1.call-start = ((), (), s32[]{:S(2)}) async-start(), calls=%async_computation.9 | async-start | bytes 983040 | tf_op jit(solution)/shard_map/reduce_scatter | solution.py:139
  163.6 122.2 %reduce-scatter.6.cloned.1.call-start = ((), (), s32[]{:S(2)}) async-start(), calls=%async_computation.8 | async-start | bytes 983040 | tf_op jit(solution)/shard_map/reduce_scatter | solution.py:130
  163.7 71.4 %copy-start.9 = (s32[2,1]{0,1:T(1,128)S(1)}, s32[2,1]{0,1:T(1,128)}, u32[]{:S(2)}) copy-start(s32[2,1]{0,1:T(1,128)} %copy-done.8) | copy-start | bytes 28
  235.1 2.1 copy-start.13
  240.4 45.4 %copy-start.4 = (bf16[128,768]{1,0:T(8,128)(2,1)S(1)}, bf16[128,768]{1,0:T(8,128)(2,1)}, u32[]{:S(2)}) copy-start(bf16[128,768]{1,0:T(8,128)(2,1)} %reduce-scatter.4.cloned.1.call-done) | copy-start | bytes 589828
  240.4 86.6 %copy-start.15 = (s32[2]{0:T(128)S(1)}, s32[2]{0:T(128)}, u32[]{:S(2)}) copy-start(s32[2]{0:T(128)} %param.16) | copy-start | bytes 28
Sparse Core Ops, SparseCore 0:
  26.8 41.1 all-gather.6
  70.7 38.9 all-gather.4
  117.4 21.9 reduce-scatter.3
  152.6 40.8 all-gather.10
  196.0 38.9 all-gather.8
  238.0 21.9 reduce-scatter.7
  262.5 23.2 reduce-scatter.5
where the time goes:
time: 337 us; the launch traced here: 336 us
  waiting for transfers between devices  198 us (59%)
  blocking collectives  57.7 us (17%)
  matrix products  33.4 us (10%)
  between operations  18.7 us (6%)
  other arithmetic  16.8 us (5%)
  local copies, waits for them, and re-layouts  11 us (3%)
    all_gather x2, waiting for transfers between devices, teacher(): key_block = lax.all_gather(key_rows, 'seq', axis=0, tiled=True)  83.3 us
    all_gather x2, waiting for transfers between devices, teacher(): value_block = lax.all_gather(value_rows, 'seq', axis=0, tiled=True)  49 us
    reduce_scatter x2, waiting for transfers between devices, on_device(): lax.psum_scatter(partial_value.astype(jnp.bfloat16), 'tp', scatter_dimens...  47.8 us
    psum x1, blocking collectives, on_device(): image_sum = lax.psum(image_part, ('seq', 'tp'))  39.3 us
    reduce_scatter x1, waiting for transfers between devices, on_device(): lax.psum_scatter(student_terms.astype(jnp.bfloat16), 'tp', scatter_dimens...  18.1 us
    all_gather x1, blocking collectives, on_device(): whole_rows = lax.all_gather(latents, 'tp', axis=1, tiled=True)  10.4 us
    all_gather x1, blocking collectives, on_device(): whole_rows = lax.all_gather(state_shard, 'tp', axis=1, tiled=True)  8.03 us
    dot_general x2, matrix products, teacher(): jnp.dot(hidden, k_weight, preferred_element_type=jnp.float32)  7.02 us
  transfers between devices with their start and end apart: 7, of which 7 were waited for; matrix products, arithmetic and copies ran while one was open for 11% of the time, Pallas kernels for 0%

commit v1 on v0

v1 whole, which is shorter than its diff:
```python
import math

import jax
import jax.numpy as jnp
from jax import lax
from jax.sharding import PartitionSpec as P

TGRID = 8
epsilon = 1e-06
kinetic_weight = 0.1
F32, BF16 = jnp.float32, jnp.bfloat16


def image_index(positions, image_ends):
    return jnp.sum((positions[:, None] >= image_ends[None, :]).astype(jnp.int32), axis=1)


def swap(value, axis, size, mask):
    return lax.ppermute(value, axis, [(i, i ^ mask) for i in range(size)])


def bits_of(size):
    return [1 << b for b in range(size.bit_length() - 1)]


def gather_blocks(own, axis, size):
    blocks = {0: own}
    for bit in reversed(bits_of(size)):
        for k in list(blocks):
            blocks[k ^ bit] = swap(blocks[k], axis, size, bit)
    return [blocks[k] for k in range(size)]


def in_order(blocks, index):
    size = len(blocks)
    current = list(blocks)
    for bit in bits_of(size):
        flip = (index & bit) != 0
        current = [jnp.where(flip, current[k ^ bit], current[k]) for k in range(size)]
    return current


def reduce_blocks(terms, axis, size, keep_last):
    held = dict(enumerate(terms))
    bits = bits_of(size)
    for bit in bits:
        last = keep_last and bit == bits[-1]
        sent = {k: swap(held[k].astype(BF16), axis, size, bit) for k in held if last or k & bit}
        if last:
            held = {k: held[k].astype(BF16).astype(F32) + sent[k ^ bit].astype(F32) for k in held}
        else:
            held = {
                k: held[k].astype(BF16).astype(F32) + sent[k ^ bit].astype(F32)
                for k in held
                if not k & bit
            }
    return held


def head_norm(projected, gain):
    shaped = projected.reshape(projected.shape[0], -1, gain.shape[0])
    normed = shaped * lax.rsqrt(jnp.mean(shaped * shaped, axis=-1, keepdims=True) + epsilon) * gain
    return normed.astype(BF16)


def on_device(
    mesh_shape,
    latents,
    lengths,
    t_index,
    mod_scale,
    q_weight,
    k_weight,
    v_weight,
    out_weight,
    q_gain,
    k_gain,
    student_weight,
):
    n_seq, n_tp = mesh_shape["seq"], mesh_shape["tp"]
    row_count, width_here = latents.shape
    head_dim = q_gain.shape[0]
    heads_here = q_weight.shape[1] // head_dim
    tp_index = lax.axis_index("tp")
    seq_index = lax.axis_index("seq")
    image_ends = jnp.cumsum(lengths)
    score_scale = 1.0 / math.sqrt(head_dim)
    step_size = 1.0 / TGRID

    spread = math.gcd(heads_here, n_seq)
    groups = n_seq // spread
    heads_kept = heads_here // spread
    twisted = groups == 2 and spread >= 4
    group_index = seq_index // spread
    head_block = seq_index % spread
    if twisted:
        head_block = head_block ^ (group_index * 2)

    def rows_image(source):
        return image_index(source * row_count + jnp.arange(row_count, dtype=jnp.int32), image_ends)

    query_image = rows_image(seq_index)
    one_hot = (
        query_image[:, None] == jnp.arange(lengths.shape[0], dtype=jnp.int32)[None, :]
    ).astype(F32)
    start_times = jnp.sum(one_hot * (t_index.astype(F32) / TGRID)[None, :], axis=1)

    group_image = jnp.concatenate([rows_image(seq_index ^ m) for m in range(spread)])
    if groups == 2:
        partner_mask = spread ^ 2 if twisted else spread
        key_image = jnp.concatenate(
            [group_image] + [rows_image(seq_index ^ partner_mask ^ m) for m in range(spread)]
        )
    else:
        key_image = jnp.concatenate(
            [
                rows_image((seq_index % spread ^ m) + g * spread)
                for g in range(groups)
                for m in range(spread)
            ]
        )
    same_image = group_image[:, None] == key_image[None, :]

    def attention(queries, key_rows, value_rows):
        wide = heads_kept * head_dim
        packed = jnp.concatenate(
            [
                part.reshape(row_count, spread, 1, wide)
                for part in (queries, key_rows, value_rows)
            ],
            axis=2,
        )
        received = []
        for m in range(spread):
            piece = lax.dynamic_index_in_dim(packed, head_block ^ m, 1, keepdims=False)
            piece = piece.reshape(row_count, 3 * wide)
            received.append(piece if m == 0 else swap(piece, "seq", n_seq, m))
        own = jnp.concatenate(received, axis=0)
        group_q, group_kv = own[:, :wide], own[:, wide:]
        if groups == 2:
            other = swap(group_kv, "seq", n_seq, partner_mask)
            whole_kv = jnp.concatenate([group_kv, other], axis=0)
        elif groups == 1:
            whole_kv = group_kv
        else:
            whole_kv = lax.all_gather(
                group_kv,
                "seq",
                axis=0,
                tiled=True,
                axis_index_groups=[
                    [a + g * spread for g in range(groups)] for a in range(spread)
                ],
            )
        outs = []
        for h in range(heads_kept):
            cut = slice(h * head_dim, (h + 1) * head_dim)
            q_h, k_h = group_q[:, cut], whole_kv[:, :wide][:, cut]
            v_h = whole_kv[:, wide:][:, cut]
            scores = jnp.dot(q_h, k_h.T, preferred_element_type=F32) * score_scale
            scores = jnp.where(same_image, scores, -1e30)
            highest = jnp.max(scores, axis=1, keepdims=True)
            weights = jnp.where(same_image, jnp.exp(scores - highest), 0.0)
            totals = jnp.sum(weights, axis=1, keepdims=True)
            mixed = jnp.dot(weights.astype(BF16), v_h, preferred_element_type=F32)
            outs.append((mixed / totals).astype(BF16))
        result = jnp.concatenate(outs, axis=1) if len(outs) > 1 else outs[0]
        back = []
        for m in range(spread):
            piece = result[m * row_count : (m + 1) * row_count]
            back.append(piece if m == 0 else swap(piece, "seq", n_seq, m))
        return jnp.concatenate(in_order(back, head_block), axis=1)

    def terms_of(left, right):
        product = jnp.dot(left, right, preferred_element_type=F32)
        return [
            lax.dynamic_slice_in_dim(product, (tp_index ^ k) * width_here, width_here, 1)
            for k in range(n_tp)
        ]

    def teacher(state_blocks, times):
        state32 = jnp.concatenate(in_order(state_blocks, tp_index), axis=1).astype(F32)
        normed = state32 * lax.rsqrt(jnp.mean(state32 * state32, axis=1, keepdims=True) + epsilon)
        hidden = (normed * (1.0 + times[:, None] * mod_scale[None, :])).astype(BF16)
        queries = head_norm(jnp.dot(hidden, q_weight, preferred_element_type=F32), q_gain)
        key_rows = head_norm(jnp.dot(hidden, k_weight, preferred_element_type=F32), k_gain)
        value_rows = jnp.dot(hidden, v_weight, preferred_element_type=F32).astype(BF16)
        mixed = attention(queries, key_rows, value_rows)
        return terms_of(mixed, out_weight), hidden

    def step(block, velocity):
        return (block.astype(F32) + step_size * velocity.astype(F32)).astype(BF16)

    blocks = gather_blocks(latents, "tp", n_tp)
    terms, first_hidden = teacher(blocks, start_times)
    held = reduce_blocks(terms, "tp", n_tp, True)
    velocity0 = held[0].astype(BF16)
    moved = {k: step(blocks[k], held[k].astype(BF16)) for k in held}
    for bit in reversed(bits_of(n_tp)[:-1]):
        for k in list(moved):
            moved[k ^ bit] = swap(moved[k], "tp", n_tp, bit)
    terms, _ = teacher([moved[k] for k in range(n_tp)], start_times + step_size)
    velocity1 = reduce_blocks(terms, "tp", n_tp, False)[0].astype(BF16)

    columns = lax.dynamic_slice_in_dim(first_hidden, tp_index * width_here, width_here, 1)
    student = reduce_blocks(terms_of(columns, student_weight), "tp", n_tp, False)[0].astype(BF16)

    target = (0.5 * (velocity0.astype(F32) + velocity1.astype(F32))).astype(BF16)
    student32 = student.astype(F32)
    residual = student32 - target.astype(F32)
    per_token = jnp.sum(residual * residual, axis=1) + kinetic_weight * jnp.sum(
        student32 * student32, axis=1
    )
    image_sum = jnp.sum(one_hot * per_token[:, None], axis=0)
    for bit in bits_of(n_tp):
        image_sum = image_sum + swap(image_sum, "tp", n_tp, bit)
    for bit in bits_of(n_seq):
        image_sum = image_sum + swap(image_sum, "seq", n_seq, bit)
    loss = jnp.mean(image_sum / (lengths.astype(F32) * mod_scale.shape[0]))
    return (target, student, loss)


def solution(mesh):
    placed = (
        P("seq", "tp"),
        P(),
        P(),
        P(),
        P(None, "tp"),
        P(None, "tp"),
        P(None, "tp"),
        P("tp", None),
        P(),
        P(),
        P("tp", None),
    )

    def body(*arguments):
        return on_device(dict(mesh.shape), *arguments)

    return jax.shard_map(
        body,
        mesh=mesh,
        in_specs=placed,
        out_specs=(P("seq", "tp"), P("seq", "tp"), P()),
        check_vma=False,
    )
```

time: 337 us -> 160 us (0.47)
  waiting for transfers between devices: 198 us -> 56.7 us
  blocking collectives: 57.7 us -> 0 us
  starting transfers between devices: 0.29 us -> 43.9 us
  between operations: 18.7 us -> 3 us
  matrix products: 33.4 us -> 18.9 us
  other arithmetic: 16.8 us -> 21.6 us
  local copies, waits for them, and re-layouts: 11 us -> 15.5 us
    all_gather x4 -> x0, waiting for transfers between devices: 132 us -> none  [the longest x2 83.3 us: teacher(): key_block = lax.all_gather(key_rows, 'seq', axis=0, tiled=True)]
    reduce_scatter x3 -> x0, waiting for transfers between devices: 65.9 us -> none  [the longest x2 47.8 us: on_device(): lax.psum_scatter(partial_value.astype(jnp.bfloat16), 'tp', scatter_dimens...]
    ppermute x0 -> x34, waiting for transfers between devices: none -> 56.7 us  [swap(): return lax.ppermute(value, axis, [(i, i ^ mask) for i in range(size)])]
    ppermute x0 -> x34, starting transfers between devices: none -> 43.9 us  [swap(): return lax.ppermute(value, axis, [(i, i ^ mask) for i in range(size)])]
    psum x1 -> x0, blocking collectives: 39.3 us -> none  [on_device(): image_sum = lax.psum(image_part, ('seq', 'tp'))]
    all_gather x2 -> x0, blocking collectives: 18.4 us -> none  [the longest x1 10.4 us: on_device(): whole_rows = lax.all_gather(latents, 'tp', axis=1, tiled=True)]
    dot_general x13, matrix products: 33.4 us -> 18.9 us  [the longest x2 4.89 us: teacher(): jnp.dot(hidden, k_weight, preferred_element_type=F32)]
  transfers between devices with their start and end apart: 7 -> 34, of which waited for: 7 -> 24; matrix products, arithmetic and copies ran while one was open for 11% -> 7% of each run, Pallas kernels for 0% -> 0%
where the time goes in v1:
time: 160 us
  waiting for transfers between devices  56.7 us (35%)
  starting transfers between devices  43.9 us (27%)
  other arithmetic  21.6 us (14%)
  matrix products  18.9 us (12%)
  local copies, waits for them, and re-layouts  15.5 us (10%)
  between operations  3 us (2%)
    ppermute x34, waiting for transfers between devices, swap(): return lax.ppermute(value, axis, [(i, i ^ mask) for i in range(size)])  56.7 us
    ppermute x34, starting transfers between devices, swap(): return lax.ppermute(value, axis, [(i, i ^ mask) for i in range(size)])  43.9 us
    mul x4, local copies, waits for them, and re-layouts, head_norm(): shaped * shaped  5.56 us
    dot_general x2, matrix products, teacher(): jnp.dot(hidden, k_weight, preferred_element_type=F32)  4.89 us
    reshape x4, local copies, waits for them, and re-layouts, head_norm(): shaped = projected.reshape(projected.shape[0], -1, gain.shape[0])  4.67 us
    dot_general x3, matrix products, terms_of(): product = jnp.dot(left, right, preferred_element_type=F32)  4.46 us
    dot_general x2, matrix products, teacher(): jnp.dot(hidden, v_weight, preferred_element_type=F32).astype(BF16)  4.03 us
  transfers between devices with their start and end apart: 34, of which 24 were waited for; matrix products, arithmetic and copies ran while one was open for 7% of the time, Pallas kernels for 0%

profile of v1, /device:TPU:0, one launch (start us, length us, event | category | flops | bytes accessed | tf_op | source)
XLA Modules:
  0.0 159.6 jit_solution(6176136015078015274)
XLA Ops:
  0.6 3.0 %collective-permute-start = (bf16[128,768]{1,0:T(8,128)(2,1)}, bf16[128,768]{1,0:T(8,128)(2,1)S(1)}, u32[]{:S(2)}, u32[]{:S(2)}) collective-permute-start(bf16[128,768]{1,0:T(8,128)(2,1)} %param.11), channel_id=1, source_target_pairs={{0,2},{1,3},{2,0},{3,1},{4,6},{5,7},{6,4},{7,5},{8,10},{9,11},{10,... | collective-permute-start | bytes 589832 | tf_op jit(solution)/shard_map/ppermute | solution.py:19
  6.6 1.6 fusion.71
  14.2 1.8 %mul.313 = f32[128,4,128]{2,1,0:T(4,128)} reshape(f32[128,512]{1,0:T(8,128)} %get-tuple-element.55) | data formatting | bytes 524288 | tf_op jit(solution)/shard_map/mul | solution.py:62
  18.0 3.4 %fusion.93 = (f32[128,512]{1,0:T(8,128)}, f32[128,512]{1,0:T(8,128)S(1)}) fusion(bf16[128,3072]{1,0:T(8,128)(2,1)} %copy-done.1, bf16[3072,512]{1,0:T(8,128)(2,1)} %param.16), kind=kOutput, calls=%fused_computation.222 | convolution fusion | flops 402718720 | bytes 4456448 | tf_op jit(solution)/shard_map/dot_general | solution.py:186
  21.5 1.7 %mul.319 = f32[128,4,128]{2,1,0:T(4,128)} reshape(f32[128,512]{1,0:T(8,128)} %get-tuple-element.53) | data formatting | bytes 524288 | tf_op jit(solution)/shard_map/mul | solution.py:62
  25.3 2.8 %convolution_convert_fusion.1 = bf16[128,512]{1,0:T(8,128)(2,1)S(1)} fusion(bf16[128,3072]{1,0:T(8,128)(2,1)} %copy-done.1, bf16[3072,512]{1,0:T(8,128)(2,1)} %param.17), kind=kOutput, calls=%fused_computation.25 | convolution fusion | flops 402718720 | bytes 4063232 | tf_op jit(solution)/shard_map/dot_general | solution.py:187
  31.1 1.6 collective-permute-start.3
  32.7 1.6 collective-permute-start.4
  34.6 1.6 collective-permute-done.3
  36.2 2.1 %collective-permute-done.4 = bf16[128,384]{0,1:T(8,128)(2,1)S(1)} collective-permute-done((bf16[128,384]{0,1:T(8,128)(2,1)S(1)}, bf16[128,384]{0,1:T(8,128)(2,1)S(1)}, u32[]{:S(2)}, u32[]{:S(2)}) %collective-permute-start.4) | collective-permute-done | bytes 98336 | tf_op jit(solution)/shard_map/ppermute | solution.py:19
  39.8 3.4 %collective-permute-start.6 = (bf16[512,256]{0,1:T(8,128)(2,1)S(1)}, bf16[512,256]{0,1:T(8,128)(2,1)S(1)}, u32[]{:S(2)}, u32[]{:S(2)}) collective-permute-start(bf16[512,256]{0,1:T(8,128)(2,1)S(1)} %pad_maximum_fusion.11), channel_id=1, source_target_pairs={{0,24},{4,28},{8,16},{12,20},{16,8},{20,12},{24,0},{28,4},{1,25},{... | collective-permute-start | bytes 786440 | tf_op jit(solution)/shard_map/ppermute | solution.py:19
  43.3 5.7 %collective-permute-done.6 = bf16[512,256]{0,1:T(8,128)(2,1)S(1)} collective-permute-done((bf16[512,256]{0,1:T(8,128)(2,1)S(1)}, bf16[512,256]{0,1:T(8,128)(2,1)S(1)}, u32[]{:S(2)}, u32[]{:S(2)}) %collective-permute-start.6) | collective-permute-done | bytes 262176 | tf_op jit(solution)/shard_map/ppermute | solution.py:19
  51.1 6.3 %collective-permute-start.7 = (bf16[128,128]{0,1:T(8,128)(2,1)S(1)}, bf16[128,128]{0,1:T(8,128)(2,1)S(1)}, u32[]{:S(2)}, u32[]{:S(2)}) collective-permute-start(bf16[128,128]{0,1:T(8,128)(2,1)S(1)} %get-tuple-element.52), channel_id=1, source_target_pairs={{0,12},{4,8},{8,4},{12,0},{16,28},{20,24},{24,20},{28,16},{1,13},{... | collective-permute-start | bytes 98312 | tf_op jit(solution)/shard_map/ppermute | solution.py:19
  59.5 1.7 %collective-permute-done.8 = bf16[128,128]{0,1:T(8,128)(2,1)S(1)} collective-permute-done((bf16[128,128]{0,1:T(8,128)(2,1)S(1)}, bf16[128,128]{0,1:T(8,128)(2,1)S(1)}, u32[]{:S(2)}, u32[]{:S(2)}) %collective-permute-start.8) | collective-permute-done | bytes 32800 | tf_op jit(solution)/shard_map/ppermute | solution.py:19
  67.4 5.9 %collective-permute-done.12 = bf16[128,768]{1,0:T(8,128)(2,1)} collective-permute-done((bf16[128,768]{1,0:T(8,128)(2,1)S(1)}, bf16[128,768]{1,0:T(8,128)(2,1)}, u32[]{:S(2)}, u32[]{:S(2)}) %collective-permute-start.12) | collective-permute-done | bytes 196640 | tf_op jit(solution)/shard_map/ppermute | solution.py:19
  75.9 5.0 %collective-permute-done.13 = bf16[128,768]{1,0:T(8,128)(2,1)S(1)} collective-permute-done((bf16[128,768]{1,0:T(8,128)(2,1)S(1)}, bf16[128,768]{1,0:T(8,128)(2,1)S(1)}, u32[]{:S(2)}, u32[]{:S(2)}) %collective-permute-start.13) | collective-permute-done | bytes 196640 | tf_op jit(solution)/shard_map/ppermute | solution.py:19
  89.5 1.8 %copy.53 = f32[128,512]{0,1:T(8,128)} copy(f32[128,512]{1,0:T(8,128)} %get-tuple-element.62) | data formatting | bytes 524288 | tf_op jit(solution)/shard_map/reshape | solution.py:61
  97.4 1.9 %collective-permute-start.17 = (bf16[128,384]{0,1:T(8,128)(2,1)S(1)}, bf16[128,384]{0,1:T(8,128)(2,1)S(1)}, u32[]{:S(2)}, u32[]{:S(2)}) collective-permute-start(bf16[128,384]{0,1:T(8,128)(2,1)S(1)} %bitcast.40), channel_id=1, source_target_pairs={{0,8},{4,12},{8,0},{12,4},{16,24},{20,28},{24,16},{28,20},{1,9},{5... | collective-permute-start | bytes 294920 | tf_op jit(solution)/shard_map/ppermute | solution.py:19
  102.5 2.7 %collective-permute-done.18 = bf16[128,384]{0,1:T(8,128)(2,1)S(1)} collective-permute-done((bf16[128,384]{0,1:T(8,128)(2,1)S(1)}, bf16[128,384]{0,1:T(8,128)(2,1)S(1)}, u32[]{:S(2)}, u32[]{:S(2)}) %collective-permute-start.18) | collective-permute-done | bytes 98336 | tf_op jit(solution)/shard_map/ppermute | solution.py:19
  105.2 2.6 %collective-permute-start.19 = (bf16[512,256]{0,1:T(8,128)(2,1)S(1)}, bf16[512,256]{0,1:T(8,128)(2,1)S(1)}, u32[]{:S(2)}, u32[]{:S(2)}) collective-permute-start(bf16[512,256]{0,1:T(8,128)(2,1)S(1)} %pad_maximum_fusion.6), channel_id=1, source_target_pairs={{0,24},{4,28},{8,16},{12,20},{16,8},{20,12},{24,0},{28,4},{1,25},{... | collective-permute-start | bytes 786440 | tf_op jit(solution)/shard_map/ppermute | solution.py:19
  107.8 3.2 %fusion.31 = bf16[128,3072]{1,0:T(8,128)(2,1)S(1)} fusion(bf16[768,3072]{1,0:T(8,128)(2,1)} %param.21, bf16[128,3072]{1,0:T(8,128)(2,1)} %copy-done.1, s32[]{:T(128)S(6)} %select_n.230), kind=kOutput, calls=%fused_computation.86 | convolution fusion | flops 603979776 | bytes 5701636 | tf_op jit(solution)/shard_map/dot_general | solution.py:175
  111.1 3.8 %collective-permute-done.19 = bf16[512,256]{0,1:T(8,128)(2,1)S(1)} collective-permute-done((bf16[512,256]{0,1:T(8,128)(2,1)S(1)}, bf16[512,256]{0,1:T(8,128)(2,1)S(1)}, u32[]{:S(2)}, u32[]{:S(2)}) %collective-permute-start.19) | collective-permute-done | bytes 262176 | tf_op jit(solution)/shard_map/ppermute | solution.py:19
  117.1 4.9 %collective-permute-start.20 = (bf16[128,128]{0,1:T(8,128)(2,1)S(1)}, bf16[128,128]{0,1:T(8,128)(2,1)S(1)}, u32[]{:S(2)}, u32[]{:S(2)}) collective-permute-start(bf16[128,128]{0,1:T(8,128)(2,1)S(1)} %get-tuple-element.49), channel_id=1, source_target_pairs={{0,12},{4,8},{8,4},{12,0},{16,28},{20,24},{24,20},{28,16},{1,13},{... | collective-permute-start | bytes 98312 | tf_op jit(solution)/shard_map/ppermute | solution.py:19
  124.1 1.9 %collective-permute-done.21 = bf16[128,128]{0,1:T(8,128)(2,1)S(1)} collective-permute-done((bf16[128,128]{0,1:T(8,128)(2,1)S(1)}, bf16[128,128]{0,1:T(8,128)(2,1)S(1)}, u32[]{:S(2)}, u32[]{:S(2)}) %collective-permute-start.21) | collective-permute-done | bytes 32800 | tf_op jit(solution)/shard_map/ppermute | solution.py:19
  129.6 5.1 %collective-permute-done.28 = bf16[128,768]{1,0:T(8,128)(2,1)S(1)} collective-permute-done((bf16[128,768]{1,0:T(8,128)(2,1)S(1)}, bf16[128,768]{1,0:T(8,128)(2,1)S(1)}, u32[]{:S(2)}, u32[]{:S(2)}) %collective-permute-start.28) | collective-permute-done | bytes 196640 | tf_op jit(solution)/shard_map/ppermute | solution.py:19
  134.7 3.7 %collective-permute-done.25 = bf16[128,768]{1,0:T(8,128)(2,1)S(1)} collective-permute-done((bf16[128,768]{1,0:T(8,128)(2,1)S(1)}, bf16[128,768]{1,0:T(8,128)(2,1)S(1)}, u32[]{:S(2)}, u32[]{:S(2)}) %collective-permute-start.25) | collective-permute-done | bytes 196640 | tf_op jit(solution)/shard_map/ppermute | solution.py:19
  138.4 1.9 %fusion.22 = (f32[128]{0:T(128)S(1)}, f32[128]{0:T(128)S(1)}, bf16[128,768]{1,0:T(8,128)(2,1)}, bf16[128,768]{1,0:T(8,128)(2,1)}) fusion(bf16[128,768]{1,0:T(8,128)(2,1)S(1)} %collective-permute-done.28, bf16[128,768]{1,0:T(8,128)(2,1)S(1)} %collective-permute-done.26, bf16[128,3072]{1,0:T(8,128)(2,1)S(1)} %fusion.31, s32[]{:T(128)S(6)} %select_n.230, ...), kind=kLoop, calls=%fused_computation.42 | loop fusion | flops 3145472 | bytes 1967108 | tf_op jit(solution)/shard_map/reduce_sum | solution.py:211
  143.0 2.3 %collective-permute-done.30 = f32[2]{0:T(128)S(1)} collective-permute-done((f32[2]{0:T(128)S(1)}, f32[2]{0:T(128)S(1)}, u32[]{:S(2)}, u32[]{:S(2)}) %collective-permute-start.30) | collective-permute-done | bytes 40 | tf_op jit(solution)/shard_map/ppermute | solution.py:19
  146.6 2.2 %collective-permute-done.31 = f32[2]{0:T(128)S(1)} collective-permute-done((f32[2]{0:T(128)S(1)}, f32[2]{0:T(128)S(1)}, u32[]{:S(2)}, u32[]{:S(2)}) %collective-permute-start.31) | collective-permute-done | bytes 40 | tf_op jit(solution)/shard_map/ppermute | solution.py:19
  148.9 2.0 %collective-permute-start.32 = (f32[2]{0:T(128)S(1)}, f32[2]{0:T(128)S(1)}, u32[]{:S(2)}, u32[]{:S(2)}) collective-permute-start(f32[2]{0:T(128)S(1)} %add.301), channel_id=1, source_target_pairs={{0,8},{4,12},{8,0},{12,4},{16,24},{20,28},{24,16},{28,20},{1,9},{5... | collective-permute-start | bytes 32 | tf_op jit(solution)/shard_map/ppermute | solution.py:19
  152.4 3.2 %collective-permute-start.33 = (f32[2]{0:T(128)S(1)}, f32[2]{0:T(128)S(1)}, u32[]{:S(2)}, u32[]{:S(2)}) collective-permute-start(f32[2]{0:T(128)S(1)} %add.302), channel_id=1, source_target_pairs={{0,16},{4,20},{8,24},{12,28},{16,0},{20,4},{24,8},{28,12},{1,17},{... | collective-permute-start | bytes 32 | tf_op jit(solution)/shard_map/ppermute | solution.py:19
  155.6 1.5 collective-permute-done.33
  (187 shorter events, 62.4 us)
Async XLA Ops:
  0.6 8.3 %collective-permute-start = (bf16[128,768]{1,0:T(8,128)(2,1)}, bf16[128,768]{1,0:T(8,128)(2,1)S(1)}, u32[]{:S(2)}, u32[]{:S(2)}) collective-permute-start(bf16[128,768]{1,0:T(8,128)(2,1)} %param.11), channel_id=1, source_target_pairs={{0,2},{1,3},{2,0},{3,1},{4,6},{5,7},{6,4},{7,5},{8,10},{9,11},{10,... | collective-permute-start | bytes 589832 | tf_op jit(solution)/shard_map/ppermute | solution.py:19
  3.7 5.8 %collective-permute-start.2 = (bf16[128,768]{1,0:T(8,128)(2,1)}, bf16[128,768]{1,0:T(8,128)(2,1)S(1)}, u32[]{:S(2)}, u32[]{:S(2)}) collective-permute-start(bf16[128,768]{1,0:T(8,128)(2,1)} %param.11), channel_id=1, source_target_pairs={{0,1},{1,0},{2,3},{3,2},{4,5},{5,4},{6,7},{7,6},{8,9},{9,8},{10,11... | collective-permute-start | bytes 589832 | tf_op jit(solution)/shard_map/ppermute | solution.py:19
  8.9 1.6 collective-permute-start.1
  31.1 5.1 %collective-permute-start.3 = (bf16[128,384]{0,1:T(8,128)(2,1)S(1)}, bf16[128,384]{0,1:T(8,128)(2,1)S(1)}, u32[]{:S(2)}, u32[]{:S(2)}) collective-permute-start(bf16[128,384]{0,1:T(8,128)(2,1)S(1)} %bitcast.43), channel_id=1, source_target_pairs={{0,4},{4,0},{8,12},{12,8},{16,20},{20,16},{24,28},{28,24},{1,5},{5... | collective-permute-start | bytes 294920 | tf_op jit(solution)/shard_map/ppermute | solution.py:19
  32.7 5.7 %collective-permute-start.4 = (bf16[128,384]{0,1:T(8,128)(2,1)S(1)}, bf16[128,384]{0,1:T(8,128)(2,1)S(1)}, u32[]{:S(2)}, u32[]{:S(2)}) collective-permute-start(bf16[128,384]{0,1:T(8,128)(2,1)S(1)} %bitcast.41), channel_id=1, source_target_pairs={{0,8},{4,12},{8,0},{12,4},{16,24},{20,28},{24,16},{28,20},{1,9},{5... | collective-permute-start | bytes 294920 | tf_op jit(solution)/shard_map/ppermute | solution.py:19
  34.2 5.5 %collective-permute-start.5 = (bf16[128,384]{0,1:T(8,128)(2,1)S(1)}, bf16[128,384]{0,1:T(8,128)(2,1)S(1)}, u32[]{:S(2)}, u32[]{:S(2)}) collective-permute-start(bf16[128,384]{0,1:T(8,128)(2,1)S(1)} %bitcast.39), channel_id=1, source_target_pairs={{0,12},{4,8},{8,4},{12,0},{16,28},{20,24},{24,20},{28,16},{1,13},{... | collective-permute-start | bytes 294920 | tf_op jit(solution)/shard_map/ppermute | solution.py:19
  39.8 9.2 %collective-permute-start.6 = (bf16[512,256]{0,1:T(8,128)(2,1)S(1)}, bf16[512,256]{0,1:T(8,128)(2,1)S(1)}, u32[]{:S(2)}, u32[]{:S(2)}) collective-permute-start(bf16[512,256]{0,1:T(8,128)(2,1)S(1)} %pad_maximum_fusion.11), channel_id=1, source_target_pairs={{0,24},{4,28},{8,16},{12,20},{16,8},{20,12},{24,0},{28,4},{1,25},{... | collective-permute-start | bytes 786440 | tf_op jit(solution)/shard_map/ppermute | solution.py:19
  51.1 8.4 %collective-permute-start.7 = (bf16[128,128]{0,1:T(8,128)(2,1)S(1)}, bf16[128,128]{0,1:T(8,128)(2,1)S(1)}, u32[]{:S(2)}, u32[]{:S(2)}) collective-permute-start(bf16[128,128]{0,1:T(8,128)(2,1)S(1)} %get-tuple-element.52), channel_id=1, source_target_pairs={{0,12},{4,8},{8,4},{12,0},{16,28},{20,24},{24,20},{28,16},{1,13},{... | collective-permute-start | bytes 98312 | tf_op jit(solution)/shard_map/ppermute | solution.py:19
  57.4 3.9 %collective-permute-start.8 = (bf16[128,128]{0,1:T(8,128)(2,1)S(1)}, bf16[128,128]{0,1:T(8,128)(2,1)S(1)}, u32[]{:S(2)}, u32[]{:S(2)}) collective-permute-start(bf16[128,128]{0,1:T(8,128)(2,1)S(1)} %get-tuple-element.51), channel_id=1, source_target_pairs={{0,8},{4,12},{8,0},{12,4},{16,24},{20,28},{24,16},{28,20},{1,9},{5... | collective-permute-start | bytes 98312 | tf_op jit(solution)/shard_map/ppermute | solution.py:19
  57.4 3.9 %collective-permute-start.9 = (bf16[128,128]{0,1:T(8,128)(2,1)S(1)}, bf16[128,128]{0,1:T(8,128)(2,1)S(1)}, u32[]{:S(2)}, u32[]{:S(2)}) collective-permute-start(bf16[128,128]{0,1:T(8,128)(2,1)S(1)} %get-tuple-element.50), channel_id=1, source_target_pairs={{0,4},{4,0},{8,12},{12,8},{16,20},{20,16},{24,28},{28,24},{1,5},{5... | collective-permute-start | bytes 98312 | tf_op jit(solution)/shard_map/ppermute | solution.py:19
  63.6 1.6 collective-permute-start.11
  63.6 3.8 %collective-permute-start.10 = (bf16[128,768]{1,0:T(8,128)(2,1)}, bf16[128,768]{1,0:T(8,128)(2,1)}, u32[]{:S(2)}, u32[]{:S(2)}) collective-permute-start(bf16[128,768]{1,0:T(8,128)(2,1)} %get-tuple-element.23), channel_id=1, source_target_pairs={{0,1},{1,0},{2,3},{3,2},{4,5},{5,4},{6,7},{7,6},{8,9},{9,8},{10,11... | collective-permute-start | bytes 589832 | tf_op jit(solution)/shard_map/ppermute | solution.py:19
  66.2 7.1 %collective-permute-start.12 = (bf16[128,768]{1,0:T(8,128)(2,1)S(1)}, bf16[128,768]{1,0:T(8,128)(2,1)}, u32[]{:S(2)}, u32[]{:S(2)}) collective-permute-start(bf16[128,768]{1,0:T(8,128)(2,1)S(1)} %add_convert_fusion.9), channel_id=1, source_target_pairs={{0,2},{1,3},{2,0},{3,1},{4,6},{5,7},{6,4},{7,5},{8,10},{9,11},{10,... | collective-permute-start | bytes 589832 | tf_op jit(solution)/shard_map/ppermute | solution.py:19
  74.7 6.2 %collective-permute-start.13 = (bf16[128,768]{1,0:T(8,128)(2,1)S(1)}, bf16[128,768]{1,0:T(8,128)(2,1)S(1)}, u32[]{:S(2)}, u32[]{:S(2)}) collective-permute-start(bf16[128,768]{1,0:T(8,128)(2,1)S(1)} %get-tuple-element.16), channel_id=1, source_target_pairs={{0,2},{1,3},{2,0},{3,1},{4,6},{5,7},{6,4},{7,5},{8,10},{9,11},{10,... | collective-permute-start | bytes 589832 | tf_op jit(solution)/shard_map/ppermute | solution.py:19
  75.9 5.2 %collective-permute-start.15 = (bf16[128,768]{1,0:T(8,128)(2,1)S(1)}, bf16[128,768]{1,0:T(8,128)(2,1)S(1)}, u32[]{:S(2)}, u32[]{:S(2)}) collective-permute-start(bf16[128,768]{1,0:T(8,128)(2,1)S(1)} %get-tuple-element.15), channel_id=1, source_target_pairs={{0,1},{1,0},{2,3},{3,2},{4,5},{5,4},{6,7},{7,6},{8,9},{9,8},{10,11... | collective-permute-start | bytes 589832 | tf_op jit(solution)/shard_map/ppermute | solution.py:19
  96.7 4.9 %collective-permute-start.16 = (bf16[128,384]{0,1:T(8,128)(2,1)S(1)}, bf16[128,384]{0,1:T(8,128)(2,1)S(1)}, u32[]{:S(2)}, u32[]{:S(2)}) collective-permute-start(bf16[128,384]{0,1:T(8,128)(2,1)S(1)} %bitcast.42), channel_id=1, source_target_pairs={{0,4},{4,0},{8,12},{12,8},{16,20},{20,16},{24,28},{28,24},{1,5},{5... | collective-permute-start | bytes 294920 | tf_op jit(solution)/shard_map/ppermute | solution.py:19
  97.4 5.0 %collective-permute-start.17 = (bf16[128,384]{0,1:T(8,128)(2,1)S(1)}, bf16[128,384]{0,1:T(8,128)(2,1)S(1)}, u32[]{:S(2)}, u32[]{:S(2)}) collective-permute-start(bf16[128,384]{0,1:T(8,128)(2,1)S(1)} %bitcast.40), channel_id=1, source_target_pairs={{0,8},{4,12},{8,0},{12,4},{16,24},{20,28},{24,16},{28,20},{1,9},{5... | collective-permute-start | bytes 294920 | tf_op jit(solution)/shard_map/ppermute | solution.py:19
  99.3 5.9 %collective-permute-start.18 = (bf16[128,384]{0,1:T(8,128)(2,1)S(1)}, bf16[128,384]{0,1:T(8,128)(2,1)S(1)}, u32[]{:S(2)}, u32[]{:S(2)}) collective-permute-start(bf16[128,384]{0,1:T(8,128)(2,1)S(1)} %bitcast.38), channel_id=1, source_target_pairs={{0,12},{4,8},{8,4},{12,0},{16,28},{20,24},{24,20},{28,16},{1,13},{... | collective-permute-start | bytes 294920 | tf_op jit(solution)/shard_map/ppermute | solution.py:19
  105.2 9.6 %collective-permute-start.19 = (bf16[512,256]{0,1:T(8,128)(2,1)S(1)}, bf16[512,256]{0,1:T(8,128)(2,1)S(1)}, u32[]{:S(2)}, u32[]{:S(2)}) collective-permute-start(bf16[512,256]{0,1:T(8,128)(2,1)S(1)} %pad_maximum_fusion.6), channel_id=1, source_target_pairs={{0,24},{4,28},{8,16},{12,20},{16,8},{20,12},{24,0},{28,4},{1,25},{... | collective-permute-start | bytes 786440 | tf_op jit(solution)/shard_map/ppermute | solution.py:19
  117.1 7.0 %collective-permute-start.20 = (bf16[128,128]{0,1:T(8,128)(2,1)S(1)}, bf16[128,128]{0,1:T(8,128)(2,1)S(1)}, u32[]{:S(2)}, u32[]{:S(2)}) collective-permute-start(bf16[128,128]{0,1:T(8,128)(2,1)S(1)} %get-tuple-element.49), channel_id=1, source_target_pairs={{0,12},{4,8},{8,4},{12,0},{16,28},{20,24},{24,20},{28,16},{1,13},{... | collective-permute-start | bytes 98312 | tf_op jit(solution)/shard_map/ppermute | solution.py:19
  122.1 3.9 %collective-permute-start.21 = (bf16[128,128]{0,1:T(8,128)(2,1)S(1)}, bf16[128,128]{0,1:T(8,128)(2,1)S(1)}, u32[]{:S(2)}, u32[]{:S(2)}) collective-permute-start(bf16[128,128]{0,1:T(8,128)(2,1)S(1)} %get-tuple-element.48), channel_id=1, source_target_pairs={{0,8},{4,12},{8,0},{12,4},{16,24},{20,28},{24,16},{28,20},{1,9},{5... | collective-permute-start | bytes 98312 | tf_op jit(solution)/shard_map/ppermute | solution.py:19
  122.1 3.9 %collective-permute-start.22 = (bf16[128,128]{0,1:T(8,128)(2,1)S(1)}, bf16[128,128]{0,1:T(8,128)(2,1)S(1)}, u32[]{:S(2)}, u32[]{:S(2)}) collective-permute-start(bf16[128,128]{0,1:T(8,128)(2,1)S(1)} %get-tuple-element.47), channel_id=1, source_target_pairs={{0,4},{4,0},{8,12},{12,8},{16,20},{20,16},{24,28},{28,24},{1,5},{5... | collective-permute-start | bytes 98312 | tf_op jit(solution)/shard_map/ppermute | solution.py:19
  123.4 3.3 %collective-permute-start.27 = (bf16[128,768]{1,0:T(8,128)(2,1)S(1)}, bf16[128,768]{1,0:T(8,128)(2,1)S(1)}, u32[]{:S(2)}, u32[]{:S(2)}) collective-permute-start(bf16[128,768]{1,0:T(8,128)(2,1)S(1)} %get-tuple-element.26), channel_id=1, source_target_pairs={{0,1},{1,0},{2,3},{3,2},{4,5},{5,4},{6,7},{7,6},{8,9},{9,8},{10,11... | collective-permute-start | bytes 589832 | tf_op jit(solution)/shard_map/ppermute | solution.py:19
  123.5 6.1 %collective-permute-start.26 = (bf16[128,768]{1,0:T(8,128)(2,1)S(1)}, bf16[128,768]{1,0:T(8,128)(2,1)S(1)}, u32[]{:S(2)}, u32[]{:S(2)}) collective-permute-start(bf16[128,768]{1,0:T(8,128)(2,1)S(1)} %get-tuple-element.25), channel_id=1, source_target_pairs={{0,1},{1,0},{2,3},{3,2},{4,5},{5,4},{6,7},{7,6},{8,9},{9,8},{10,11... | collective-permute-start | bytes 589832 | tf_op jit(solution)/shard_map/ppermute | solution.py:19
  126.7 1.7 %collective-permute-start.24 = (bf16[128,768]{1,0:T(8,128)(2,1)S(1)}, bf16[128,768]{1,0:T(8,128)(2,1)S(1)}, u32[]{:S(2)}, u32[]{:S(2)}) collective-permute-start(bf16[128,768]{1,0:T(8,128)(2,1)S(1)} %get-tuple-element.18), channel_id=1, source_target_pairs={{0,1},{1,0},{2,3},{3,2},{4,5},{5,4},{6,7},{7,6},{8,9},{9,8},{10,11... | collective-permute-start | bytes 589832 | tf_op jit(solution)/shard_map/ppermute | solution.py:19
  126.9 7.8 %collective-permute-start.28 = (bf16[128,768]{1,0:T(8,128)(2,1)S(1)}, bf16[128,768]{1,0:T(8,128)(2,1)S(1)}, u32[]{:S(2)}, u32[]{:S(2)}) collective-permute-start(bf16[128,768]{1,0:T(8,128)(2,1)S(1)} %add_convert_fusion.1), channel_id=1, source_target_pairs={{0,2},{1,3},{2,0},{3,1},{4,6},{5,7},{6,4},{7,5},{8,10},{9,11},{10,... | collective-permute-start | bytes 589832 | tf_op jit(solution)/shard_map/ppermute | solution.py:19
  128.2 6.5 %collective-permute-start.23 = (bf16[128,768]{1,0:T(8,128)(2,1)S(1)}, bf16[128,768]{1,0:T(8,128)(2,1)S(1)}, u32[]{:S(2)}, u32[]{:S(2)}) collective-permute-start(bf16[128,768]{1,0:T(8,128)(2,1)S(1)} %get-tuple-element.17), channel_id=1, source_target_pairs={{0,1},{1,0},{2,3},{3,2},{4,5},{5,4},{6,7},{7,6},{8,9},{9,8},{10,11... | collective-permute-start | bytes 589832 | tf_op jit(solution)/shard_map/ppermute | solution.py:19
  128.4 10.0 %collective-permute-start.25 = (bf16[128,768]{1,0:T(8,128)(2,1)S(1)}, bf16[128,768]{1,0:T(8,128)(2,1)S(1)}, u32[]{:S(2)}, u32[]{:S(2)}) collective-permute-start(bf16[128,768]{1,0:T(8,128)(2,1)S(1)} %add_convert_fusion.4), channel_id=1, source_target_pairs={{0,2},{1,3},{2,0},{3,1},{4,6},{5,7},{6,4},{7,5},{8,10},{9,11},{10,... | collective-permute-start | bytes 589832 | tf_op jit(solution)/shard_map/ppermute | solution.py:19
  141.7 3.6 %collective-permute-start.30 = (f32[2]{0:T(128)S(1)}, f32[2]{0:T(128)S(1)}, u32[]{:S(2)}, u32[]{:S(2)}) collective-permute-start(f32[2]{0:T(128)S(1)} %add.299), channel_id=1, source_target_pairs={{0,2},{1,3},{2,0},{3,1},{4,6},{5,7},{6,4},{7,5},{8,10},{9,11},{10,... | collective-permute-start | bytes 32 | tf_op jit(solution)/shard_map/ppermute | solution.py:19
  145.3 3.6 %collective-permute-start.31 = (f32[2]{0:T(128)S(1)}, f32[2]{0:T(128)S(1)}, u32[]{:S(2)}, u32[]{:S(2)}) collective-permute-start(f32[2]{0:T(128)S(1)} %add.300), channel_id=1, source_target_pairs={{0,4},{4,0},{8,12},{12,8},{16,20},{20,16},{24,28},{28,24},{1,5},{5... | collective-permute-start | bytes 32 | tf_op jit(solution)/shard_map/ppermute | solution.py:19
  148.9 3.6 %collective-permute-start.32 = (f32[2]{0:T(128)S(1)}, f32[2]{0:T(128)S(1)}, u32[]{:S(2)}, u32[]{:S(2)}) collective-permute-start(f32[2]{0:T(128)S(1)} %add.301), channel_id=1, source_target_pairs={{0,8},{4,12},{8,0},{12,4},{16,24},{20,28},{24,16},{28,20},{1,9},{5... | collective-permute-start | bytes 32 | tf_op jit(solution)/shard_map/ppermute | solution.py:19
  152.4 4.7 %collective-permute-start.33 = (f32[2]{0:T(128)S(1)}, f32[2]{0:T(128)S(1)}, u32[]{:S(2)}, u32[]{:S(2)}) collective-permute-start(f32[2]{0:T(128)S(1)} %add.302), channel_id=1, source_target_pairs={{0,16},{4,20},{8,24},{12,28},{16,0},{20,4},{24,8},{28,12},{1,17},{... | collective-permute-start | bytes 32 | tf_op jit(solution)/shard_map/ppermute | solution.py:19
  (31 other events, 317.9 us)

commit v2 on v1

--- a/solution.py
+++ b/solution.py
@@ -1,14 +1,18 @@
+import functools
 import math
 
 import jax
 import jax.numpy as jnp
 from jax import lax
+from jax.experimental import pallas as pl
+from jax.experimental.pallas import tpu as pltpu
 from jax.sharding import PartitionSpec as P
 
 TGRID = 8
 epsilon = 1e-06
 kinetic_weight = 0.1
 F32, BF16 = jnp.float32, jnp.bfloat16
+KERNEL_VMEM = 24 * 1024 * 1024
 
 
 def image_index(positions, image_ends):
@@ -220,6 +224,354 @@
     return (target, student, loss)
 
 
+def whole(shape, dtype=BF16):
+    return jax.ShapeDtypeStruct(shape, dtype)
+
+
+VM = pl.BlockSpec(memory_space=pltpu.VMEM)
+
+
+def call(body, outs, flops, *operands):
+    size = sum(math.prod(a.shape) * a.dtype.itemsize for a in operands)
+    return pl.pallas_call(
+        body,
+        out_shape=outs,
+        in_specs=[VM] * len(operands),
+        out_specs=jax.tree.map(lambda _: VM, outs),
+        compiler_params=pltpu.CompilerParams(vmem_limit_bytes=KERNEL_VMEM),
+        cost_estimate=pl.CostEstimate(flops=flops, bytes_accessed=size, transcendentals=0),
+    )(*operands)
+
+
+def head_at(block, m, width):
+    return pl.ds(pl.multiple_of((block ^ m) * width, width), width)
+
+
+def normed_head(raw, gain):
+    return (raw * lax.rsqrt(jnp.mean(raw * raw, axis=1, keepdims=True) + epsilon) * gain).astype(
+        BF16
+    )
+
+
+def head_block_of(spread, twisted):
+    seq_index = lax.axis_index("seq")
+    block = lax.rem(seq_index, spread)
+    if twisted:
+        block = block ^ (lax.div(seq_index, spread) * 2)
+    return block
+
+
+def kv_kernel(plan, moving, *refs):
+    n_tp, _, spread, twisted, head_dim, step_size = plan
+    state, refs = refs[:n_tp], refs[n_tp:]
+    if moving:
+        near, far, refs = refs[:n_tp], refs[n_tp : 2 * n_tp], refs[2 * n_tp :]
+    time_ref, mod_ref, k_ref, v_ref, gain_ref, rows_ref, scale_ref = refs[:7]
+    outs = refs[7:]
+    tp_index = lax.axis_index("tp")
+    block = head_block_of(spread, twisted)
+    width = state[0].shape[1]
+    times = time_ref[...]
+    squares = jnp.zeros_like(times)
+    for k in range(n_tp):
+        x = state[k][...].astype(F32)
+        if moving:
+            velocity = (near[k][...].astype(F32) + far[k][...].astype(F32)).astype(BF16)
+            x = (x + step_size * velocity.astype(F32)).astype(BF16).astype(F32)
+        squares = squares + jnp.sum(x * x, axis=1, keepdims=True)
+        mod = mod_ref[:, head_at(tp_index, k, width)]
+        rows_ref[:, k * width : (k + 1) * width] = (x * (1.0 + times * mod)).astype(BF16)
+    scale = lax.rsqrt(squares / (n_tp * width) + epsilon)
+    scale_ref[...] = scale
+    for m in range(spread):
+        columns = head_at(block, m, head_dim)
+        total = None
+        for k in range(n_tp):
+            rows = head_at(tp_index, k, width)
+            weight = jnp.concatenate([k_ref[rows, columns], v_ref[rows, columns]], axis=1)
+            part = jnp.dot(
+                rows_ref[:, k * width : (k + 1) * width], weight, preferred_element_type=F32
+            )
+            total = part if total is None else total + part
+        total = total * scale
+        outs[m][:, :head_dim] = normed_head(total[:, :head_dim], gain_ref[...])
+        outs[m][:, head_dim:] = total[:, head_dim:].astype(BF16)
+
+
+def q_kernel(plan, rows_ref, scale_ref, q_ref, gain_ref, *outs):
+    n_tp, _, spread, twisted, head_dim, _ = plan
+    tp_index = lax.axis_index("tp")
+    block = head_block_of(spread, twisted)
+    width = rows_ref.shape[1] // n_tp
+    for first in range(0, spread, 2):
+        total = None
+        for k in range(n_tp):
+            rows = head_at(tp_index, k, width)
+            weight = jnp.concatenate(
+                [q_ref[rows, head_at(block, m, head_dim)] for m in (first, first + 1)], axis=1
+            )
+            part = jnp.dot(
+                rows_ref[:, k * width : (k + 1) * width], weight, preferred_element_type=F32
+            )
+            total = part if total is None else total + part
+        total = total * scale_ref[...]
+        for m in range(2):
+            cut = total[:, m * head_dim : (m + 1) * head_dim]
+            outs[first + m][...] = normed_head(cut, gain_ref[...])
+
+
+def terms_kernel(n_tp, left_ref, right_ref, scale_ref, *outs):
+    tp_index = lax.axis_index("tp")
+    width = outs[0].shape[1]
+    for k in range(n_tp):
+        product = jnp.dot(
+            left_ref[...],
+            right_ref[:, head_at(tp_index, k, width)],
+            preferred_element_type=F32,
+        )
+        outs[k][...] = (product * scale_ref[...]).astype(BF16)
+
+
+def out_kernel(plan, *refs):
+    n_tp, _, spread, twisted, head_dim, _ = plan
+    pieces, right_ref, outs = refs[:spread], refs[spread], refs[spread + 1 :]
+    tp_index = lax.axis_index("tp")
+    block = head_block_of(spread, twisted)
+    width = outs[0].shape[1]
+    left = jnp.concatenate([piece[...] for piece in pieces], axis=1)
+    for k in list(range(1, n_tp, 2)) + list(range(0, n_tp, 2)):
+        columns = head_at(tp_index, k, width)
+        right = jnp.concatenate(
+            [right_ref[head_at(block, m, head_dim), columns] for m in range(spread)], axis=0
+        )
+        outs[k][...] = jnp.dot(left, right, preferred_element_type=F32).astype(BF16)
+
+
+def scores_of(query, keys, query_image, key_image, head_dim):
+    scores = lax.dot_general(
+        query, keys, (((1,), (1,)), ((), ())), preferred_element_type=F32
+    ) * (1.0 / math.sqrt(head_dim))
+    return jnp.where(query_image == key_image, scores, -1e30)
+
+
+def near_kernel(spread, head_dim, *refs):
+    queries, pairs, refs = refs[:spread], refs[spread : 2 * spread], refs[2 * spread :]
+    query_image, key_image, top_ref, total_ref, sum_ref = refs
+    rows = queries[0].shape[0]
+    keys = jnp.concatenate([pair[:, :head_dim] for pair in pairs], axis=0)
+    values = jnp.concatenate([pair[:, head_dim:] for pair in pairs], axis=0)
+    for m in range(spread):
+        cut = slice(m * rows, (m + 1) * rows)
+        scores = scores_of(queries[m][...], keys, query_image[cut], key_image[...], head_dim)
+        top = jnp.max(scores, axis=1, keepdims=True)
+        weights = jnp.exp(scores - top)
+        top_ref[cut] = top
+        total_ref[cut] = jnp.sum(weights, axis=1, keepdims=True)
+        sum_ref[cut] = jnp.dot(weights.astype(BF16), values, preferred_element_type=F32)
+
+
+def far_kernel(spread, head_dim, *refs):
+    queries, pairs, refs = refs[:spread], refs[spread : 2 * spread], refs[2 * spread :]
+    query_image, key_image, top_ref, total_ref, sum_ref = refs[:5]
+    outs = refs[5:]
+    rows = queries[0].shape[0]
+    keys = jnp.concatenate([pair[:, :head_dim] for pair in pairs], axis=0)
+    values = jnp.concatenate([pair[:, head_dim:] for pair in pairs], axis=0)
+    for m in range(spread):
+        cut = slice(m * rows, (m + 1) * rows)
+        scores = scores_of(queries[m][...], keys, query_image[cut], key_image[...], head_dim)
+        old = top_ref[cut]
+        top = jnp.maximum(old, jnp.max(scores, axis=1, keepdims=True))
+        weights = jnp.exp(scores - top)
+        fade = jnp.exp(old - top)
+        total = total_ref[cut] * fade + jnp.sum(weights, axis=1, keepdims=True)
+        mixed = sum_ref[cut] * fade + jnp.dot(
+            weights.astype(BF16), values, preferred_element_type=F32
+        )
+        outs[m][...] = (mixed / total).astype(BF16)
+
+
+def loss_kernel(*refs):
+    near0, far0, near1, far1, student_ref, image_ref, target_ref, part_ref = refs
+    velocity0 = (near0[...].astype(F32) + far0[...].astype(F32)).astype(BF16).astype(F32)
+    velocity1 = (near1[...].astype(F32) + far1[...].astype(F32)).astype(BF16).astype(F32)
+    target = (0.5 * (velocity0 + velocity1)).astype(BF16)
+    target_ref[...] = target
+    student = student_ref[...].astype(F32)
+    residual = student - target.astype(F32)
+    per_token = jnp.sum(residual * residual + kinetic_weight * (student * student), axis=1, keepdims=True)
+    lanes = lax.broadcasted_iota(jnp.int32, part_ref.shape, 1)
+    part_ref[...] = jnp.sum(
+        jnp.where(image_ref[...] == lanes[:1], per_token, 0.0), axis=0, keepdims=True
+    ) + jnp.zeros(part_ref.shape, F32)
+
+
+def on_device_fused(
+    mesh_shape,
+    latents,
+    lengths,
+    t_index,
+    mod_scale,
+    q_weight,
+    k_weight,
+    v_weight,
+    out_weight,
+    q_gain,
+    k_gain,
+    student_weight,
+):
+    n_seq, n_tp = mesh_shape["seq"], mesh_shape["tp"]
+    row_count, width = latents.shape
+    head_dim = q_gain.shape[0]
+    heads_here = q_weight.shape[1] // head_dim
+    seq_index = lax.axis_index("seq")
+    inner = n_tp * width
+    step_size = 1.0 / TGRID
+    spread = heads_here
+    twisted = spread >= 4
+    partner = spread ^ 2 if twisted else spread
+    plan = (n_tp, n_seq, spread, twisted, head_dim, step_size)
+
+    ends = [lengths[0]]
+    for i in range(1, lengths.shape[0]):
+        ends.append(ends[-1] + lengths[i])
+    row = jnp.arange(row_count, dtype=jnp.int32)
+    groups = jnp.arange(spread, dtype=jnp.int32)
+
+    def images_of(sources):
+        positions = (sources[:, None] * row_count + row[None, :]).reshape(-1)
+        return sum((positions >= end).astype(jnp.int32) for end in ends)
+
+    near_image = images_of(seq_index ^ groups)
+    far_image = images_of(seq_index ^ partner ^ groups)
+    own_image = images_of(seq_index[None])
+    start_time = sum(
+        jnp.where(own_image == i, t_index[i].astype(F32) / TGRID, 0.0)
+        for i in range(lengths.shape[0])
+    )[:, None]
+    near_rows, near_keys, far_keys = near_image[:, None], near_image[None, :], far_image[None, :]
+    own_rows = own_image[:, None]
+    mod_row = mod_scale[None, :]
+    q_row, k_row = q_gain[None, :], k_gain[None, :]
+
+    def tp_swap(value, mask):
+        return swap(value, "tp", n_tp, mask)
+
+    def seq_swap(value, mask):
+        return swap(value, "seq", n_seq, mask)
+
+    def mixed_terms(state, velocity, times):
+        operands = list(state)
+        if velocity is not None:
+            operands += velocity[0] + velocity[1]
+        rows, scale, *pairs = call(
+            functools.partial(kv_kernel, plan, velocity is not None),
+            [whole((row_count, inner)), whole((row_count, 1), F32)]
+            + [whole((row_count, 2 * head_dim))] * spread,
+            4 * row_count * inner * spread * head_dim,
+            *operands, times, mod_row, k_weight, v_weight, k_row,
+        )
+        near, far = [pairs[0]], [seq_swap(pairs[0], partner)]
+        for m in range(1, spread):
+            near.append(seq_swap(pairs[m], m))
+        for m in range(1, spread):
+            far.append(seq_swap(near[m], partner))
+        queries = call(
+            functools.partial(q_kernel, plan),
+            [whole((row_count, head_dim))] * spread,
+            2 * row_count * inner * spread * head_dim,
+            rows, scale, q_weight, q_row,
+        )
+        queries = [queries[0]] + [seq_swap(queries[m], m) for m in range(1, spread)]
+        flops = 4 * (spread * row_count) ** 2 * head_dim
+        state3 = call(
+            functools.partial(near_kernel, spread, head_dim),
+            [whole((spread * row_count, 1), F32)] * 2
+            + [whole((spread * row_count, head_dim), F32)],
+            flops,
+            *queries, *near, near_rows, near_keys,
+        )
+        pieces = call(
+            functools.partial(far_kernel, spread, head_dim),
+            [whole((row_count, head_dim))] * spread,
+            flops,
+            *queries, *far, near_rows, far_keys, *state3,
+        )
+        pieces = [pieces[0]] + [seq_swap(pieces[m], m) for m in range(1, spread)]
+        terms = call(
+            functools.partial(out_kernel, plan),
+            [whole((row_count, width))] * n_tp,
+            2 * row_count * spread * head_dim * inner,
+            *pieces, out_weight,
+        )
+        return terms, rows, scale
+
+    def halve(terms):
+        held = dict(enumerate(terms))
+        for bit in bits_of(n_tp)[:-1]:
+            sent = {k: tp_swap(held[k], bit) for k in held if k & bit}
+            held = {
+                k: (held[k].astype(F32) + sent[k ^ bit].astype(F32)).astype(BF16)
+                for k in held
+                if not k & bit
+            }
+        return held
+
+    def spread_low(held):
+        held = dict(held)
+        for bit in reversed(bits_of(n_tp)[:-1]):
+            for k in list(held):
+                held[k ^ bit] = tp_swap(held[k], bit)
+        return [held[k] for k in range(n_tp)]
+
+    top_bit = n_tp // 2
+    blocks = gather_blocks(latents, "tp", n_tp)
+    terms, rows, scale = mixed_terms(blocks, None, start_time)
+
+    student_terms = call(
+        functools.partial(terms_kernel, n_tp),
+        [whole((row_count, width))] * n_tp,
+        2 * row_count * width * inner,
+        rows[:, :width], student_weight, scale,
+    )
+    held_s = halve(student_terms)
+    student = (held_s[0].astype(F32) + tp_swap(held_s[top_bit], top_bit).astype(F32)).astype(BF16)
+
+    held = halve(terms)
+    other = {k ^ top_bit: tp_swap(held[k], top_bit) for k in sorted(held, reverse=True)}
+    near_blocks, far_blocks = spread_low(held), spread_low(other)
+    terms, _, _ = mixed_terms(blocks, (near_blocks, far_blocks), start_time + step_size)
+    held1 = halve(terms)
+    other1 = tp_swap(held1[top_bit], top_bit)
+    target, part = call(
+        loss_kernel,
+        [whole((row_count, width)), whole((8, 128), F32)],
+        10 * row_count * width,
+        held[0], other[0], held1[0], other1, student, own_rows,
+    )
+    part = part + tp_swap(part, 1)
+    for bit in bits_of(n_tp)[1:-1]:
+        part = part + tp_swap(part, bit)
+
+    def both(value, seq_mask, tp_mask):
+        return lax.ppermute(
+            value,
+            ("seq", "tp"),
+            [
+                (s * n_tp + t, (s ^ seq_mask) * n_tp + (t ^ tp_mask))
+                for s in range(n_seq)
+                for t in range(n_tp)
+            ],
+        )
+
+    part = (part + both(part, 0, top_bit)) + (both(part, 1, 0) + both(part, 1, top_bit))
+    low = n_seq // 4
+    part = (part + seq_swap(part, low)) + (seq_swap(part, 2 * low) + seq_swap(part, 3 * low))
+    image_sum = part[0, : lengths.shape[0]]
+    loss = jnp.mean(image_sum / (lengths.astype(F32) * inner))
+    return (target, student, loss)
+
+
 def solution(mesh):
     placed = (
         P("seq", "tp"),
@@ -236,7 +588,17 @@
     )
 
     def body(*arguments):
-        return on_device(dict(mesh.shape), *arguments)
+        latents, q_weight, q_gain = arguments[0], arguments[4], arguments[8]
+        n_seq, n_tp = mesh.shape["seq"], mesh.shape["tp"]
+        heads_here = q_weight.shape[1] // q_gain.shape[0]
+        fused = (
+            latents.shape[1] % 128 == 0
+            and q_gain.shape[0] == 128
+            and n_seq == 2 * heads_here == 8
+            and n_tp in (2, 4)
+        )
+        run = on_device_fused if fused else on_device
+        return run(dict(mesh.shape), *arguments)
 
     return jax.shard_map(
         body,

time: 160 us -> 130 us (0.81)
  waiting for transfers between devices: 56.7 us -> 36.7 us
  matrix products: 18.9 us -> 0 us
  other arithmetic: 21.6 us -> 3.96 us
  Pallas kernels: 0 us -> 16.1 us
  starting transfers between devices: 43.9 us -> 55.5 us
  local copies, waits for them, and re-layouts: 15.5 us -> 11.4 us
  between operations: 3 us -> 5.39 us
    ppermute x34 -> x47, waiting for transfers between devices: 56.7 us -> 33.9 us  [swap(): return lax.ppermute(value, axis, [(i, i ^ mask) for i in range(size)])]
    dot_general x13 -> x0, matrix products: 18.9 us -> none  [the longest x2 4.89 us: teacher(): jnp.dot(hidden, k_weight, preferred_element_type=F32)]
    pallas_call x0 -> x12, Pallas kernels: none -> 16.1 us  [call(): pl.pallas_call(body, out_shape=outs, in_specs=[VM] * len(operands), out_s...]
    reduce_sum x13 -> x1, other arithmetic: 9.09 us -> 0.61 us  [on_device_fused(): loss = jnp.mean(image_sum / (lengths.astype(F32) * inner))]
    ppermute x34 -> x47, starting transfers between devices: 43.9 us -> 52 us  [swap(): return lax.ppermute(value, axis, [(i, i ^ mask) for i in range(size)])]
    reshape x6 -> x0, local copies, waits for them, and re-layouts: 6.46 us -> none  [the longest x4 4.67 us: head_norm(): shaped = projected.reshape(projected.shape[0], -1, gain.shape[0])]
    convert_element_type x10 -> x6, other arithmetic: 6.6 us -> 0.32 us  [the longest x5 0.24 us: halve(): (held[k].astype(F32) + sent[k ^ bit].astype(F32)).astype(BF16)]
    mul x4 -> x0, local copies, waits for them, and re-layouts: 5.56 us -> none  [head_norm(): shaped * shaped]
  transfers between devices with their start and end apart: 34 -> 50, of which waited for: 24 -> 20; matrix products, arithmetic and copies ran while one was open for 7% -> 5% of each run, Pallas kernels for 0% -> 7%
where the time goes in v2:
time: 130 us; the launch traced here: 129 us
  starting transfers between devices  55.5 us (43%)
  waiting for transfers between devices  36.7 us (28%)
  Pallas kernels  16.1 us (12%)
  local copies, waits for them, and re-layouts  11.4 us (9%)
  between operations  5.39 us (4%)
  other arithmetic  3.96 us (3%)
    ppermute x47, starting transfers between devices, swap(): return lax.ppermute(value, axis, [(i, i ^ mask) for i in range(size)])  52 us
    ppermute x47, waiting for transfers between devices, swap(): return lax.ppermute(value, axis, [(i, i ^ mask) for i in range(size)])  33.9 us
    pallas_call x12, Pallas kernels, call(): pl.pallas_call(body, out_shape=outs, in_specs=[VM] * len(operands), out_s...  16.1 us
    unnamed x52, local copies, waits for them, and re-layouts  7.72 us
    ppermute x3, starting transfers between devices, both(): lax.ppermute(value, ('seq', 'tp'), [(s * n_tp + t, (s ^ seq_mask) * n_tp...  3.49 us
    ppermute x3, waiting for transfers between devices, both(): lax.ppermute(value, ('seq', 'tp'), [(s * n_tp + t, (s ^ seq_mask) * n_tp...  2.8 us
  transfers between devices with their start and end apart: 50, of which 20 were waited for; matrix products, arithmetic and copies ran while one was open for 5% of the time, Pallas kernels for 7%

profile of v2, /device:TPU:0, one launch (start us, length us, event | category | flops | bytes accessed | tf_op | source)
XLA Modules:
  0.0 129.1 jit_solution(15851008907163771516)
XLA Ops:
  0.6 3.0 %collective-permute-start.1 = (bf16[128,768]{1,0:T(8,128)(2,1)}, bf16[128,768]{1,0:T(8,128)(2,1)S(1)}, u32[]{:S(2)}, u32[]{:S(2)}) collective-permute-start(bf16[128,768]{1,0:T(8,128)(2,1)} %refs_0_.3), channel_id=1, source_target_pairs={{0,2},{1,3},{2,0},{3,1},{4,6},{5,7},{6,4},{7,5},{8,10},{9,11},{10,... | collective-permute-start | bytes 589832 | tf_op jit(solution)/shard_map/ppermute | solution.py:23
  11.1 2.0 %copy-done.1 = bf16[3072,512]{1,0:T(8,128)(2,1)S(1)} copy-done((bf16[3072,512]{1,0:T(8,128)(2,1)S(1)}, bf16[3072,512]{1,0:T(8,128)(2,1)}, u32[]{:S(2)}) %copy-start.1) | copy-done | bytes 3145752
  13.0 1.9 %copy-done.3 = bf16[3072,512]{1,0:T(8,128)(2,1)S(1)} copy-done((bf16[3072,512]{1,0:T(8,128)(2,1)S(1)}, bf16[3072,512]{1,0:T(8,128)(2,1)}, u32[]{:S(2)}) %copy-start.3) | copy-done | bytes 3145752
  17.2 1.7 %shard_map.130 = (bf16[128,3072]{1,0:T(8,128)(2,1)S(1)}, f32[128,1]{1,0:T(8,128)S(1)}, bf16[128,256]{1,0:T(8,128)(2,1)}, bf16[128,256]{1,0:T(8,128)(2,1)S(1)}, b...) custom-call(bf16[128,768]{1,0:T(8,128)(2,1)S(1)} %copy-done.10, ...), custom_call_target="tpu_custom_call" | custom-call | flops 805306368 | bytes 7091200 | tf_op jit(solution)/shard_map/pallas_call | solution.py:236
  22.0 1.6 %collective-permute-start.4 = (bf16[128,128]{1,0:T(8,128)(2,1)S(1)}, bf16[128,128]{1,0:T(8,128)(2,1)S(1)}, u32[]{:S(2)}, u32[]{:S(2)}) collective-permute-start(bf16[128,128]{1,0:T(8,128)(2,1)S(1)} %get-tuple-element.55), channel_id=1, source_target_pairs={{0,8},{4,12},{8,0},{12,4},{16,24},{20,28},{24,16},{28,20},{1,9},{5... | collective-permute-start | bytes 98312 | tf_op jit(solution)/shard_map/ppermute | solution.py:23
  25.5 1.6 %collective-permute-start.9 = (bf16[128,256]{1,0:T(8,128)(2,1)S(1)}, bf16[128,256]{1,0:T(8,128)(2,1)}, u32[]{:S(2)}, u32[]{:S(2)}) collective-permute-start(bf16[128,256]{1,0:T(8,128)(2,1)S(1)} %get-tuple-element.59), channel_id=1, source_target_pairs={{0,8},{4,12},{8,0},{12,4},{16,24},{20,28},{24,16},{28,20},{1,9},{5... | collective-permute-start | bytes 196616 | tf_op jit(solution)/shard_map/ppermute | solution.py:23
  28.1 3.6 %collective-permute-start.6 = (bf16[128,256]{1,0:T(8,128)(2,1)}, bf16[128,256]{1,0:T(8,128)(2,1)}, u32[]{:S(2)}, u32[]{:S(2)}) collective-permute-start(bf16[128,256]{1,0:T(8,128)(2,1)} %get-tuple-element.57.refs_4_), channel_id=1, source_target_pairs={{0,24},{4,28},{8,16},{12,20},{16,8},{20,12},{24,0},{28,4},{1,25},{... | collective-permute-start | bytes 196616 | tf_op jit(solution)/shard_map/ppermute | solution.py:23
  31.7 1.8 %collective-permute-start.10 = (bf16[128,256]{1,0:T(8,128)(2,1)}, bf16[128,256]{1,0:T(8,128)(2,1)}, u32[]{:S(2)}, u32[]{:S(2)}) collective-permute-start(bf16[128,256]{1,0:T(8,128)(2,1)} %collective-permute-done.9.refs_6_), channel_id=1, source_target_pairs={{0,24},{4,28},{8,16},{12,20},{16,8},{20,12},{24,0},{28,4},{1,25},{... | collective-permute-start | bytes 196616 | tf_op jit(solution)/shard_map/ppermute | solution.py:23
  33.5 2.0 %collective-permute-start.12 = (bf16[128,256]{1,0:T(8,128)(2,1)}, bf16[128,256]{1,0:T(8,128)(2,1)}, u32[]{:S(2)}, u32[]{:S(2)}) collective-permute-start(bf16[128,256]{1,0:T(8,128)(2,1)} %collective-permute-done.11.refs_7_), channel_id=1, source_target_pairs={{0,24},{4,28},{8,16},{12,20},{16,8},{20,12},{24,0},{28,4},{1,25},{... | collective-permute-start | bytes 196616 | tf_op jit(solution)/shard_map/ppermute | solution.py:23
  35.5 1.8 %collective-permute-start.8 = (bf16[128,256]{1,0:T(8,128)(2,1)}, bf16[128,256]{1,0:T(8,128)(2,1)}, u32[]{:S(2)}, u32[]{:S(2)}) collective-permute-start(bf16[128,256]{1,0:T(8,128)(2,1)} %collective-permute-done.7.refs_5_), channel_id=1, source_target_pairs={{0,24},{4,28},{8,16},{12,20},{16,8},{20,12},{24,0},{28,4},{1,25},{... | collective-permute-start | bytes 196616 | tf_op jit(solution)/shard_map/ppermute | solution.py:23
  38.9 2.2 %shard_map.132 = (f32[512,1]{1,0:T(8,128)S(1)}, f32[512,1]{1,0:T(8,128)S(1)}, f32[512,128]{1,0:T(8,128)S(1)}) custom-call(bf16[128,128]{1,0:T(8,128)(2,1)S(1)} %get-tuple-element.53.refs_0_, bf16[128,128]{1,0:T(8,128)(2,1)S(1)} %collective-permute-done.3.refs_1_, bf16[128,128]{1,0:T(8,128)(2,1)S(1)} %copy-done.19, ...), custom_call_target="tpu_custom_call" | custom-call | flops 134217728 | bytes 397312 | tf_op jit(solution)/shard_map/pallas_call | solution.py:236
  42.0 2.7 %shard_map.133 = (bf16[128,128]{1,0:T(8,128)(2,1)S(1)}, bf16[128,128]{1,0:T(8,128)(2,1)S(1)}, bf16[128,128]{1,0:T(8,128)(2,1)S(1)}, bf16[128,128]{1,0:T(8,128)(2,1)S(1)}) custom-call(bf16[128,128]{1,0:T(8,128)(2,1)S(1)} %get-tuple-element.53.refs_0_, bf16[128,128]{1,0:T(8,128)(2,1)S(1)} %collective-permute-done.3.refs_1_, bf16[128,128]{1,0:T(8,128)(2,1)S(1)} %copy-done.19, ...), custom_call_target="tpu_custom_call" | custom-call | flops 134217728 | bytes 663552 | tf_op jit(solution)/shard_map/pallas_call | solution.py:236
  44.7 1.6 %collective-permute-start.13 = (bf16[128,128]{1,0:T(8,128)(2,1)S(1)}, bf16[128,128]{1,0:T(8,128)(2,1)S(1)}, u32[]{:S(2)}, u32[]{:S(2)}) collective-permute-start(bf16[128,128]{1,0:T(8,128)(2,1)S(1)} %get-tuple-element.65), channel_id=1, source_target_pairs={{0,4},{4,0},{8,12},{12,8},{16,20},{20,16},{24,28},{28,24},{1,5},{5... | collective-permute-start | bytes 98312 | tf_op jit(solution)/shard_map/ppermute | solution.py:23
  50.1 1.6 %collective-permute-done.15.refs_3_ = bf16[128,128]{1,0:T(8,128)(2,1)S(1)} collective-permute-done((bf16[128,128]{1,0:T(8,128)(2,1)S(1)}, bf16[128,128]{1,0:T(8,128)(2,1)S(1)}, u32[]{:S(2)}, u32[]{:S(2)}) %collective-permute-start.15) | collective-permute-done | bytes 32800 | tf_op jit(solution)/shard_map/ppermute | solution.py:23
  54.2 2.0 %collective-permute-start.22 = (bf16[128,768]{1,0:T(8,128)(2,1)S(1)}, bf16[128,768]{1,0:T(8,128)(2,1)S(1)}, u32[]{:S(2)}, u32[]{:S(2)}) collective-permute-start(bf16[128,768]{1,0:T(8,128)(2,1)S(1)} %add_convert_fusion.6.refs_4_.refs_0_), channel_id=1, source_target_pairs={{0,2},{1,3},{2,0},{3,1},{4,6},{5,7},{6,4},{7,5},{8,10},{9,11},{10,... | collective-permute-start | bytes 589832 | tf_op jit(solution)/shard_map/ppermute | solution.py:23
  56.7 5.1 %collective-permute-done.18.refs_8_.refs_1_ = bf16[128,768]{1,0:T(8,128)(2,1)S(1)} collective-permute-done((bf16[128,768]{1,0:T(8,128)(2,1)S(1)}, bf16[128,768]{1,0:T(8,128)(2,1)S(1)}, u32[]{:S(2)}, u32[]{:S(2)}) %collective-permute-start.18) | collective-permute-done | bytes 196640 | tf_op jit(solution)/shard_map/ppermute | solution.py:23
  61.8 3.4 %collective-permute-done.22.refs_10_ = bf16[128,768]{1,0:T(8,128)(2,1)S(1)} collective-permute-done((bf16[128,768]{1,0:T(8,128)(2,1)S(1)}, bf16[128,768]{1,0:T(8,128)(2,1)S(1)}, u32[]{:S(2)}, u32[]{:S(2)}) %collective-permute-start.22) | collective-permute-done | bytes 196640 | tf_op jit(solution)/shard_map/ppermute | solution.py:23
  68.3 1.5 %shard_map.135 = (bf16[128,3072]{1,0:T(8,128)(2,1)S(1)}, f32[128,1]{1,0:T(8,128)S(1)}, bf16[128,256]{1,0:T(8,128)(2,1)S(1)}, bf16[128,256]{1,0:T(8,128)(2,1)S(1)...) custom-call(bf16[128,768]{1,0:T(8,128)(2,1)S(1)} %copy-done.11, bf16[128,768]{1,0:T(8,128)(2,1)S(1)} %copy-done.15, ...), custom_call_target="tpu_custom_call" | custom-call | flops 805306368 | bytes 8664064 | tf_op jit(solution)/shard_map/pallas_call | solution.py:236
  71.9 1.5 %collective-permute-start.32 = (bf16[128,256]{1,0:T(8,128)(2,1)S(1)}, bf16[128,256]{1,0:T(8,128)(2,1)S(1)}, u32[]{:S(2)}, u32[]{:S(2)}) collective-permute-start(bf16[128,256]{1,0:T(8,128)(2,1)S(1)} %get-tuple-element.81), channel_id=1, source_target_pairs={{0,12},{4,8},{8,4},{12,0},{16,28},{20,24},{24,20},{28,16},{1,13},{... | collective-permute-start | bytes 196616 | tf_op jit(solution)/shard_map/ppermute | solution.py:23
  76.2 2.0 %collective-permute-done.24.refs_1_ = bf16[128,128]{1,0:T(8,128)(2,1)S(1)} collective-permute-done((bf16[128,128]{1,0:T(8,128)(2,1)S(1)}, bf16[128,128]{1,0:T(8,128)(2,1)S(1)}, u32[]{:S(2)}, u32[]{:S(2)}) %collective-permute-start.24) | collective-permute-done | bytes 32800 | tf_op jit(solution)/shard_map/ppermute | solution.py:23
  79.5 2.6 %collective-permute-start.27 = (bf16[128,256]{1,0:T(8,128)(2,1)S(1)}, bf16[128,256]{1,0:T(8,128)(2,1)S(1)}, u32[]{:S(2)}, u32[]{:S(2)}) collective-permute-start(bf16[128,256]{1,0:T(8,128)(2,1)S(1)} %get-tuple-element.78.refs_4_), channel_id=1, source_target_pairs={{0,24},{4,28},{8,16},{12,20},{16,8},{20,12},{24,0},{28,4},{1,25},{... | collective-permute-start | bytes 196616 | tf_op jit(solution)/shard_map/ppermute | solution.py:23
  83.4 2.6 %collective-permute-start.31 = (bf16[128,256]{1,0:T(8,128)(2,1)S(1)}, bf16[128,256]{1,0:T(8,128)(2,1)S(1)}, u32[]{:S(2)}, u32[]{:S(2)}) collective-permute-start(bf16[128,256]{1,0:T(8,128)(2,1)S(1)} %collective-permute-done.30.refs_6_), channel_id=1, source_target_pairs={{0,24},{4,28},{8,16},{12,20},{16,8},{20,12},{24,0},{28,4},{1,25},{... | collective-permute-start | bytes 196616 | tf_op jit(solution)/shard_map/ppermute | solution.py:23
  89.5 2.6 %collective-permute-done.33.refs_7_ = bf16[128,256]{1,0:T(8,128)(2,1)S(1)} collective-permute-done((bf16[128,256]{1,0:T(8,128)(2,1)S(1)}, bf16[128,256]{1,0:T(8,128)(2,1)S(1)}, u32[]{:S(2)}, u32[]{:S(2)}) %collective-permute-start.33) | collective-permute-done | bytes 65568 | tf_op jit(solution)/shard_map/ppermute | solution.py:23
  92.2 1.6 %shard_map.138 = (bf16[128,128]{1,0:T(8,128)(2,1)S(1)}, bf16[128,128]{1,0:T(8,128)(2,1)S(1)}, bf16[128,128]{1,0:T(8,128)(2,1)S(1)}, bf16[128,128]{1,0:T(8,128)(2,1)S(1)}) custom-call(bf16[128,128]{1,0:T(8,128)(2,1)S(1)} %get-tuple-element.74.refs_0_, bf16[128,128]{1,0:T(8,128)(2,1)S(1)} %collective-permute-done.24.refs_1_, ...), custom_call_target="tpu_custom_call" | custom-call | flops 134217728 | bytes 663552 | tf_op jit(solution)/shard_map/pallas_call | solution.py:236
  94.7 1.5 %collective-permute-start.35 = (bf16[128,128]{1,0:T(8,128)(2,1)S(1)}, bf16[128,128]{1,0:T(8,128)(2,1)S(1)}, u32[]{:S(2)}, u32[]{:S(2)}) collective-permute-start(bf16[128,128]{1,0:T(8,128)(2,1)S(1)} %get-tuple-element.87), channel_id=1, source_target_pairs={{0,8},{4,12},{8,0},{12,4},{16,24},{20,28},{24,16},{28,20},{1,9},{5... | collective-permute-start | bytes 98312 | tf_op jit(solution)/shard_map/ppermute | solution.py:23
  98.8 2.2 %collective-permute-done.36.refs_3_ = bf16[128,128]{1,0:T(8,128)(2,1)S(1)} collective-permute-done((bf16[128,128]{1,0:T(8,128)(2,1)S(1)}, bf16[128,128]{1,0:T(8,128)(2,1)S(1)}, u32[]{:S(2)}, u32[]{:S(2)}) %collective-permute-start.36) | collective-permute-done | bytes 32800 | tf_op jit(solution)/shard_map/ppermute | solution.py:23
  104.0 6.3 %collective-permute-done.39.refs_3_ = bf16[128,768]{1,0:T(8,128)(2,1)S(1)} collective-permute-done((bf16[128,768]{1,0:T(8,128)(2,1)S(1)}, bf16[128,768]{1,0:T(8,128)(2,1)S(1)}, u32[]{:S(2)}, u32[]{:S(2)}) %collective-permute-start.39) | collective-permute-done | bytes 196640 | tf_op jit(solution)/shard_map/ppermute | solution.py:23
  114.1 1.7 %collective-permute-start.46 = (f32[8,128]{1,0:T(8,128)S(1)}, f32[8,128]{1,0:T(8,128)S(1)}, u32[]{:S(2)}, u32[]{:S(2)}) collective-permute-start(f32[8,128]{1,0:T(8,128)S(1)} %add.222), channel_id=1, source_target_pairs={{0,6},{1,7},{2,4},{3,5},{4,2},{5,3},{6,0},{7,1},{8,14},{9,15},{10,... | collective-permute-start | bytes 12296 | tf_op jit(solution)/shard_map/ppermute | solution.py:557
  116.6 2.1 %collective-permute-done.46 = f32[8,128]{1,0:T(8,128)S(1)} collective-permute-done((f32[8,128]{1,0:T(8,128)S(1)}, f32[8,128]{1,0:T(8,128)S(1)}, u32[]{:S(2)}, u32[]{:S(2)}) %collective-permute-start.46) | collective-permute-done | bytes 4128 | tf_op jit(solution)/shard_map/ppermute | solution.py:557
  119.2 2.1 %collective-permute-start.48 = (f32[8,128]{1,0:T(8,128)S(1)}, f32[8,128]{1,0:T(8,128)S(1)}, u32[]{:S(2)}, u32[]{:S(2)}) collective-permute-start(f32[8,128]{1,0:T(8,128)S(1)} %add_add_fusion.1), channel_id=1, source_target_pairs={{0,16},{4,20},{8,24},{12,28},{16,0},{20,4},{24,8},{28,12},{1,17},{... | collective-permute-start | bytes 12296 | tf_op jit(solution)/shard_map/ppermute | solution.py:23
  121.2 1.8 %collective-permute-start.49 = (f32[8,128]{1,0:T(8,128)S(1)}, f32[8,128]{1,0:T(8,128)S(1)}, u32[]{:S(2)}, u32[]{:S(2)}) collective-permute-start(f32[8,128]{1,0:T(8,128)S(1)} %add_add_fusion.1), channel_id=1, source_target_pairs={{0,24},{4,28},{8,16},{12,20},{16,8},{20,12},{24,0},{28,4},{1,25},{... | collective-permute-start | bytes 12296 | tf_op jit(solution)/shard_map/ppermute | solution.py:23
  123.7 3.0 %collective-permute-done.49 = f32[8,128]{1,0:T(8,128)S(1)} collective-permute-done((f32[8,128]{1,0:T(8,128)S(1)}, f32[8,128]{1,0:T(8,128)S(1)}, u32[]{:S(2)}, u32[]{:S(2)}) %collective-permute-start.49) | collective-permute-done | bytes 4128 | tf_op jit(solution)/shard_map/ppermute | solution.py:23
  (153 shorter events, 49.0 us)
Async XLA Ops:
  0.6 8.8 %collective-permute-start.1 = (bf16[128,768]{1,0:T(8,128)(2,1)}, bf16[128,768]{1,0:T(8,128)(2,1)S(1)}, u32[]{:S(2)}, u32[]{:S(2)}) collective-permute-start(bf16[128,768]{1,0:T(8,128)(2,1)} %refs_0_.3), channel_id=1, source_target_pairs={{0,2},{1,3},{2,0},{3,1},{4,6},{5,7},{6,4},{7,5},{8,10},{9,11},{10,... | collective-permute-start | bytes 589832 | tf_op jit(solution)/shard_map/ppermute | solution.py:23
  3.7 7.0 %collective-permute-start = (bf16[128,768]{1,0:T(8,128)(2,1)}, bf16[128,768]{1,0:T(8,128)(2,1)S(1)}, u32[]{:S(2)}, u32[]{:S(2)}) collective-permute-start(bf16[128,768]{1,0:T(8,128)(2,1)} %refs_0_.3), channel_id=1, source_target_pairs={{0,1},{1,0},{2,3},{3,2},{4,5},{5,4},{6,7},{7,6},{8,9},{9,8},{10,11... | collective-permute-start | bytes 589832 | tf_op jit(solution)/shard_map/ppermute | solution.py:23
  20.5 6.6 %collective-permute-start.3 = (bf16[128,128]{1,0:T(8,128)(2,1)S(1)}, bf16[128,128]{1,0:T(8,128)(2,1)S(1)}, u32[]{:S(2)}, u32[]{:S(2)}) collective-permute-start(bf16[128,128]{1,0:T(8,128)(2,1)S(1)} %get-tuple-element.54), channel_id=1, source_target_pairs={{0,4},{4,0},{8,12},{12,8},{16,20},{20,16},{24,28},{28,24},{1,5},{5... | collective-permute-start | bytes 98312 | tf_op jit(solution)/shard_map/ppermute | solution.py:23
  22.0 5.5 %collective-permute-start.4 = (bf16[128,128]{1,0:T(8,128)(2,1)S(1)}, bf16[128,128]{1,0:T(8,128)(2,1)S(1)}, u32[]{:S(2)}, u32[]{:S(2)}) collective-permute-start(bf16[128,128]{1,0:T(8,128)(2,1)S(1)} %get-tuple-element.55), channel_id=1, source_target_pairs={{0,8},{4,12},{8,0},{12,4},{16,24},{20,28},{24,16},{28,20},{1,9},{5... | collective-permute-start | bytes 98312 | tf_op jit(solution)/shard_map/ppermute | solution.py:23
  23.6 9.9 %collective-permute-start.11 = (bf16[128,256]{1,0:T(8,128)(2,1)S(1)}, bf16[128,256]{1,0:T(8,128)(2,1)}, u32[]{:S(2)}, u32[]{:S(2)}) collective-permute-start(bf16[128,256]{1,0:T(8,128)(2,1)S(1)} %get-tuple-element.60), channel_id=1, source_target_pairs={{0,12},{4,8},{8,4},{12,0},{16,28},{20,24},{24,20},{28,16},{1,13},{... | collective-permute-start | bytes 196616 | tf_op jit(solution)/shard_map/ppermute | solution.py:23
  24.0 11.5 %collective-permute-start.7 = (bf16[128,256]{1,0:T(8,128)(2,1)S(1)}, bf16[128,256]{1,0:T(8,128)(2,1)}, u32[]{:S(2)}, u32[]{:S(2)}) collective-permute-start(bf16[128,256]{1,0:T(8,128)(2,1)S(1)} %get-tuple-element.58), channel_id=1, source_target_pairs={{0,4},{4,0},{8,12},{12,8},{16,20},{20,16},{24,28},{28,24},{1,5},{5... | collective-permute-start | bytes 196616 | tf_op jit(solution)/shard_map/ppermute | solution.py:23
  25.5 6.2 %collective-permute-start.9 = (bf16[128,256]{1,0:T(8,128)(2,1)S(1)}, bf16[128,256]{1,0:T(8,128)(2,1)}, u32[]{:S(2)}, u32[]{:S(2)}) collective-permute-start(bf16[128,256]{1,0:T(8,128)(2,1)S(1)} %get-tuple-element.59), channel_id=1, source_target_pairs={{0,8},{4,12},{8,0},{12,4},{16,24},{20,28},{24,16},{28,20},{1,9},{5... | collective-permute-start | bytes 196616 | tf_op jit(solution)/shard_map/ppermute | solution.py:23
  27.1 11.0 %collective-permute-start.5 = (bf16[128,128]{1,0:T(8,128)(2,1)}, bf16[128,128]{1,0:T(8,128)(2,1)}, u32[]{:S(2)}, u32[]{:S(2)}) collective-permute-start(bf16[128,128]{1,0:T(8,128)(2,1)} %get-tuple-element.56), channel_id=1, source_target_pairs={{0,12},{4,8},{8,4},{12,0},{16,28},{20,24},{24,20},{28,16},{1,13},{... | collective-permute-start | bytes 98312 | tf_op jit(solution)/shard_map/ppermute | solution.py:23
  28.1 13.0 %collective-permute-start.6 = (bf16[128,256]{1,0:T(8,128)(2,1)}, bf16[128,256]{1,0:T(8,128)(2,1)}, u32[]{:S(2)}, u32[]{:S(2)}) collective-permute-start(bf16[128,256]{1,0:T(8,128)(2,1)} %get-tuple-element.57.refs_4_), channel_id=1, source_target_pairs={{0,24},{4,28},{8,16},{12,20},{16,8},{20,12},{24,0},{28,4},{1,25},{... | collective-permute-start | bytes 196616 | tf_op jit(solution)/shard_map/ppermute | solution.py:23
  31.7 9.4 %collective-permute-start.10 = (bf16[128,256]{1,0:T(8,128)(2,1)}, bf16[128,256]{1,0:T(8,128)(2,1)}, u32[]{:S(2)}, u32[]{:S(2)}) collective-permute-start(bf16[128,256]{1,0:T(8,128)(2,1)} %collective-permute-done.9.refs_6_), channel_id=1, source_target_pairs={{0,24},{4,28},{8,16},{12,20},{16,8},{20,12},{24,0},{28,4},{1,25},{... | collective-permute-start | bytes 196616 | tf_op jit(solution)/shard_map/ppermute | solution.py:23
  33.5 7.6 %collective-permute-start.12 = (bf16[128,256]{1,0:T(8,128)(2,1)}, bf16[128,256]{1,0:T(8,128)(2,1)}, u32[]{:S(2)}, u32[]{:S(2)}) collective-permute-start(bf16[128,256]{1,0:T(8,128)(2,1)} %collective-permute-done.11.refs_7_), channel_id=1, source_target_pairs={{0,24},{4,28},{8,16},{12,20},{16,8},{20,12},{24,0},{28,4},{1,25},{... | collective-permute-start | bytes 196616 | tf_op jit(solution)/shard_map/ppermute | solution.py:23
  35.5 6.5 %collective-permute-start.8 = (bf16[128,256]{1,0:T(8,128)(2,1)}, bf16[128,256]{1,0:T(8,128)(2,1)}, u32[]{:S(2)}, u32[]{:S(2)}) collective-permute-start(bf16[128,256]{1,0:T(8,128)(2,1)} %collective-permute-done.7.refs_5_), channel_id=1, source_target_pairs={{0,24},{4,28},{8,16},{12,20},{16,8},{20,12},{24,0},{28,4},{1,25},{... | collective-permute-start | bytes 196616 | tf_op jit(solution)/shard_map/ppermute | solution.py:23
  46.9 4.8 %collective-permute-start.15 = (bf16[128,128]{1,0:T(8,128)(2,1)S(1)}, bf16[128,128]{1,0:T(8,128)(2,1)S(1)}, u32[]{:S(2)}, u32[]{:S(2)}) collective-permute-start(bf16[128,128]{1,0:T(8,128)(2,1)S(1)} %get-tuple-element.67), channel_id=1, source_target_pairs={{0,12},{4,8},{8,4},{12,0},{16,28},{20,24},{24,20},{28,16},{1,13},{... | collective-permute-start | bytes 98312 | tf_op jit(solution)/shard_map/ppermute | solution.py:23
  54.0 7.8 %collective-permute-start.18 = (bf16[128,768]{1,0:T(8,128)(2,1)S(1)}, bf16[128,768]{1,0:T(8,128)(2,1)S(1)}, u32[]{:S(2)}, u32[]{:S(2)}) collective-permute-start(bf16[128,768]{1,0:T(8,128)(2,1)S(1)} %add_convert_fusion.5.refs_6_), channel_id=1, source_target_pairs={{0,2},{1,3},{2,0},{3,1},{4,6},{5,7},{6,4},{7,5},{8,10},{9,11},{10,... | collective-permute-start | bytes 589832 | tf_op jit(solution)/shard_map/ppermute | solution.py:23
  54.2 11.0 %collective-permute-start.22 = (bf16[128,768]{1,0:T(8,128)(2,1)S(1)}, bf16[128,768]{1,0:T(8,128)(2,1)S(1)}, u32[]{:S(2)}, u32[]{:S(2)}) collective-permute-start(bf16[128,768]{1,0:T(8,128)(2,1)S(1)} %add_convert_fusion.6.refs_4_.refs_0_), channel_id=1, source_target_pairs={{0,2},{1,3},{2,0},{3,1},{4,6},{5,7},{6,4},{7,5},{8,10},{9,11},{10,... | collective-permute-start | bytes 589832 | tf_op jit(solution)/shard_map/ppermute | solution.py:23
  56.2 12.0 %collective-permute-start.20 = (bf16[128,768]{1,0:T(8,128)(2,1)S(1)}, bf16[128,768]{1,0:T(8,128)(2,1)S(1)}, u32[]{:S(2)}, u32[]{:S(2)}) collective-permute-start(bf16[128,768]{1,0:T(8,128)(2,1)S(1)} %add_convert_fusion.5.refs_6_), channel_id=1, source_target_pairs={{0,1},{1,0},{2,3},{3,2},{4,5},{5,4},{6,7},{7,6},{8,9},{9,8},{10,11... | collective-permute-start | bytes 589832 | tf_op jit(solution)/shard_map/ppermute | solution.py:23
  56.2 12.0 %collective-permute-start.19 = (bf16[128,768]{1,0:T(8,128)(2,1)S(1)}, bf16[128,768]{1,0:T(8,128)(2,1)S(1)}, u32[]{:S(2)}, u32[]{:S(2)}) collective-permute-start(bf16[128,768]{1,0:T(8,128)(2,1)S(1)} %add_convert_fusion.6.refs_4_.refs_0_), channel_id=1, source_target_pairs={{0,1},{1,0},{2,3},{3,2},{4,5},{5,4},{6,7},{7,6},{8,9},{9,8},{10,11... | collective-permute-start | bytes 589832 | tf_op jit(solution)/shard_map/ppermute | solution.py:23
  61.8 6.4 %collective-permute-start.21 = (bf16[128,768]{1,0:T(8,128)(2,1)S(1)}, bf16[128,768]{1,0:T(8,128)(2,1)S(1)}, u32[]{:S(2)}, u32[]{:S(2)}) collective-permute-start(bf16[128,768]{1,0:T(8,128)(2,1)S(1)} %collective-permute-done.18.refs_8_.refs_1_), channel_id=1, source_target_pairs={{0,1},{1,0},{2,3},{3,2},{4,5},{5,4},{6,7},{7,6},{8,9},{9,8},{10,11... | collective-permute-start | bytes 589832 | tf_op jit(solution)/shard_map/ppermute | solution.py:23
  67.0 8.2 %collective-permute-start.41 = (bf16[128,768]{1,0:T(8,128)(2,1)S(1)}, bf16[128,768]{1,0:T(8,128)(2,1)S(1)}, u32[]{:S(2)}, u32[]{:S(2)}) collective-permute-start(bf16[128,768]{1,0:T(8,128)(2,1)S(1)} %get-tuple-element.96), channel_id=1, source_target_pairs={{0,1},{1,0},{2,3},{3,2},{4,5},{5,4},{6,7},{7,6},{8,9},{9,8},{10,11... | collective-permute-start | bytes 589832 | tf_op jit(solution)/shard_map/ppermute | solution.py:23
  69.8 12.3 %collective-permute-start.28 = (bf16[128,256]{1,0:T(8,128)(2,1)S(1)}, bf16[128,256]{1,0:T(8,128)(2,1)S(1)}, u32[]{:S(2)}, u32[]{:S(2)}) collective-permute-start(bf16[128,256]{1,0:T(8,128)(2,1)S(1)} %get-tuple-element.79), channel_id=1, source_target_pairs={{0,4},{4,0},{8,12},{12,8},{16,20},{20,16},{24,28},{28,24},{1,5},{5... | collective-permute-start | bytes 196616 | tf_op jit(solution)/shard_map/ppermute | solution.py:23
  70.8 12.5 %collective-permute-start.30 = (bf16[128,256]{1,0:T(8,128)(2,1)S(1)}, bf16[128,256]{1,0:T(8,128)(2,1)S(1)}, u32[]{:S(2)}, u32[]{:S(2)}) collective-permute-start(bf16[128,256]{1,0:T(8,128)(2,1)S(1)} %get-tuple-element.80), channel_id=1, source_target_pairs={{0,8},{4,12},{8,0},{12,4},{16,24},{20,28},{24,16},{28,20},{1,9},{5... | collective-permute-start | bytes 196616 | tf_op jit(solution)/shard_map/ppermute | solution.py:23
  71.9 14.2 %collective-permute-start.32 = (bf16[128,256]{1,0:T(8,128)(2,1)S(1)}, bf16[128,256]{1,0:T(8,128)(2,1)S(1)}, u32[]{:S(2)}, u32[]{:S(2)}) collective-permute-start(bf16[128,256]{1,0:T(8,128)(2,1)S(1)} %get-tuple-element.81), channel_id=1, source_target_pairs={{0,12},{4,8},{8,4},{12,0},{16,28},{20,24},{24,20},{28,16},{1,13},{... | collective-permute-start | bytes 196616 | tf_op jit(solution)/shard_map/ppermute | solution.py:23
  78.2 9.1 %collective-permute-start.26 = (bf16[128,128]{1,0:T(8,128)(2,1)S(1)}, bf16[128,128]{1,0:T(8,128)(2,1)S(1)}, u32[]{:S(2)}, u32[]{:S(2)}) collective-permute-start(bf16[128,128]{1,0:T(8,128)(2,1)S(1)} %get-tuple-element.77), channel_id=1, source_target_pairs={{0,12},{4,8},{8,4},{12,0},{16,28},{20,24},{24,20},{28,16},{1,13},{... | collective-permute-start | bytes 98312 | tf_op jit(solution)/shard_map/ppermute | solution.py:23
  79.5 7.8 %collective-permute-start.27 = (bf16[128,256]{1,0:T(8,128)(2,1)S(1)}, bf16[128,256]{1,0:T(8,128)(2,1)S(1)}, u32[]{:S(2)}, u32[]{:S(2)}) collective-permute-start(bf16[128,256]{1,0:T(8,128)(2,1)S(1)} %get-tuple-element.78.refs_4_), channel_id=1, source_target_pairs={{0,24},{4,28},{8,16},{12,20},{16,8},{20,12},{24,0},{28,4},{1,25},{... | collective-permute-start | bytes 196616 | tf_op jit(solution)/shard_map/ppermute | solution.py:23
  82.2 7.3 %collective-permute-start.29 = (bf16[128,256]{1,0:T(8,128)(2,1)S(1)}, bf16[128,256]{1,0:T(8,128)(2,1)S(1)}, u32[]{:S(2)}, u32[]{:S(2)}) collective-permute-start(bf16[128,256]{1,0:T(8,128)(2,1)S(1)} %collective-permute-done.28.refs_5_), channel_id=1, source_target_pairs={{0,24},{4,28},{8,16},{12,20},{16,8},{20,12},{24,0},{28,4},{1,25},{... | collective-permute-start | bytes 196616 | tf_op jit(solution)/shard_map/ppermute | solution.py:23
  83.4 6.2 %collective-permute-start.31 = (bf16[128,256]{1,0:T(8,128)(2,1)S(1)}, bf16[128,256]{1,0:T(8,128)(2,1)S(1)}, u32[]{:S(2)}, u32[]{:S(2)}) collective-permute-start(bf16[128,256]{1,0:T(8,128)(2,1)S(1)} %collective-permute-done.30.refs_6_), channel_id=1, source_target_pairs={{0,24},{4,28},{8,16},{12,20},{16,8},{20,12},{24,0},{28,4},{1,25},{... | collective-permute-start | bytes 196616 | tf_op jit(solution)/shard_map/ppermute | solution.py:23
  86.0 6.2 %collective-permute-start.33 = (bf16[128,256]{1,0:T(8,128)(2,1)S(1)}, bf16[128,256]{1,0:T(8,128)(2,1)S(1)}, u32[]{:S(2)}, u32[]{:S(2)}) collective-permute-start(bf16[128,256]{1,0:T(8,128)(2,1)S(1)} %collective-permute-done.32.refs_7_), channel_id=1, source_target_pairs={{0,24},{4,28},{8,16},{12,20},{16,8},{20,12},{24,0},{28,4},{1,25},{... | collective-permute-start | bytes 196616 | tf_op jit(solution)/shard_map/ppermute | solution.py:23
  87.3 14.5 %collective-permute-start.40 = (bf16[128,768]{1,0:T(8,128)(2,1)S(1)}, bf16[128,768]{1,0:T(8,128)(2,1)S(1)}, u32[]{:S(2)}, u32[]{:S(2)}) collective-permute-start(bf16[128,768]{1,0:T(8,128)(2,1)S(1)} %get-tuple-element.94), channel_id=1, source_target_pairs={{0,1},{1,0},{2,3},{3,2},{4,5},{5,4},{6,7},{7,6},{8,9},{9,8},{10,11... | collective-permute-start | bytes 589832 | tf_op jit(solution)/shard_map/ppermute | solution.py:23
  87.4 14.4 %collective-permute-start.42 = (bf16[128,768]{1,0:T(8,128)(2,1)S(1)}, bf16[128,768]{1,0:T(8,128)(2,1)S(1)}, u32[]{:S(2)}, u32[]{:S(2)}) collective-permute-start(bf16[128,768]{1,0:T(8,128)(2,1)S(1)} %add_convert_fusion.1), channel_id=1, source_target_pairs={{0,2},{1,3},{2,0},{3,1},{4,6},{5,7},{6,4},{7,5},{8,10},{9,11},{10,... | collective-permute-start | bytes 589832 | tf_op jit(solution)/shard_map/ppermute | solution.py:23
  96.2 4.8 %collective-permute-start.36 = (bf16[128,128]{1,0:T(8,128)(2,1)S(1)}, bf16[128,128]{1,0:T(8,128)(2,1)S(1)}, u32[]{:S(2)}, u32[]{:S(2)}) collective-permute-start(bf16[128,128]{1,0:T(8,128)(2,1)S(1)} %get-tuple-element.88), channel_id=1, source_target_pairs={{0,12},{4,8},{8,4},{12,0},{16,28},{20,24},{24,20},{28,16},{1,13},{... | collective-permute-start | bytes 98312 | tf_op jit(solution)/shard_map/ppermute | solution.py:23
  103.3 7.0 %collective-permute-start.39 = (bf16[128,768]{1,0:T(8,128)(2,1)S(1)}, bf16[128,768]{1,0:T(8,128)(2,1)S(1)}, u32[]{:S(2)}, u32[]{:S(2)}) collective-permute-start(bf16[128,768]{1,0:T(8,128)(2,1)S(1)} %add_convert_fusion.3), channel_id=1, source_target_pairs={{0,2},{1,3},{2,0},{3,1},{4,6},{5,7},{6,4},{7,5},{8,10},{9,11},{10,... | collective-permute-start | bytes 589832 | tf_op jit(solution)/shard_map/ppermute | solution.py:23
  121.2 5.4 %collective-permute-start.49 = (f32[8,128]{1,0:T(8,128)S(1)}, f32[8,128]{1,0:T(8,128)S(1)}, u32[]{:S(2)}, u32[]{:S(2)}) collective-permute-start(f32[8,128]{1,0:T(8,128)S(1)} %add_add_fusion.1), channel_id=1, source_target_pairs={{0,24},{4,28},{8,16},{12,20},{16,8},{20,12},{24,0},{28,4},{1,25},{... | collective-permute-start | bytes 12296 | tf_op jit(solution)/shard_map/ppermute | solution.py:23
  (44 other events, 387.5 us)

commit v3 on v2

--- a/solution.py
+++ b/solution.py
@@ -8,11 +8,12 @@
 from jax.experimental.pallas import tpu as pltpu
 from jax.sharding import PartitionSpec as P
 
+
 TGRID = 8
 epsilon = 1e-06
 kinetic_weight = 0.1
 F32, BF16 = jnp.float32, jnp.bfloat16
-KERNEL_VMEM = 24 * 1024 * 1024
+KERNEL_VMEM = 16 * 1024 * 1024
 
 
 def image_index(positions, image_ends):
@@ -231,12 +232,12 @@
 VM = pl.BlockSpec(memory_space=pltpu.VMEM)
 
 
-def call(body, outs, flops, *operands):
+def call(body, outs, flops, *operands, specs=None):
     size = sum(math.prod(a.shape) * a.dtype.itemsize for a in operands)
     return pl.pallas_call(
         body,
         out_shape=outs,
-        in_specs=[VM] * len(operands),
+        in_specs=specs or [VM] * len(operands),
         out_specs=jax.tree.map(lambda _: VM, outs),
         compiler_params=pltpu.CompilerParams(vmem_limit_bytes=KERNEL_VMEM),
         cost_estimate=pl.CostEstimate(flops=flops, bytes_accessed=size, transcendentals=0),
@@ -253,25 +254,74 @@
     )
 
 
-def head_block_of(spread, twisted):
+def head_block_of(spread):
+    return lax.rem(lax.axis_index("seq"), spread)
+
+
+def fetch_kernel(count, *refs):
+    sources, targets, sems = refs[:count], refs[count : 2 * count], refs[2 * count]
+    copies = [
+        pltpu.make_async_copy(source, target, sems.at[i])
+        for i, (source, target) in enumerate(zip(sources, targets))
+    ]
+    for copy in copies:
+        copy.start()
+    for copy in copies:
+        copy.wait()
+
+
+def fetch(*arrays):
+    count = len(arrays)
+    size = sum(math.prod(a.shape) * a.dtype.itemsize for a in arrays)
+    return pl.pallas_call(
+        functools.partial(fetch_kernel, count),
+        out_shape=[whole(a.shape, a.dtype) for a in arrays],
+        in_specs=[pl.BlockSpec(memory_space=pltpu.HBM)] * count,
+        out_specs=[VM] * count,
+        scratch_shapes=[pltpu.SemaphoreType.DMA((count,))],
+        compiler_params=pltpu.CompilerParams(vmem_limit_bytes=KERNEL_VMEM),
+        cost_estimate=pl.CostEstimate(flops=200 * size, bytes_accessed=size, transcendentals=0),
+    )(*[pltpu.with_memory_space_constraint(a, pltpu.HBM) for a in arrays])
+
+
+def setup_kernel(partner, row_count, *refs):
+    length_ref, index_ref, near_rows, near_keys, far_keys, own_rows, time_ref = refs
     seq_index = lax.axis_index("seq")
-    block = lax.rem(seq_index, spread)
-    if twisted:
-        block = block ^ (lax.div(seq_index, spread) * 2)
-    return block
-
-
-def kv_kernel(plan, moving, *refs):
-    n_tp, _, spread, twisted, head_dim, step_size = plan
+    images = length_ref.shape[0]
+    ends = [length_ref[0]]
+    for i in range(1, images):
+        ends.append(ends[-1] + length_ref[i])
+
+    def image_of(shape, axis, source):
+        places = lax.broadcasted_iota(jnp.int32, shape, axis)
+        blocks = lax.div(places, row_count)
+        places = ((source ^ blocks) - blocks) * row_count + places
+        return sum((places >= end).astype(jnp.int32) for end in ends)
+
+    near_rows[...] = image_of(near_rows.shape, 0, seq_index)
+    near_keys[...] = image_of(near_keys.shape, 1, seq_index)
+    far_keys[...] = image_of(far_keys.shape, 1, seq_index ^ partner)
+    own = image_of(own_rows.shape, 0, seq_index)
+    own_rows[...] = own
+    time = jnp.zeros(own.shape, F32)
+    for i in range(images):
+        time = jnp.where(own == i, index_ref[i].astype(F32) / TGRID, time)
+    time_ref[...] = time
+
+
+def qkv_kernel(plan, moving, *refs):
+    n_tp, _, spread, head_dim, step_size = plan
     state, refs = refs[:n_tp], refs[n_tp:]
     if moving:
         near, far, refs = refs[:n_tp], refs[n_tp : 2 * n_tp], refs[2 * n_tp :]
-    time_ref, mod_ref, k_ref, v_ref, gain_ref, rows_ref, scale_ref = refs[:7]
-    outs = refs[7:]
+    time_ref, mod_ref, q_ref, k_ref, v_ref, q_gain, k_gain, rows_ref, scale_ref = refs[:9]
+    outs, pairs = refs[9 : 9 + spread], refs[9 + spread :]
     tp_index = lax.axis_index("tp")
-    block = head_block_of(spread, twisted)
+    block = head_block_of(spread)
     width = state[0].shape[1]
     times = time_ref[...]
+    if moving:
+        times = times + step_size
     squares = jnp.zeros_like(times)
     for k in range(n_tp):
         x = state[k][...].astype(F32)
@@ -283,41 +333,33 @@
         rows_ref[:, k * width : (k + 1) * width] = (x * (1.0 + times * mod)).astype(BF16)
     scale = lax.rsqrt(squares / (n_tp * width) + epsilon)
     scale_ref[...] = scale
-    for m in range(spread):
-        columns = head_at(block, m, head_dim)
-        total = None
-        for k in range(n_tp):
-            rows = head_at(tp_index, k, width)
-            weight = jnp.concatenate([k_ref[rows, columns], v_ref[rows, columns]], axis=1)
-            part = jnp.dot(
-                rows_ref[:, k * width : (k + 1) * width], weight, preferred_element_type=F32
-            )
-            total = part if total is None else total + part
-        total = total * scale
-        outs[m][:, :head_dim] = normed_head(total[:, :head_dim], gain_ref[...])
-        outs[m][:, head_dim:] = total[:, head_dim:].astype(BF16)
-
-
-def q_kernel(plan, rows_ref, scale_ref, q_ref, gain_ref, *outs):
-    n_tp, _, spread, twisted, head_dim, _ = plan
-    tp_index = lax.axis_index("tp")
-    block = head_block_of(spread, twisted)
-    width = rows_ref.shape[1] // n_tp
-    for first in range(0, spread, 2):
+
+    def project(pieces):
         total = None
         for k in range(n_tp):
             rows = head_at(tp_index, k, width)
             weight = jnp.concatenate(
-                [q_ref[rows, head_at(block, m, head_dim)] for m in (first, first + 1)], axis=1
+                [ref[rows, head_at(block, m, head_dim)] for ref, m in pieces], axis=1
             )
             part = jnp.dot(
                 rows_ref[:, k * width : (k + 1) * width], weight, preferred_element_type=F32
             )
             total = part if total is None else total + part
-        total = total * scale_ref[...]
+        return total * scale
+
+    for m in [*range(1, spread), 0]:
+        total = project([(k_ref, m), (v_ref, m)])
+        keys = normed_head(total[:, :head_dim], k_gain[...])
+        values = total[:, head_dim:].astype(BF16)
+        outs[m][:, head_dim : 2 * head_dim] = keys
+        outs[m][:, 2 * head_dim :] = values
+        pairs[m][:, :head_dim] = keys
+        pairs[m][:, head_dim:] = values
+    for first in range(0, spread, 2):
+        total = project([(q_ref, first), (q_ref, first + 1)])
         for m in range(2):
             cut = total[:, m * head_dim : (m + 1) * head_dim]
-            outs[first + m][...] = normed_head(cut, gain_ref[...])
+            outs[first + m][:, :head_dim] = normed_head(cut, q_gain[...])
 
 
 def terms_kernel(n_tp, left_ref, right_ref, scale_ref, *outs):
@@ -325,18 +367,23 @@
     width = outs[0].shape[1]
     for k in range(n_tp):
         product = jnp.dot(
-            left_ref[...],
+            left_ref[:, :width],
             right_ref[:, head_at(tp_index, k, width)],
             preferred_element_type=F32,
         )
         outs[k][...] = (product * scale_ref[...]).astype(BF16)
 
 
+def add_kernel(count, *refs):
+    for own, other, out in zip(refs[:count], refs[count : 2 * count], refs[2 * count :]):
+        out[...] = (own[...].astype(F32) + other[...].astype(F32)).astype(BF16)
+
+
 def out_kernel(plan, *refs):
-    n_tp, _, spread, twisted, head_dim, _ = plan
+    n_tp, _, spread, head_dim, _ = plan
     pieces, right_ref, outs = refs[:spread], refs[spread], refs[spread + 1 :]
     tp_index = lax.axis_index("tp")
-    block = head_block_of(spread, twisted)
+    block = head_block_of(spread)
     width = outs[0].shape[1]
     left = jnp.concatenate([piece[...] for piece in pieces], axis=1)
     for k in list(range(1, n_tp, 2)) + list(range(0, n_tp, 2)):
@@ -355,14 +402,16 @@
 
 
 def near_kernel(spread, head_dim, *refs):
-    queries, pairs, refs = refs[:spread], refs[spread : 2 * spread], refs[2 * spread :]
+    triples, refs = refs[:spread], refs[spread:]
     query_image, key_image, top_ref, total_ref, sum_ref = refs
-    rows = queries[0].shape[0]
-    keys = jnp.concatenate([pair[:, :head_dim] for pair in pairs], axis=0)
-    values = jnp.concatenate([pair[:, head_dim:] for pair in pairs], axis=0)
+    rows = triples[0].shape[0]
+    keys = jnp.concatenate([triple[:, head_dim : 2 * head_dim] for triple in triples], axis=0)
+    values = jnp.concatenate([triple[:, 2 * head_dim :] for triple in triples], axis=0)
     for m in range(spread):
         cut = slice(m * rows, (m + 1) * rows)
-        scores = scores_of(queries[m][...], keys, query_image[cut], key_image[...], head_dim)
+        scores = scores_of(
+            triples[m][:, :head_dim], keys, query_image[cut], key_image[...], head_dim
+        )
         top = jnp.max(scores, axis=1, keepdims=True)
         weights = jnp.exp(scores - top)
         top_ref[cut] = top
@@ -371,15 +420,17 @@
 
 
 def far_kernel(spread, head_dim, *refs):
-    queries, pairs, refs = refs[:spread], refs[spread : 2 * spread], refs[2 * spread :]
+    triples, pairs, refs = refs[:spread], refs[spread : 2 * spread], refs[2 * spread :]
     query_image, key_image, top_ref, total_ref, sum_ref = refs[:5]
     outs = refs[5:]
-    rows = queries[0].shape[0]
+    rows = triples[0].shape[0]
     keys = jnp.concatenate([pair[:, :head_dim] for pair in pairs], axis=0)
     values = jnp.concatenate([pair[:, head_dim:] for pair in pairs], axis=0)
-    for m in range(spread):
+    for m in [*range(1, spread), 0]:
         cut = slice(m * rows, (m + 1) * rows)
-        scores = scores_of(queries[m][...], keys, query_image[cut], key_image[...], head_dim)
+        scores = scores_of(
+            triples[m][:, :head_dim], keys, query_image[cut], key_image[...], head_dim
+        )
         old = top_ref[cut]
         top = jnp.maximum(old, jnp.max(scores, axis=1, keepdims=True))
         weights = jnp.exp(scores - top)
@@ -424,33 +475,12 @@
     row_count, width = latents.shape
     head_dim = q_gain.shape[0]
     heads_here = q_weight.shape[1] // head_dim
-    seq_index = lax.axis_index("seq")
     inner = n_tp * width
     step_size = 1.0 / TGRID
     spread = heads_here
-    twisted = spread >= 4
-    partner = spread ^ 2 if twisted else spread
-    plan = (n_tp, n_seq, spread, twisted, head_dim, step_size)
-
-    ends = [lengths[0]]
-    for i in range(1, lengths.shape[0]):
-        ends.append(ends[-1] + lengths[i])
-    row = jnp.arange(row_count, dtype=jnp.int32)
-    groups = jnp.arange(spread, dtype=jnp.int32)
-
-    def images_of(sources):
-        positions = (sources[:, None] * row_count + row[None, :]).reshape(-1)
-        return sum((positions >= end).astype(jnp.int32) for end in ends)
-
-    near_image = images_of(seq_index ^ groups)
-    far_image = images_of(seq_index ^ partner ^ groups)
-    own_image = images_of(seq_index[None])
-    start_time = sum(
-        jnp.where(own_image == i, t_index[i].astype(F32) / TGRID, 0.0)
-        for i in range(lengths.shape[0])
-    )[:, None]
-    near_rows, near_keys, far_keys = near_image[:, None], near_image[None, :], far_image[None, :]
-    own_rows = own_image[:, None]
+    plan = (n_tp, n_seq, spread, head_dim, step_size)
+
+    grouped = spread * row_count
     mod_row = mod_scale[None, :]
     q_row, k_row = q_gain[None, :], k_gain[None, :]
 
@@ -460,61 +490,61 @@
     def seq_swap(value, mask):
         return swap(value, "seq", n_seq, mask)
 
-    def mixed_terms(state, velocity, times):
+    def project(state, velocity, times):
         operands = list(state)
         if velocity is not None:
             operands += velocity[0] + velocity[1]
-        rows, scale, *pairs = call(
-            functools.partial(kv_kernel, plan, velocity is not None),
+        rows, scale, *blocks = call(
+            functools.partial(qkv_kernel, plan, velocity is not None),
             [whole((row_count, inner)), whole((row_count, 1), F32)]
+            + [whole((row_count, 3 * head_dim))] * spread
             + [whole((row_count, 2 * head_dim))] * spread,
-            4 * row_count * inner * spread * head_dim,
-            *operands, times, mod_row, k_weight, v_weight, k_row,
-        )
-        near, far = [pairs[0]], [seq_swap(pairs[0], partner)]
+            6 * row_count * inner * spread * head_dim,
+            *operands, times, mod_row, q_weight, k_weight, v_weight, q_row, k_row,
+        )
+        return rows, scale, blocks[:spread], blocks[spread:]
+
+    def attend(triples, pairs):
+        far_pairs, near_triples = [], [triples[0]]
+        for m in range(spread):
+            far_pairs.append(seq_swap(pairs[m], spread ^ m))
         for m in range(1, spread):
-            near.append(seq_swap(pairs[m], m))
-        for m in range(1, spread):
-            far.append(seq_swap(near[m], partner))
-        queries = call(
-            functools.partial(q_kernel, plan),
-            [whole((row_count, head_dim))] * spread,
-            2 * row_count * inner * spread * head_dim,
-            rows, scale, q_weight, q_row,
-        )
-        queries = [queries[0]] + [seq_swap(queries[m], m) for m in range(1, spread)]
-        flops = 4 * (spread * row_count) ** 2 * head_dim
-        state3 = call(
+            near_triples.append(seq_swap(triples[m], m))
+        flops = 4 * grouped**2 * head_dim
+        sums = call(
             functools.partial(near_kernel, spread, head_dim),
-            [whole((spread * row_count, 1), F32)] * 2
-            + [whole((spread * row_count, head_dim), F32)],
+            [whole((grouped, 1), F32)] * 2 + [whole((grouped, head_dim), F32)],
             flops,
-            *queries, *near, near_rows, near_keys,
+            *near_triples, near_rows, near_keys,
         )
         pieces = call(
             functools.partial(far_kernel, spread, head_dim),
             [whole((row_count, head_dim))] * spread,
             flops,
-            *queries, *far, near_rows, far_keys, *state3,
-        )
-        pieces = [pieces[0]] + [seq_swap(pieces[m], m) for m in range(1, spread)]
-        terms = call(
+            *near_triples, *far_pairs, near_rows, far_keys, *sums,
+        )
+        back = [pieces[0]]
+        for m in range(1, spread):
+            back.append(seq_swap(pieces[m], m))
+        return call(
             functools.partial(out_kernel, plan),
             [whole((row_count, width))] * n_tp,
             2 * row_count * spread * head_dim * inner,
-            *pieces, out_weight,
-        )
-        return terms, rows, scale
+            *back, out_weight,
+        )
 
     def halve(terms):
         held = dict(enumerate(terms))
         for bit in bits_of(n_tp)[:-1]:
             sent = {k: tp_swap(held[k], bit) for k in held if k & bit}
-            held = {
-                k: (held[k].astype(F32) + sent[k ^ bit].astype(F32)).astype(BF16)
-                for k in held
-                if not k & bit
-            }
+            kept = [k for k in held if not k & bit]
+            sums = call(
+                functools.partial(add_kernel, len(kept)),
+                [whole((row_count, width))] * len(kept),
+                1000 * row_count,
+                *[held[k] for k in kept], *[sent[k ^ bit] for k in kept],
+            )
+            held = dict(zip(kept, sums))
         return held
 
     def spread_low(held):
@@ -522,25 +552,51 @@
         for bit in reversed(bits_of(n_tp)[:-1]):
             for k in list(held):
                 held[k ^ bit] = tp_swap(held[k], bit)
-        return [held[k] for k in range(n_tp)]
+        return held
 
     top_bit = n_tp // 2
-    blocks = gather_blocks(latents, "tp", n_tp)
-    terms, rows, scale = mixed_terms(blocks, None, start_time)
-
+    top_block = tp_swap(latents, top_bit)
+    held = spread_low({0: latents}) | spread_low({top_bit: top_block})
+    blocks = [held[k] for k in range(n_tp)]
+    blocks[0], q_weight, k_weight, v_weight, mod_row, q_row, k_row = fetch(
+        latents, q_weight, k_weight, v_weight, mod_row, q_row, k_row
+    )
+    near_rows, near_keys, far_keys, own_rows, start_time = call(
+        functools.partial(setup_kernel, spread, row_count),
+        [
+            whole((grouped, 1), jnp.int32),
+            whole((1, grouped), jnp.int32),
+            whole((1, grouped), jnp.int32),
+            whole((row_count, 1), jnp.int32),
+            whole((row_count, 1), F32),
+        ],
+        1000 * row_count,
+        lengths,
+        t_index,
+        specs=[pl.BlockSpec(memory_space=pltpu.SMEM)] * 2,
+    )
+
+    rows, scale, triples, pairs = project(blocks, None, start_time)
+    terms = attend(triples, pairs)
     student_terms = call(
         functools.partial(terms_kernel, n_tp),
         [whole((row_count, width))] * n_tp,
         2 * row_count * width * inner,
-        rows[:, :width], student_weight, scale,
+        rows, student_weight, scale,
     )
     held_s = halve(student_terms)
-    student = (held_s[0].astype(F32) + tp_swap(held_s[top_bit], top_bit).astype(F32)).astype(BF16)
-
     held = halve(terms)
     other = {k ^ top_bit: tp_swap(held[k], top_bit) for k in sorted(held, reverse=True)}
-    near_blocks, far_blocks = spread_low(held), spread_low(other)
-    terms, _, _ = mixed_terms(blocks, (near_blocks, far_blocks), start_time + step_size)
+    velocity = tuple([low[k] for k in range(n_tp)] for low in map(spread_low, (held, other)))
+    _, _, triples, pairs = project(blocks, velocity, start_time)
+    other_s = tp_swap(held_s[top_bit], top_bit)
+    terms = attend(triples, pairs)
+    (student,) = call(
+        functools.partial(add_kernel, 1),
+        [whole((row_count, width))],
+        1000 * row_count,
+        held_s[0], other_s,
+    )
     held1 = halve(terms)
     other1 = tp_swap(held1[top_bit], top_bit)
     target, part = call(

time: 130 us -> 120 us (0.923)
  waiting for transfers between devices: 36.7 us -> 48 us
  local copies, waits for them, and re-layouts: 11.4 us -> 2.25 us
  starting transfers between devices: 55.5 us -> 48 us
  other arithmetic: 3.96 us -> 0.62 us
  between operations: 5.39 us -> 2.61 us
  Pallas kernels: 16.1 us -> 18.6 us
    ppermute x47 -> x41, waiting for transfers between devices: 33.9 us -> 44.9 us  [swap(): return lax.ppermute(value, axis, [(i, i ^ mask) for i in range(size)])]
    ppermute x47 -> x41, starting transfers between devices: 52 us -> 44.5 us  [swap(): return lax.ppermute(value, axis, [(i, i ^ mask) for i in range(size)])]
    unnamed x52 -> x14, local copies, waits for them, and re-layouts: 7.72 us -> 2.25 us
    slice x3 -> x0, local copies, waits for them, and re-layouts: 3.57 us -> none  [the longest x1 1.31 us: on_device_fused(): ends.append(ends[-1] + lengths[i])]
    add x5 -> x0, other arithmetic: 3.01 us -> none  [the longest x3 1.83 us: images_of(): return sum(((positions >= end).astype(jnp.int32) for end in ends))]
    pallas_call x12 -> x16, Pallas kernels: 16.1 us -> 18.6 us  [the longest x15 14.7 us: call(): pl.pallas_call(body, out_shape=outs, in_specs=specs or [VM] * len(operand...]
  transfers between devices with their start and end apart: 50 -> 44, of which waited for: 20 -> 24; matrix products, arithmetic and copies ran while one was open for 5% -> 0% of each run, Pallas kernels for 7% -> 8%
where the time goes in v3:
time: 120 us
  starting transfers between devices  48 us (40%)
  waiting for transfers between devices  48 us (40%)
  Pallas kernels  18.6 us (16%)
  between operations  2.61 us (2%)
  local copies, waits for them, and re-layouts  2.25 us (2%)
    ppermute x41, waiting for transfers between devices, swap(): return lax.ppermute(value, axis, [(i, i ^ mask) for i in range(size)])  44.9 us
    ppermute x41, starting transfers between devices, swap(): return lax.ppermute(value, axis, [(i, i ^ mask) for i in range(size)])  44.5 us
    pallas_call x15, Pallas kernels, call(): pl.pallas_call(body, out_shape=outs, in_specs=specs or [VM] * len(operand...  14.7 us
    pallas_call x1, Pallas kernels, fetch(): pl.pallas_call(functools.partial(fetch_kernel, count), out_shape=[whole(a...  3.93 us
    ppermute x3, starting transfers between devices, both(): lax.ppermute(value, ('seq', 'tp'), [(s * n_tp + t, (s ^ seq_mask) * n_tp...  3.49 us
    ppermute x3, waiting for transfers between devices, both(): lax.ppermute(value, ('seq', 'tp'), [(s * n_tp + t, (s ^ seq_mask) * n_tp...  3.12 us
  transfers between devices with their start and end apart: 44, of which 24 were waited for; matrix products, arithmetic and copies ran while one was open for 0% of the time, Pallas kernels for 8%

profile of v3, /device:TPU:0, one launch (start us, length us, event | category | flops | bytes accessed | tf_op | source)
XLA Modules:
  0.0 120.1 jit_solution(7883648896751648427)
XLA Ops:
  0.6 3.0 %collective-permute-start.1 = (bf16[128,768]{1,0:T(8,128)(2,1)}, bf16[128,768]{1,0:T(8,128)(2,1)S(1)}, u32[]{:S(2)}, u32[]{:S(2)}) collective-permute-start(bf16[128,768]{1,0:T(8,128)(2,1)} %refs_0_.2), channel_id=1, source_target_pairs={{0,2},{1,3},{2,0},{3,1},{4,6},{5,7},{6,4},{7,5},{8,10},{9,11},{10,... | collective-permute-start | bytes 589832 | tf_op jit(solution)/shard_map/ppermute | solution.py:24
  3.7 5.1 %collective-permute-done.1.refs_2_ = bf16[128,768]{1,0:T(8,128)(2,1)S(1)} collective-permute-done((bf16[128,768]{1,0:T(8,128)(2,1)}, bf16[128,768]{1,0:T(8,128)(2,1)S(1)}, u32[]{:S(2)}, u32[]{:S(2)}) %collective-permute-start.1) | collective-permute-done | bytes 196640 | tf_op jit(solution)/shard_map/ppermute | solution.py:24
  10.8 3.9 %shard_map.130 = (bf16[128,768]{1,0:T(8,128)(2,1)S(1)}, bf16[3072,512]{1,0:T(8,128)(2,1)S(1)}, bf16[3072,512]{1,0:T(8,128)(2,1)S(1)}, bf16[3072,512]{1,0:T(8,128...) custom-call(bf16[128,768]{1,0:T(8,128)(2,1)} %refs_0_.2, ...), custom_call_target="tpu_custom_call" | custom-call | flops 1929420800 | bytes 9647104 | tf_op jit(solution)/shard_map/pallas_call | solution.py:276
  14.7 1.9 %shard_map.132 = (bf16[128,3072]{1,0:T(8,128)(2,1)S(1)}, f32[128,1]{1,0:T(8,128)S(1)}, bf16[128,384]{1,0:T(8,128)(2,1)S(1)}, bf16[128,384]{1,0:T(8,128)(2,1)S(1)...) custom-call(bf16[128,768]{1,0:T(8,128)(2,1)S(1)} %get-tuple-element., ...), custom_call_target="tpu_custom_call" | custom-call | flops 1207959552 | bytes 10237440 | tf_op jit(solution)/shard_map/pallas_call | solution.py:237
  16.6 1.8 %collective-permute-start.3 = (bf16[128,384]{1,0:T(8,128)(2,1)S(1)}, bf16[128,384]{1,0:T(8,128)(2,1)S(1)}, u32[]{:S(2)}, u32[]{:S(2)}) collective-permute-start(bf16[128,384]{1,0:T(8,128)(2,1)S(1)} %get-tuple-element.76), channel_id=1, source_target_pairs={{0,4},{4,0},{8,12},{12,8},{16,20},{20,16},{24,28},{28,24},{1,5},{5... | collective-permute-start | bytes 294920 | tf_op jit(solution)/shard_map/ppermute | solution.py:24
  18.4 1.6 %collective-permute-start.4 = (bf16[128,384]{1,0:T(8,128)(2,1)S(1)}, bf16[128,384]{1,0:T(8,128)(2,1)S(1)}, u32[]{:S(2)}, u32[]{:S(2)}) collective-permute-start(bf16[128,384]{1,0:T(8,128)(2,1)S(1)} %get-tuple-element.77), channel_id=1, source_target_pairs={{0,8},{4,12},{8,0},{12,4},{16,24},{20,28},{24,16},{28,20},{1,9},{5... | collective-permute-start | bytes 294920 | tf_op jit(solution)/shard_map/ppermute | solution.py:24
  20.2 2.8 %collective-permute-start.6 = (bf16[128,256]{1,0:T(8,128)(2,1)S(1)}, bf16[128,256]{1,0:T(8,128)(2,1)S(1)}, u32[]{:S(2)}, u32[]{:S(2)}) collective-permute-start(bf16[128,256]{1,0:T(8,128)(2,1)S(1)} %get-tuple-element.79), channel_id=1, source_target_pairs={{0,16},{4,20},{8,24},{12,28},{16,0},{20,4},{24,8},{28,12},{1,17},{... | collective-permute-start | bytes 196616 | tf_op jit(solution)/shard_map/ppermute | solution.py:24
  24.3 3.6 %collective-permute-start.8 = (bf16[128,256]{1,0:T(8,128)(2,1)S(1)}, bf16[128,256]{1,0:T(8,128)(2,1)S(1)}, u32[]{:S(2)}, u32[]{:S(2)}) collective-permute-start(bf16[128,256]{1,0:T(8,128)(2,1)S(1)} %get-tuple-element.81), channel_id=1, source_target_pairs={{0,24},{4,28},{8,16},{12,20},{16,8},{20,12},{24,0},{28,4},{1,25},{... | collective-permute-start | bytes 196616 | tf_op jit(solution)/shard_map/ppermute | solution.py:24
  29.2 4.6 %collective-permute-done.7.refs_5_ = bf16[128,256]{1,0:T(8,128)(2,1)S(1)} collective-permute-done((bf16[128,256]{1,0:T(8,128)(2,1)S(1)}, bf16[128,256]{1,0:T(8,128)(2,1)S(1)}, u32[]{:S(2)}, u32[]{:S(2)}) %collective-permute-start.7) | collective-permute-done | bytes 65568 | tf_op jit(solution)/shard_map/ppermute | solution.py:24
  35.0 1.6 %shard_map.134 = (bf16[128,128]{1,0:T(8,128)(2,1)S(1)}, bf16[128,128]{1,0:T(8,128)(2,1)S(1)}, bf16[128,128]{1,0:T(8,128)(2,1)S(1)}, bf16[128,128]{1,0:T(8,128)(2,1)S(1)}) custom-call(bf16[128,384]{1,0:T(8,128)(2,1)S(1)} %get-tuple-element.75.refs_0_, bf16[128,384]{1,0:T(8,128)(2,1)S(1)} %collective-permute-done.3.refs_1_, ...), custom_call_target="tpu_custom_call" | custom-call | flops 134217728 | bytes 925696 | tf_op jit(solution)/shard_map/pallas_call | solution.py:237
  37.7 2.6 %collective-permute-start.11 = (bf16[128,128]{1,0:T(8,128)(2,1)S(1)}, bf16[128,128]{1,0:T(8,128)(2,1)S(1)}, u32[]{:S(2)}, u32[]{:S(2)}) collective-permute-start(bf16[128,128]{1,0:T(8,128)(2,1)S(1)} %get-tuple-element.91), channel_id=1, source_target_pairs={{0,8},{4,12},{8,0},{12,4},{16,24},{20,28},{24,16},{28,20},{1,9},{5... | collective-permute-start | bytes 98312 | tf_op jit(solution)/shard_map/ppermute | solution.py:24
  40.5 1.6 %collective-permute-done.11.refs_2_ = bf16[128,128]{1,0:T(8,128)(2,1)S(1)} collective-permute-done((bf16[128,128]{1,0:T(8,128)(2,1)S(1)}, bf16[128,128]{1,0:T(8,128)(2,1)S(1)}, u32[]{:S(2)}, u32[]{:S(2)}) %collective-permute-start.11) | collective-permute-done | bytes 32800 | tf_op jit(solution)/shard_map/ppermute | solution.py:24
  42.2 2.9 %collective-permute-done.12.refs_3_ = bf16[128,128]{1,0:T(8,128)(2,1)S(1)} collective-permute-done((bf16[128,128]{1,0:T(8,128)(2,1)S(1)}, bf16[128,128]{1,0:T(8,128)(2,1)S(1)}, u32[]{:S(2)}, u32[]{:S(2)}) %collective-permute-start.12) | collective-permute-done | bytes 32800 | tf_op jit(solution)/shard_map/ppermute | solution.py:24
  47.7 1.5 %collective-permute-start.15 = (bf16[128,768]{1,0:T(8,128)(2,1)S(1)}, bf16[128,768]{1,0:T(8,128)(2,1)S(1)}, u32[]{:S(2)}, u32[]{:S(2)}) collective-permute-start(bf16[128,768]{1,0:T(8,128)(2,1)S(1)} %get-tuple-element.98.refs_6_), channel_id=1, source_target_pairs={{0,2},{1,3},{2,0},{3,1},{4,6},{5,7},{6,4},{7,5},{8,10},{9,11},{10,... | collective-permute-start | bytes 589832 | tf_op jit(solution)/shard_map/ppermute | solution.py:24
  50.3 5.2 %collective-permute-done.15.refs_8_.refs_1_ = bf16[128,768]{1,0:T(8,128)(2,1)S(1)} collective-permute-done((bf16[128,768]{1,0:T(8,128)(2,1)S(1)}, bf16[128,768]{1,0:T(8,128)(2,1)S(1)}, u32[]{:S(2)}, u32[]{:S(2)}) %collective-permute-start.15) | collective-permute-done | bytes 196640 | tf_op jit(solution)/shard_map/ppermute | solution.py:24
  55.5 3.5 %collective-permute-done.19.refs_10_ = bf16[128,768]{1,0:T(8,128)(2,1)S(1)} collective-permute-done((bf16[128,768]{1,0:T(8,128)(2,1)S(1)}, bf16[128,768]{1,0:T(8,128)(2,1)S(1)}, u32[]{:S(2)}, u32[]{:S(2)}) %collective-permute-start.19) | collective-permute-done | bytes 196640 | tf_op jit(solution)/shard_map/ppermute | solution.py:24
  59.0 1.4 %collective-permute-done.20.refs_11_ = bf16[128,768]{1,0:T(8,128)(2,1)S(1)} collective-permute-done((bf16[128,768]{1,0:T(8,128)(2,1)S(1)}, bf16[128,768]{1,0:T(8,128)(2,1)S(1)}, u32[]{:S(2)}, u32[]{:S(2)}) %collective-permute-start.20) | collective-permute-done | bytes 196640 | tf_op jit(solution)/shard_map/ppermute | solution.py:24
  60.4 2.6 %shard_map.137 = (bf16[128,3072]{1,0:T(8,128)(2,1)}, f32[128,1]{1,0:T(8,128)}, bf16[128,384]{1,0:T(8,128)(2,1)S(1)}, bf16[128,384]{1,0:T(8,128)(2,1)S(1)}, bf16[...) custom-call(bf16[128,768]{1,0:T(8,128)(2,1)S(1)} %get-tuple-element., ...), custom_call_target="tpu_custom_call" | custom-call | flops 1207959552 | bytes 11810304 | tf_op jit(solution)/shard_map/pallas_call | solution.py:237
  64.0 2.6 %collective-permute-start.23 = (bf16[128,384]{1,0:T(8,128)(2,1)S(1)}, bf16[128,384]{1,0:T(8,128)(2,1)S(1)}, u32[]{:S(2)}, u32[]{:S(2)}) collective-permute-start(bf16[128,384]{1,0:T(8,128)(2,1)S(1)} %get-tuple-element.102), channel_id=1, source_target_pairs={{0,12},{4,8},{8,4},{12,0},{16,28},{20,24},{24,20},{28,16},{1,13},{... | collective-permute-start | bytes 294920 | tf_op jit(solution)/shard_map/ppermute | solution.py:24
  67.2 2.1 %collective-permute-start.25 = (bf16[128,256]{1,0:T(8,128)(2,1)S(1)}, bf16[128,256]{1,0:T(8,128)(2,1)S(1)}, u32[]{:S(2)}, u32[]{:S(2)}) collective-permute-start(bf16[128,256]{1,0:T(8,128)(2,1)S(1)} %get-tuple-element.104), channel_id=1, source_target_pairs={{0,20},{4,16},{8,28},{12,24},{16,4},{20,0},{24,12},{28,8},{1,21},{... | collective-permute-start | bytes 196616 | tf_op jit(solution)/shard_map/ppermute | solution.py:24
  69.4 2.8 %collective-permute-start.26 = (bf16[128,256]{1,0:T(8,128)(2,1)S(1)}, bf16[128,256]{1,0:T(8,128)(2,1)S(1)}, u32[]{:S(2)}, u32[]{:S(2)}) collective-permute-start(bf16[128,256]{1,0:T(8,128)(2,1)S(1)} %get-tuple-element.105), channel_id=1, source_target_pairs={{0,24},{4,28},{8,16},{12,20},{16,8},{20,12},{24,0},{28,4},{1,25},{... | collective-permute-start | bytes 196616 | tf_op jit(solution)/shard_map/ppermute | solution.py:24
  72.2 2.0 %collective-permute-start.27 = (bf16[128,256]{1,0:T(8,128)(2,1)S(1)}, bf16[128,256]{1,0:T(8,128)(2,1)S(1)}, u32[]{:S(2)}, u32[]{:S(2)}) collective-permute-start(bf16[128,256]{1,0:T(8,128)(2,1)S(1)} %get-tuple-element.106), channel_id=1, source_target_pairs={{0,28},{4,24},{8,20},{12,16},{16,12},{20,8},{24,4},{28,0},{1,29},{... | collective-permute-start | bytes 196616 | tf_op jit(solution)/shard_map/ppermute | solution.py:24
  75.4 1.5 %collective-permute-done.24.refs_4_ = bf16[128,256]{1,0:T(8,128)(2,1)S(1)} collective-permute-done((bf16[128,256]{1,0:T(8,128)(2,1)S(1)}, bf16[128,256]{1,0:T(8,128)(2,1)S(1)}, u32[]{:S(2)}, u32[]{:S(2)}) %collective-permute-start.24) | collective-permute-done | bytes 65568 | tf_op jit(solution)/shard_map/ppermute | solution.py:24
  79.2 1.6 %shard_map.139 = (bf16[128,128]{1,0:T(8,128)(2,1)S(1)}, bf16[128,128]{1,0:T(8,128)(2,1)S(1)}, bf16[128,128]{1,0:T(8,128)(2,1)S(1)}, bf16[128,128]{1,0:T(8,128)(2,1)S(1)}) custom-call(bf16[128,384]{1,0:T(8,128)(2,1)S(1)} %get-tuple-element.99.refs_0_, bf16[128,384]{1,0:T(8,128)(2,1)S(1)} %collective-permute-done.21.refs_1_, ...), custom_call_target="tpu_custom_call" | custom-call | flops 134217728 | bytes 925696 | tf_op jit(solution)/shard_map/pallas_call | solution.py:237
  82.1 2.5 %collective-permute-start.29 = (bf16[128,128]{1,0:T(8,128)(2,1)S(1)}, bf16[128,128]{1,0:T(8,128)(2,1)S(1)}, u32[]{:S(2)}, u32[]{:S(2)}) collective-permute-start(bf16[128,128]{1,0:T(8,128)(2,1)S(1)} %get-tuple-element.112), channel_id=1, source_target_pairs={{0,8},{4,12},{8,0},{12,4},{16,24},{20,28},{24,16},{28,20},{1,9},{5... | collective-permute-start | bytes 98312 | tf_op jit(solution)/shard_map/ppermute | solution.py:24
  86.5 2.9 %collective-permute-done.30.refs_3_ = bf16[128,128]{1,0:T(8,128)(2,1)S(1)} collective-permute-done((bf16[128,128]{1,0:T(8,128)(2,1)S(1)}, bf16[128,128]{1,0:T(8,128)(2,1)S(1)}, u32[]{:S(2)}, u32[]{:S(2)}) %collective-permute-start.30) | collective-permute-done | bytes 32800 | tf_op jit(solution)/shard_map/ppermute | solution.py:24
  90.7 1.6 %collective-permute-start.36 = (bf16[128,768]{1,0:T(8,128)(2,1)S(1)}, bf16[128,768]{1,0:T(8,128)(2,1)S(1)}, u32[]{:S(2)}, u32[]{:S(2)}) collective-permute-start(bf16[128,768]{1,0:T(8,128)(2,1)S(1)} %get-tuple-element.127), channel_id=1, source_target_pairs={{0,2},{1,3},{2,0},{3,1},{4,6},{5,7},{6,4},{7,5},{8,10},{9,11},{10,... | collective-permute-start | bytes 589832 | tf_op jit(solution)/shard_map/ppermute | solution.py:24
  93.5 5.0 %collective-permute-done.36.refs_1_ = bf16[128,768]{1,0:T(8,128)(2,1)S(1)} collective-permute-done((bf16[128,768]{1,0:T(8,128)(2,1)S(1)}, bf16[128,768]{1,0:T(8,128)(2,1)S(1)}, u32[]{:S(2)}, u32[]{:S(2)}) %collective-permute-start.36) | collective-permute-done | bytes 196640 | tf_op jit(solution)/shard_map/ppermute | solution.py:24
  99.3 2.6 %collective-permute-done.33.refs_3_ = bf16[128,768]{1,0:T(8,128)(2,1)S(1)} collective-permute-done((bf16[128,768]{1,0:T(8,128)(2,1)S(1)}, bf16[128,768]{1,0:T(8,128)(2,1)S(1)}, u32[]{:S(2)}, u32[]{:S(2)}) %collective-permute-start.33) | collective-permute-done | bytes 196640 | tf_op jit(solution)/shard_map/ppermute | solution.py:24
  104.9 1.6 %collective-permute-start.40 = (f32[8,128]{1,0:T(8,128)S(1)}, f32[8,128]{1,0:T(8,128)S(1)}, u32[]{:S(2)}, u32[]{:S(2)}) collective-permute-start(f32[8,128]{1,0:T(8,128)S(1)} %add.21), channel_id=1, source_target_pairs={{0,6},{1,7},{2,4},{3,5},{4,2},{5,3},{6,0},{7,1},{8,14},{9,15},{10,... | collective-permute-start | bytes 12296 | tf_op jit(solution)/shard_map/ppermute | solution.py:613
  111.5 1.7 %collective-permute-start.43 = (f32[8,128]{1,0:T(8,128)S(1)}, f32[8,128]{1,0:T(8,128)S(1)}, u32[]{:S(2)}, u32[]{:S(2)}) collective-permute-start(f32[8,128]{1,0:T(8,128)S(1)} %add_add_fusion.1), channel_id=1, source_target_pairs={{0,24},{4,28},{8,16},{12,20},{16,8},{20,12},{24,0},{28,4},{1,25},{... | collective-permute-start | bytes 12296 | tf_op jit(solution)/shard_map/ppermute | solution.py:24
  113.2 2.7 %collective-permute-start.41 = (f32[8,128]{1,0:T(8,128)S(1)}, f32[8,128]{1,0:T(8,128)S(1)}, u32[]{:S(2)}, u32[]{:S(2)}) collective-permute-start(f32[8,128]{1,0:T(8,128)S(1)} %add_add_fusion.1), channel_id=1, source_target_pairs={{0,8},{4,12},{8,0},{12,4},{16,24},{20,28},{24,16},{28,20},{1,9},{5... | collective-permute-start | bytes 12296 | tf_op jit(solution)/shard_map/ppermute | solution.py:24
  (91 shorter events, 32.8 us)
Async XLA Ops:
  0.6 8.1 %collective-permute-start.1 = (bf16[128,768]{1,0:T(8,128)(2,1)}, bf16[128,768]{1,0:T(8,128)(2,1)S(1)}, u32[]{:S(2)}, u32[]{:S(2)}) collective-permute-start(bf16[128,768]{1,0:T(8,128)(2,1)} %refs_0_.2), channel_id=1, source_target_pairs={{0,2},{1,3},{2,0},{3,1},{4,6},{5,7},{6,4},{7,5},{8,10},{9,11},{10,... | collective-permute-start | bytes 589832 | tf_op jit(solution)/shard_map/ppermute | solution.py:24
  3.7 11.0 %collective-permute-start = (bf16[128,768]{1,0:T(8,128)(2,1)}, bf16[128,768]{1,0:T(8,128)(2,1)S(1)}, u32[]{:S(2)}, u32[]{:S(2)}) collective-permute-start(bf16[128,768]{1,0:T(8,128)(2,1)} %refs_0_.2), channel_id=1, source_target_pairs={{0,1},{1,0},{2,3},{3,2},{4,5},{5,4},{6,7},{7,6},{8,9},{9,8},{10,11... | collective-permute-start | bytes 589832 | tf_op jit(solution)/shard_map/ppermute | solution.py:24
  8.8 5.9 %collective-permute-start.2 = (bf16[128,768]{1,0:T(8,128)(2,1)S(1)}, bf16[128,768]{1,0:T(8,128)(2,1)S(1)}, u32[]{:S(2)}, u32[]{:S(2)}) collective-permute-start(bf16[128,768]{1,0:T(8,128)(2,1)S(1)} %collective-permute-done.1.refs_2_), channel_id=1, source_target_pairs={{0,1},{1,0},{2,3},{3,2},{4,5},{5,4},{6,7},{7,6},{8,9},{9,8},{10,11... | collective-permute-start | bytes 589832 | tf_op jit(solution)/shard_map/ppermute | solution.py:24
  16.6 7.7 %collective-permute-start.3 = (bf16[128,384]{1,0:T(8,128)(2,1)S(1)}, bf16[128,384]{1,0:T(8,128)(2,1)S(1)}, u32[]{:S(2)}, u32[]{:S(2)}) collective-permute-start(bf16[128,384]{1,0:T(8,128)(2,1)S(1)} %get-tuple-element.76), channel_id=1, source_target_pairs={{0,4},{4,0},{8,12},{12,8},{16,20},{20,16},{24,28},{28,24},{1,5},{5... | collective-permute-start | bytes 294920 | tf_op jit(solution)/shard_map/ppermute | solution.py:24
  18.4 9.5 %collective-permute-start.4 = (bf16[128,384]{1,0:T(8,128)(2,1)S(1)}, bf16[128,384]{1,0:T(8,128)(2,1)S(1)}, u32[]{:S(2)}, u32[]{:S(2)}) collective-permute-start(bf16[128,384]{1,0:T(8,128)(2,1)S(1)} %get-tuple-element.77), channel_id=1, source_target_pairs={{0,8},{4,12},{8,0},{12,4},{16,24},{20,28},{24,16},{28,20},{1,9},{5... | collective-permute-start | bytes 294920 | tf_op jit(solution)/shard_map/ppermute | solution.py:24
  20.0 7.9 %collective-permute-start.5 = (bf16[128,384]{1,0:T(8,128)(2,1)S(1)}, bf16[128,384]{1,0:T(8,128)(2,1)S(1)}, u32[]{:S(2)}, u32[]{:S(2)}) collective-permute-start(bf16[128,384]{1,0:T(8,128)(2,1)S(1)} %get-tuple-element.78), channel_id=1, source_target_pairs={{0,12},{4,8},{8,4},{12,0},{16,28},{20,24},{24,20},{28,16},{1,13},{... | collective-permute-start | bytes 294920 | tf_op jit(solution)/shard_map/ppermute | solution.py:24
  20.2 9.0 %collective-permute-start.6 = (bf16[128,256]{1,0:T(8,128)(2,1)S(1)}, bf16[128,256]{1,0:T(8,128)(2,1)S(1)}, u32[]{:S(2)}, u32[]{:S(2)}) collective-permute-start(bf16[128,256]{1,0:T(8,128)(2,1)S(1)} %get-tuple-element.79), channel_id=1, source_target_pairs={{0,16},{4,20},{8,24},{12,28},{16,0},{20,4},{24,8},{28,12},{1,17},{... | collective-permute-start | bytes 196616 | tf_op jit(solution)/shard_map/ppermute | solution.py:24
  23.0 10.8 %collective-permute-start.7 = (bf16[128,256]{1,0:T(8,128)(2,1)S(1)}, bf16[128,256]{1,0:T(8,128)(2,1)S(1)}, u32[]{:S(2)}, u32[]{:S(2)}) collective-permute-start(bf16[128,256]{1,0:T(8,128)(2,1)S(1)} %get-tuple-element.80), channel_id=1, source_target_pairs={{0,20},{4,16},{8,28},{12,24},{16,4},{20,0},{24,12},{28,8},{1,21},{... | collective-permute-start | bytes 196616 | tf_op jit(solution)/shard_map/ppermute | solution.py:24
  24.3 9.5 %collective-permute-start.8 = (bf16[128,256]{1,0:T(8,128)(2,1)S(1)}, bf16[128,256]{1,0:T(8,128)(2,1)S(1)}, u32[]{:S(2)}, u32[]{:S(2)}) collective-permute-start(bf16[128,256]{1,0:T(8,128)(2,1)S(1)} %get-tuple-element.81), channel_id=1, source_target_pairs={{0,24},{4,28},{8,16},{12,20},{16,8},{20,12},{24,0},{28,4},{1,25},{... | collective-permute-start | bytes 196616 | tf_op jit(solution)/shard_map/ppermute | solution.py:24
  27.9 7.1 %collective-permute-start.9 = (bf16[128,256]{1,0:T(8,128)(2,1)S(1)}, bf16[128,256]{1,0:T(8,128)(2,1)S(1)}, u32[]{:S(2)}, u32[]{:S(2)}) collective-permute-start(bf16[128,256]{1,0:T(8,128)(2,1)S(1)} %get-tuple-element.82), channel_id=1, source_target_pairs={{0,28},{4,24},{8,20},{12,16},{16,12},{20,8},{24,4},{28,0},{1,29},{... | collective-permute-start | bytes 196616 | tf_op jit(solution)/shard_map/ppermute | solution.py:24
  40.3 4.8 %collective-permute-start.12 = (bf16[128,128]{1,0:T(8,128)(2,1)S(1)}, bf16[128,128]{1,0:T(8,128)(2,1)S(1)}, u32[]{:S(2)}, u32[]{:S(2)}) collective-permute-start(bf16[128,128]{1,0:T(8,128)(2,1)S(1)} %get-tuple-element.92), channel_id=1, source_target_pairs={{0,12},{4,8},{8,4},{12,0},{16,28},{20,24},{24,20},{28,16},{1,13},{... | collective-permute-start | bytes 98312 | tf_op jit(solution)/shard_map/ppermute | solution.py:24
  47.7 7.8 %collective-permute-start.15 = (bf16[128,768]{1,0:T(8,128)(2,1)S(1)}, bf16[128,768]{1,0:T(8,128)(2,1)S(1)}, u32[]{:S(2)}, u32[]{:S(2)}) collective-permute-start(bf16[128,768]{1,0:T(8,128)(2,1)S(1)} %get-tuple-element.98.refs_6_), channel_id=1, source_target_pairs={{0,2},{1,3},{2,0},{3,1},{4,6},{5,7},{6,4},{7,5},{8,10},{9,11},{10,... | collective-permute-start | bytes 589832 | tf_op jit(solution)/shard_map/ppermute | solution.py:24
  49.2 9.8 %collective-permute-start.19 = (bf16[128,768]{1,0:T(8,128)(2,1)S(1)}, bf16[128,768]{1,0:T(8,128)(2,1)S(1)}, u32[]{:S(2)}, u32[]{:S(2)}) collective-permute-start(bf16[128,768]{1,0:T(8,128)(2,1)S(1)} %get-tuple-element.97.refs_4_.refs_0_), channel_id=1, source_target_pairs={{0,2},{1,3},{2,0},{3,1},{4,6},{5,7},{6,4},{7,5},{8,10},{9,11},{10,... | collective-permute-start | bytes 589832 | tf_op jit(solution)/shard_map/ppermute | solution.py:24
  49.8 9.2 %collective-permute-start.17 = (bf16[128,768]{1,0:T(8,128)(2,1)S(1)}, bf16[128,768]{1,0:T(8,128)(2,1)S(1)}, u32[]{:S(2)}, u32[]{:S(2)}) collective-permute-start(bf16[128,768]{1,0:T(8,128)(2,1)S(1)} %get-tuple-element.98.refs_6_), channel_id=1, source_target_pairs={{0,1},{1,0},{2,3},{3,2},{4,5},{5,4},{6,7},{7,6},{8,9},{9,8},{10,11... | collective-permute-start | bytes 589832 | tf_op jit(solution)/shard_map/ppermute | solution.py:24
  49.8 9.2 %collective-permute-start.16 = (bf16[128,768]{1,0:T(8,128)(2,1)S(1)}, bf16[128,768]{1,0:T(8,128)(2,1)S(1)}, u32[]{:S(2)}, u32[]{:S(2)}) collective-permute-start(bf16[128,768]{1,0:T(8,128)(2,1)S(1)} %get-tuple-element.97.refs_4_.refs_0_), channel_id=1, source_target_pairs={{0,1},{1,0},{2,3},{3,2},{4,5},{5,4},{6,7},{7,6},{8,9},{9,8},{10,11... | collective-permute-start | bytes 589832 | tf_op jit(solution)/shard_map/ppermute | solution.py:24
  63.0 6.3 %collective-permute-start.21 = (bf16[128,384]{1,0:T(8,128)(2,1)S(1)}, bf16[128,384]{1,0:T(8,128)(2,1)S(1)}, u32[]{:S(2)}, u32[]{:S(2)}) collective-permute-start(bf16[128,384]{1,0:T(8,128)(2,1)S(1)} %get-tuple-element.100), channel_id=1, source_target_pairs={{0,4},{4,0},{8,12},{12,8},{16,20},{20,16},{24,28},{28,24},{1,5},{5... | collective-permute-start | bytes 294920 | tf_op jit(solution)/shard_map/ppermute | solution.py:24
  63.5 8.7 %collective-permute-start.22 = (bf16[128,384]{1,0:T(8,128)(2,1)S(1)}, bf16[128,384]{1,0:T(8,128)(2,1)S(1)}, u32[]{:S(2)}, u32[]{:S(2)}) collective-permute-start(bf16[128,384]{1,0:T(8,128)(2,1)S(1)} %get-tuple-element.101), channel_id=1, source_target_pairs={{0,8},{4,12},{8,0},{12,4},{16,24},{20,28},{24,16},{28,20},{1,9},{5... | collective-permute-start | bytes 294920 | tf_op jit(solution)/shard_map/ppermute | solution.py:24
  64.0 10.2 %collective-permute-start.23 = (bf16[128,384]{1,0:T(8,128)(2,1)S(1)}, bf16[128,384]{1,0:T(8,128)(2,1)S(1)}, u32[]{:S(2)}, u32[]{:S(2)}) collective-permute-start(bf16[128,384]{1,0:T(8,128)(2,1)S(1)} %get-tuple-element.102), channel_id=1, source_target_pairs={{0,12},{4,8},{8,4},{12,0},{16,28},{20,24},{24,20},{28,16},{1,13},{... | collective-permute-start | bytes 294920 | tf_op jit(solution)/shard_map/ppermute | solution.py:24
  66.5 10.4 %collective-permute-start.24 = (bf16[128,256]{1,0:T(8,128)(2,1)S(1)}, bf16[128,256]{1,0:T(8,128)(2,1)S(1)}, u32[]{:S(2)}, u32[]{:S(2)}) collective-permute-start(bf16[128,256]{1,0:T(8,128)(2,1)S(1)} %get-tuple-element.103), channel_id=1, source_target_pairs={{0,16},{4,20},{8,24},{12,28},{16,0},{20,4},{24,8},{28,12},{1,17},{... | collective-permute-start | bytes 196616 | tf_op jit(solution)/shard_map/ppermute | solution.py:24
  67.2 11.0 %collective-permute-start.25 = (bf16[128,256]{1,0:T(8,128)(2,1)S(1)}, bf16[128,256]{1,0:T(8,128)(2,1)S(1)}, u32[]{:S(2)}, u32[]{:S(2)}) collective-permute-start(bf16[128,256]{1,0:T(8,128)(2,1)S(1)} %get-tuple-element.104), channel_id=1, source_target_pairs={{0,20},{4,16},{8,28},{12,24},{16,4},{20,0},{24,12},{28,8},{1,21},{... | collective-permute-start | bytes 196616 | tf_op jit(solution)/shard_map/ppermute | solution.py:24
  69.4 8.9 %collective-permute-start.26 = (bf16[128,256]{1,0:T(8,128)(2,1)S(1)}, bf16[128,256]{1,0:T(8,128)(2,1)S(1)}, u32[]{:S(2)}, u32[]{:S(2)}) collective-permute-start(bf16[128,256]{1,0:T(8,128)(2,1)S(1)} %get-tuple-element.105), channel_id=1, source_target_pairs={{0,24},{4,28},{8,16},{12,20},{16,8},{20,12},{24,0},{28,4},{1,25},{... | collective-permute-start | bytes 196616 | tf_op jit(solution)/shard_map/ppermute | solution.py:24
  72.2 7.1 %collective-permute-start.27 = (bf16[128,256]{1,0:T(8,128)(2,1)S(1)}, bf16[128,256]{1,0:T(8,128)(2,1)S(1)}, u32[]{:S(2)}, u32[]{:S(2)}) collective-permute-start(bf16[128,256]{1,0:T(8,128)(2,1)S(1)} %get-tuple-element.106), channel_id=1, source_target_pairs={{0,28},{4,24},{8,20},{12,16},{16,12},{20,8},{24,4},{28,0},{1,29},{... | collective-permute-start | bytes 196616 | tf_op jit(solution)/shard_map/ppermute | solution.py:24
  80.8 5.3 %collective-permute-start.28 = (bf16[128,128]{1,0:T(8,128)(2,1)S(1)}, bf16[128,128]{1,0:T(8,128)(2,1)S(1)}, u32[]{:S(2)}, u32[]{:S(2)}) collective-permute-start(bf16[128,128]{1,0:T(8,128)(2,1)S(1)} %get-tuple-element.111), channel_id=1, source_target_pairs={{0,4},{4,0},{8,12},{12,8},{16,20},{20,16},{24,28},{28,24},{1,5},{5... | collective-permute-start | bytes 98312 | tf_op jit(solution)/shard_map/ppermute | solution.py:24
  84.6 4.8 %collective-permute-start.30 = (bf16[128,128]{1,0:T(8,128)(2,1)S(1)}, bf16[128,128]{1,0:T(8,128)(2,1)S(1)}, u32[]{:S(2)}, u32[]{:S(2)}) collective-permute-start(bf16[128,128]{1,0:T(8,128)(2,1)S(1)} %get-tuple-element.113), channel_id=1, source_target_pairs={{0,12},{4,8},{8,4},{12,0},{16,28},{20,24},{24,20},{28,16},{1,13},{... | collective-permute-start | bytes 98312 | tf_op jit(solution)/shard_map/ppermute | solution.py:24
  85.5 5.1 %collective-permute-start.34 = (bf16[128,768]{1,0:T(8,128)(2,1)S(1)}, bf16[128,768]{1,0:T(8,128)(2,1)S(1)}, u32[]{:S(2)}, u32[]{:S(2)}) collective-permute-start(bf16[128,768]{1,0:T(8,128)(2,1)S(1)} %get-tuple-element.124), channel_id=1, source_target_pairs={{0,1},{1,0},{2,3},{3,2},{4,5},{5,4},{6,7},{7,6},{8,9},{9,8},{10,11... | collective-permute-start | bytes 589832 | tf_op jit(solution)/shard_map/ppermute | solution.py:24
  85.6 5.1 %collective-permute-start.35 = (bf16[128,768]{1,0:T(8,128)(2,1)S(1)}, bf16[128,768]{1,0:T(8,128)(2,1)S(1)}, u32[]{:S(2)}, u32[]{:S(2)}) collective-permute-start(bf16[128,768]{1,0:T(8,128)(2,1)S(1)} %get-tuple-element.125), channel_id=1, source_target_pairs={{0,1},{1,0},{2,3},{3,2},{4,5},{5,4},{6,7},{7,6},{8,9},{9,8},{10,11... | collective-permute-start | bytes 589832 | tf_op jit(solution)/shard_map/ppermute | solution.py:24
  90.7 7.8 %collective-permute-start.36 = (bf16[128,768]{1,0:T(8,128)(2,1)S(1)}, bf16[128,768]{1,0:T(8,128)(2,1)S(1)}, u32[]{:S(2)}, u32[]{:S(2)}) collective-permute-start(bf16[128,768]{1,0:T(8,128)(2,1)S(1)} %get-tuple-element.127), channel_id=1, source_target_pairs={{0,2},{1,3},{2,0},{3,1},{4,6},{5,7},{6,4},{7,5},{8,10},{9,11},{10,... | collective-permute-start | bytes 589832 | tf_op jit(solution)/shard_map/ppermute | solution.py:24
  92.4 9.5 %collective-permute-start.33 = (bf16[128,768]{1,0:T(8,128)(2,1)S(1)}, bf16[128,768]{1,0:T(8,128)(2,1)S(1)}, u32[]{:S(2)}, u32[]{:S(2)}) collective-permute-start(bf16[128,768]{1,0:T(8,128)(2,1)S(1)} %get-tuple-element.119), channel_id=1, source_target_pairs={{0,2},{1,3},{2,0},{3,1},{4,6},{5,7},{6,4},{7,5},{8,10},{9,11},{10,... | collective-permute-start | bytes 589832 | tf_op jit(solution)/shard_map/ppermute | solution.py:24
  104.9 4.5 %collective-permute-start.40 = (f32[8,128]{1,0:T(8,128)S(1)}, f32[8,128]{1,0:T(8,128)S(1)}, u32[]{:S(2)}, u32[]{:S(2)}) collective-permute-start(f32[8,128]{1,0:T(8,128)S(1)} %add.21), channel_id=1, source_target_pairs={{0,6},{1,7},{2,4},{3,5},{4,2},{5,3},{6,0},{7,1},{8,14},{9,15},{10,... | collective-permute-start | bytes 12296 | tf_op jit(solution)/shard_map/ppermute | solution.py:613
  111.5 5.4 %collective-permute-start.43 = (f32[8,128]{1,0:T(8,128)S(1)}, f32[8,128]{1,0:T(8,128)S(1)}, u32[]{:S(2)}, u32[]{:S(2)}) collective-permute-start(f32[8,128]{1,0:T(8,128)S(1)} %add_add_fusion.1), channel_id=1, source_target_pairs={{0,24},{4,28},{8,16},{12,20},{16,8},{20,12},{24,0},{28,4},{1,25},{... | collective-permute-start | bytes 12296 | tf_op jit(solution)/shard_map/ppermute | solution.py:24
  113.2 4.5 %collective-permute-start.42 = (f32[8,128]{1,0:T(8,128)S(1)}, f32[8,128]{1,0:T(8,128)S(1)}, u32[]{:S(2)}, u32[]{:S(2)}) collective-permute-start(f32[8,128]{1,0:T(8,128)S(1)} %add_add_fusion.1), channel_id=1, source_target_pairs={{0,16},{4,20},{8,24},{12,28},{16,0},{20,4},{24,8},{28,12},{1,17},{... | collective-permute-start | bytes 12296 | tf_op jit(solution)/shard_map/ppermute | solution.py:24
  113.2 4.5 %collective-permute-start.41 = (f32[8,128]{1,0:T(8,128)S(1)}, f32[8,128]{1,0:T(8,128)S(1)}, u32[]{:S(2)}, u32[]{:S(2)}) collective-permute-start(f32[8,128]{1,0:T(8,128)S(1)} %add_add_fusion.1), channel_id=1, source_target_pairs={{0,8},{4,12},{8,0},{12,4},{16,24},{20,28},{24,16},{28,20},{1,9},{5... | collective-permute-start | bytes 12296 | tf_op jit(solution)/shard_map/ppermute | solution.py:24
  (19 other events, 165.7 us)

commit v4 on v3

--- a/solution.py
+++ b/solution.py
@@ -13,6 +13,7 @@
 epsilon = 1e-06
 kinetic_weight = 0.1
 F32, BF16 = jnp.float32, jnp.bfloat16
+AHEAD, BEHIND = (2, 0), (3, 1)
 KERNEL_VMEM = 16 * 1024 * 1024
 
 
@@ -258,36 +259,19 @@
     return lax.rem(lax.axis_index("seq"), spread)
 
 
-def fetch_kernel(count, *refs):
-    sources, targets, sems = refs[:count], refs[count : 2 * count], refs[2 * count]
+def setup_kernel(plan, images, count, *refs):
+    n_tp, _, spread, _, _ = plan
+    length_ref, index_ref, refs = refs[0], refs[1], refs[2:]
+    sources, targets, refs = refs[:count], refs[count : 2 * count], refs[2 * count :]
+    near_rows, near_keys, far_keys, time_ref, weight_ref, sems = refs
     copies = [
         pltpu.make_async_copy(source, target, sems.at[i])
         for i, (source, target) in enumerate(zip(sources, targets))
     ]
     for copy in copies:
         copy.start()
-    for copy in copies:
-        copy.wait()
-
-
-def fetch(*arrays):
-    count = len(arrays)
-    size = sum(math.prod(a.shape) * a.dtype.itemsize for a in arrays)
-    return pl.pallas_call(
-        functools.partial(fetch_kernel, count),
-        out_shape=[whole(a.shape, a.dtype) for a in arrays],
-        in_specs=[pl.BlockSpec(memory_space=pltpu.HBM)] * count,
-        out_specs=[VM] * count,
-        scratch_shapes=[pltpu.SemaphoreType.DMA((count,))],
-        compiler_params=pltpu.CompilerParams(vmem_limit_bytes=KERNEL_VMEM),
-        cost_estimate=pl.CostEstimate(flops=200 * size, bytes_accessed=size, transcendentals=0),
-    )(*[pltpu.with_memory_space_constraint(a, pltpu.HBM) for a in arrays])
-
-
-def setup_kernel(partner, row_count, *refs):
-    length_ref, index_ref, near_rows, near_keys, far_keys, own_rows, time_ref = refs
+    row_count, width = time_ref.shape[0], sources[0].shape[1]
     seq_index = lax.axis_index("seq")
-    images = length_ref.shape[0]
     ends = [length_ref[0]]
     for i in range(1, images):
         ends.append(ends[-1] + length_ref[i])
@@ -300,20 +284,58 @@
 
     near_rows[...] = image_of(near_rows.shape, 0, seq_index)
     near_keys[...] = image_of(near_keys.shape, 1, seq_index)
-    far_keys[...] = image_of(far_keys.shape, 1, seq_index ^ partner)
-    own = image_of(own_rows.shape, 0, seq_index)
-    own_rows[...] = own
+    far_keys[...] = image_of(far_keys.shape, 1, seq_index ^ spread)
+    own = image_of(time_ref.shape, 0, seq_index)
     time = jnp.zeros(own.shape, F32)
+    length = jnp.ones(own.shape, F32)
     for i in range(images):
         time = jnp.where(own == i, index_ref[i].astype(F32) / TGRID, time)
+        length = jnp.where(own == i, length_ref[i].astype(F32), length)
     time_ref[...] = time
-
-
-def qkv_kernel(plan, moving, *refs):
+    weight_ref[...] = 1.0 / (length * (n_tp * width * images))
+    for copy in copies:
+        copy.wait()
+
+
+def setup(plan, lengths, t_index, row_count, *arrays):
+    spread = plan[2]
+    count, grouped = len(arrays), spread * row_count
+    size = sum(math.prod(a.shape) * a.dtype.itemsize for a in arrays)
+    outs = [whole(a.shape, a.dtype) for a in arrays] + [
+        whole((grouped, 1), jnp.int32),
+        whole((1, grouped), jnp.int32),
+        whole((1, grouped), jnp.int32),
+        whole((row_count, 1), F32),
+        whole((row_count, 1), F32),
+    ]
+    results = pl.pallas_call(
+        functools.partial(setup_kernel, plan, lengths.shape[0], count),
+        out_shape=outs,
+        in_specs=[pl.BlockSpec(memory_space=pltpu.SMEM)] * 2
+        + [pl.BlockSpec(memory_space=pltpu.HBM)] * count,
+        out_specs=[VM] * len(outs),
+        scratch_shapes=[pltpu.SemaphoreType.DMA((count,))],
+        compiler_params=pltpu.CompilerParams(vmem_limit_bytes=KERNEL_VMEM),
+        cost_estimate=pl.CostEstimate(flops=200 * size, bytes_accessed=size, transcendentals=0),
+    )(lengths, t_index, *[pltpu.with_memory_space_constraint(a, pltpu.HBM) for a in arrays])
+    return results[:count], results[count:]
+
+
+def early_kernel(plan, moving, *refs):
+    part_kernel(plan, moving, 0, None, refs)
+
+
+def late_kernel(plan, moving, *refs):
+    rows_ref, squares_ref, *sums = refs[: 2 + plan[2] + plan[2] // 2]
+    part_kernel(plan, moving, plan[0] // 2, (rows_ref, squares_ref, sums), refs[2 + len(sums) :])
+
+
+def part_kernel(plan, moving, first, early, refs):
     n_tp, _, spread, head_dim, step_size = plan
-    state, refs = refs[:n_tp], refs[n_tp:]
+    half = n_tp // 2
+    state, refs = refs[:half], refs[half:]
     if moving:
-        near, far, refs = refs[:n_tp], refs[n_tp : 2 * n_tp], refs[2 * n_tp :]
+        near, far, refs = refs[:half], refs[half : 2 * half], refs[2 * half :]
     time_ref, mod_ref, q_ref, k_ref, v_ref, q_gain, k_gain, rows_ref, scale_ref = refs[:9]
     outs, pairs = refs[9 : 9 + spread], refs[9 + spread :]
     tp_index = lax.axis_index("tp")
@@ -322,22 +344,22 @@
     times = time_ref[...]
     if moving:
         times = times + step_size
-    squares = jnp.zeros_like(times)
-    for k in range(n_tp):
+    squares = early[1][...] if early else jnp.zeros_like(times)
+    for k in range(half):
         x = state[k][...].astype(F32)
         if moving:
             velocity = (near[k][...].astype(F32) + far[k][...].astype(F32)).astype(BF16)
             x = (x + step_size * velocity.astype(F32)).astype(BF16).astype(F32)
         squares = squares + jnp.sum(x * x, axis=1, keepdims=True)
-        mod = mod_ref[:, head_at(tp_index, k, width)]
+        mod = mod_ref[:, head_at(tp_index, first + k, width)]
         rows_ref[:, k * width : (k + 1) * width] = (x * (1.0 + times * mod)).astype(BF16)
-    scale = lax.rsqrt(squares / (n_tp * width) + epsilon)
-    scale_ref[...] = scale
-
-    def project(pieces):
-        total = None
-        for k in range(n_tp):
-            rows = head_at(tp_index, k, width)
+    scale = lax.rsqrt(squares / (n_tp * width) + epsilon) if early else None
+    scale_ref[...] = scale if early else squares
+
+    def project(pieces, before):
+        total = before[...] if early else None
+        for k in range(half):
+            rows = head_at(tp_index, first + k, width)
             weight = jnp.concatenate(
                 [ref[rows, head_at(block, m, head_dim)] for ref, m in pieces], axis=1
             )
@@ -345,21 +367,28 @@
                 rows_ref[:, k * width : (k + 1) * width], weight, preferred_element_type=F32
             )
             total = part if total is None else total + part
-        return total * scale
-
-    for m in [*range(1, spread), 0]:
-        total = project([(k_ref, m), (v_ref, m)])
+        return total * scale if early else total
+
+    sums = early[2] if early else [None] * (spread + spread // 2)
+    for m in range(spread):
+        total = project([(k_ref, m), (v_ref, m)], sums[m])
+        if not early:
+            outs[m][...] = total
+            continue
         keys = normed_head(total[:, :head_dim], k_gain[...])
         values = total[:, head_dim:].astype(BF16)
         outs[m][:, head_dim : 2 * head_dim] = keys
         outs[m][:, 2 * head_dim :] = values
         pairs[m][:, :head_dim] = keys
         pairs[m][:, head_dim:] = values
-    for first in range(0, spread, 2):
-        total = project([(q_ref, first), (q_ref, first + 1)])
+    for i in range(spread // 2):
+        total = project([(q_ref, 2 * i), (q_ref, 2 * i + 1)], sums[spread + i])
+        if not early:
+            pairs[i][...] = total
+            continue
         for m in range(2):
-            cut = total[:, m * head_dim : (m + 1) * head_dim]
-            outs[first + m][:, :head_dim] = normed_head(cut, q_gain[...])
+            piece = total[:, m * head_dim : (m + 1) * head_dim]
+            outs[2 * i + m][:, :head_dim] = normed_head(piece, q_gain[...])
 
 
 def terms_kernel(n_tp, left_ref, right_ref, scale_ref, *outs):
@@ -379,19 +408,19 @@
         out[...] = (own[...].astype(F32) + other[...].astype(F32)).astype(BF16)
 
 
-def out_kernel(plan, *refs):
-    n_tp, _, spread, head_dim, _ = plan
+def out_kernel(plan, places, *refs):
+    _, _, spread, head_dim, _ = plan
     pieces, right_ref, outs = refs[:spread], refs[spread], refs[spread + 1 :]
     tp_index = lax.axis_index("tp")
     block = head_block_of(spread)
     width = outs[0].shape[1]
     left = jnp.concatenate([piece[...] for piece in pieces], axis=1)
-    for k in list(range(1, n_tp, 2)) + list(range(0, n_tp, 2)):
+    for k, out in zip(places, outs):
         columns = head_at(tp_index, k, width)
         right = jnp.concatenate(
             [right_ref[head_at(block, m, head_dim), columns] for m in range(spread)], axis=0
         )
-        outs[k][...] = jnp.dot(left, right, preferred_element_type=F32).astype(BF16)
+        out[...] = jnp.dot(left, right, preferred_element_type=F32).astype(BF16)
 
 
 def scores_of(query, keys, query_image, key_image, head_dim):
@@ -401,17 +430,25 @@
     return jnp.where(query_image == key_image, scores, -1e30)
 
 
-def near_kernel(spread, head_dim, *refs):
-    triples, refs = refs[:spread], refs[spread:]
-    query_image, key_image, top_ref, total_ref, sum_ref = refs
+def near_kernel(spread, head_dim, ahead, *refs):
+    triples, pairs, refs = refs[:spread], refs[spread : spread + len(ahead)], refs[spread + len(ahead) :]
+    query_image, near_image, far_image, top_ref, total_ref, sum_ref = refs
     rows = triples[0].shape[0]
-    keys = jnp.concatenate([triple[:, head_dim : 2 * head_dim] for triple in triples], axis=0)
-    values = jnp.concatenate([triple[:, 2 * head_dim :] for triple in triples], axis=0)
+    keys = jnp.concatenate(
+        [triple[:, head_dim : 2 * head_dim] for triple in triples]
+        + [pair[:, :head_dim] for pair in pairs],
+        axis=0,
+    )
+    values = jnp.concatenate(
+        [triple[:, 2 * head_dim :] for triple in triples] + [pair[:, head_dim:] for pair in pairs],
+        axis=0,
+    )
+    key_image = jnp.concatenate(
+        [near_image[...]] + [far_image[:, m * rows : (m + 1) * rows] for m in ahead], axis=1
+    )
     for m in range(spread):
         cut = slice(m * rows, (m + 1) * rows)
-        scores = scores_of(
-            triples[m][:, :head_dim], keys, query_image[cut], key_image[...], head_dim
-        )
+        scores = scores_of(triples[m][:, :head_dim], keys, query_image[cut], key_image, head_dim)
         top = jnp.max(scores, axis=1, keepdims=True)
         weights = jnp.exp(scores - top)
         top_ref[cut] = top
@@ -419,18 +456,17 @@
         sum_ref[cut] = jnp.dot(weights.astype(BF16), values, preferred_element_type=F32)
 
 
-def far_kernel(spread, head_dim, *refs):
-    triples, pairs, refs = refs[:spread], refs[spread : 2 * spread], refs[2 * spread :]
-    query_image, key_image, top_ref, total_ref, sum_ref = refs[:5]
+def far_kernel(spread, head_dim, behind, *refs):
+    triples, pairs, refs = refs[:spread], refs[spread : spread + len(behind)], refs[spread + len(behind) :]
+    query_image, far_image, top_ref, total_ref, sum_ref = refs[:5]
     outs = refs[5:]
     rows = triples[0].shape[0]
     keys = jnp.concatenate([pair[:, :head_dim] for pair in pairs], axis=0)
     values = jnp.concatenate([pair[:, head_dim:] for pair in pairs], axis=0)
+    key_image = jnp.concatenate([far_image[:, m * rows : (m + 1) * rows] for m in behind], axis=1)
     for m in [*range(1, spread), 0]:
         cut = slice(m * rows, (m + 1) * rows)
-        scores = scores_of(
-            triples[m][:, :head_dim], keys, query_image[cut], key_image[...], head_dim
-        )
+        scores = scores_of(triples[m][:, :head_dim], keys, query_image[cut], key_image, head_dim)
         old = top_ref[cut]
         top = jnp.maximum(old, jnp.max(scores, axis=1, keepdims=True))
         weights = jnp.exp(scores - top)
@@ -442,19 +478,25 @@
         outs[m][...] = (mixed / total).astype(BF16)
 
 
-def loss_kernel(*refs):
-    near0, far0, near1, far1, student_ref, image_ref, target_ref, part_ref = refs
-    velocity0 = (near0[...].astype(F32) + far0[...].astype(F32)).astype(BF16).astype(F32)
+def base_kernel(near0, far0, near_s, far_s, student_ref, base_ref):
+    width = student_ref.shape[1]
+    student = (near_s[...].astype(F32) + far_s[...].astype(F32)).astype(BF16)
+    student_ref[...] = student
+    base_ref[:, :width] = (near0[...].astype(F32) + far0[...].astype(F32)).astype(BF16)
+    base_ref[:, width:] = student
+
+
+def loss_kernel(near1, far1, base_ref, weight_ref, target_ref, part_ref):
+    width = target_ref.shape[1]
+    velocity0 = base_ref[:, :width].astype(F32)
     velocity1 = (near1[...].astype(F32) + far1[...].astype(F32)).astype(BF16).astype(F32)
     target = (0.5 * (velocity0 + velocity1)).astype(BF16)
     target_ref[...] = target
-    student = student_ref[...].astype(F32)
+    student = base_ref[:, width:].astype(F32)
     residual = student - target.astype(F32)
-    per_token = jnp.sum(residual * residual + kinetic_weight * (student * student), axis=1, keepdims=True)
-    lanes = lax.broadcasted_iota(jnp.int32, part_ref.shape, 1)
-    part_ref[...] = jnp.sum(
-        jnp.where(image_ref[...] == lanes[:1], per_token, 0.0), axis=0, keepdims=True
-    ) + jnp.zeros(part_ref.shape, F32)
+    terms = residual * residual + kinetic_weight * (student * student)
+    per_token = jnp.sum(terms, axis=1, keepdims=True) * weight_ref[...]
+    part_ref[...] = jnp.sum(per_token, axis=0, keepdims=True) + jnp.zeros(part_ref.shape, F32)
 
 
 def on_device_fused(
@@ -490,19 +532,31 @@
     def seq_swap(value, mask):
         return swap(value, "seq", n_seq, mask)
 
-    def project(state, velocity, times):
-        operands = list(state)
+    def half_call(body, state, velocity, first, before, outs, flops):
+        half = slice(first, first + n_tp // 2)
+        operands = list(before) + list(state[half])
         if velocity is not None:
-            operands += velocity[0] + velocity[1]
-        rows, scale, *blocks = call(
-            functools.partial(qkv_kernel, plan, velocity is not None),
-            [whole((row_count, inner)), whole((row_count, 1), F32)]
-            + [whole((row_count, 3 * head_dim))] * spread
+            operands += velocity[0][half] + velocity[1][half]
+        return call(
+            functools.partial(body, plan, velocity is not None),
+            [whole((row_count, inner // 2)), whole((row_count, 1), F32)] + outs,
+            flops,
+            *operands, start_time, mod_row, q_weight, k_weight, v_weight, q_row, k_row,
+        )
+
+    def project(state, velocity):
+        flops = 3 * row_count * inner * spread * head_dim
+        wide = whole((row_count, 2 * head_dim), F32)
+        early = half_call(
+            early_kernel, state, velocity, 0, (), [wide] * (spread + spread // 2), flops
+        )
+        late = half_call(
+            late_kernel, state, velocity, n_tp // 2, early,
+            [whole((row_count, 3 * head_dim))] * spread
             + [whole((row_count, 2 * head_dim))] * spread,
-            6 * row_count * inner * spread * head_dim,
-            *operands, times, mod_row, q_weight, k_weight, v_weight, q_row, k_row,
-        )
-        return rows, scale, blocks[:spread], blocks[spread:]
+            flops,
+        )
+        return early[0], late[1], late[2 : 2 + spread], late[2 + spread :]
 
     def attend(triples, pairs):
         far_pairs, near_triples = [], [triples[0]]
@@ -512,39 +566,42 @@
             near_triples.append(seq_swap(triples[m], m))
         flops = 4 * grouped**2 * head_dim
         sums = call(
-            functools.partial(near_kernel, spread, head_dim),
+            functools.partial(near_kernel, spread, head_dim, AHEAD),
             [whole((grouped, 1), F32)] * 2 + [whole((grouped, head_dim), F32)],
             flops,
-            *near_triples, near_rows, near_keys,
+            *near_triples, *[far_pairs[m] for m in AHEAD], near_rows, near_keys, far_keys,
         )
         pieces = call(
-            functools.partial(far_kernel, spread, head_dim),
+            functools.partial(far_kernel, spread, head_dim, BEHIND),
             [whole((row_count, head_dim))] * spread,
             flops,
-            *near_triples, *far_pairs, near_rows, far_keys, *sums,
+            *near_triples, *[far_pairs[m] for m in BEHIND], near_rows, far_keys, *sums,
         )
         back = [pieces[0]]
         for m in range(1, spread):
             back.append(seq_swap(pieces[m], m))
-        return call(
-            functools.partial(out_kernel, plan),
-            [whole((row_count, width))] * n_tp,
-            2 * row_count * spread * head_dim * inner,
-            *back, out_weight,
-        )
+        terms = [None] * n_tp
+        for places in ((3, 2), (1, 0)):
+            results = call(
+                functools.partial(out_kernel, plan, places),
+                [whole((row_count, width))] * len(places),
+                len(places) * 2 * row_count * spread * head_dim * width,
+                *back, out_weight,
+            )
+            for k, result in zip(places, results):
+                terms[k] = result
+        return terms
 
     def halve(terms):
-        held = dict(enumerate(terms))
-        for bit in bits_of(n_tp)[:-1]:
-            sent = {k: tp_swap(held[k], bit) for k in held if k & bit}
-            kept = [k for k in held if not k & bit]
-            sums = call(
-                functools.partial(add_kernel, len(kept)),
-                [whole((row_count, width))] * len(kept),
+        held = {}
+        for k in (2, 0):
+            other_term = tp_swap(terms[k ^ 1], 1)
+            (held[k],) = call(
+                functools.partial(add_kernel, 1),
+                [whole((row_count, width))],
                 1000 * row_count,
-                *[held[k] for k in kept], *[sent[k ^ bit] for k in kept],
+                terms[k], other_term,
             )
-            held = dict(zip(kept, sums))
         return held
 
     def spread_low(held):
@@ -558,25 +615,13 @@
     top_block = tp_swap(latents, top_bit)
     held = spread_low({0: latents}) | spread_low({top_bit: top_block})
     blocks = [held[k] for k in range(n_tp)]
-    blocks[0], q_weight, k_weight, v_weight, mod_row, q_row, k_row = fetch(
-        latents, q_weight, k_weight, v_weight, mod_row, q_row, k_row
-    )
-    near_rows, near_keys, far_keys, own_rows, start_time = call(
-        functools.partial(setup_kernel, spread, row_count),
-        [
-            whole((grouped, 1), jnp.int32),
-            whole((1, grouped), jnp.int32),
-            whole((1, grouped), jnp.int32),
-            whole((row_count, 1), jnp.int32),
-            whole((row_count, 1), F32),
-        ],
-        1000 * row_count,
-        lengths,
-        t_index,
-        specs=[pl.BlockSpec(memory_space=pltpu.SMEM)] * 2,
-    )
-
-    rows, scale, triples, pairs = project(blocks, None, start_time)
+    fetched, places = setup(
+        plan, lengths, t_index, row_count,
+        latents, q_weight, k_weight, v_weight, mod_row, q_row, k_row,
+    )
+    blocks[0], q_weight, k_weight, v_weight, mod_row, q_row, k_row = fetched
+    near_rows, near_keys, far_keys, start_time, loss_weight = places
+    rows, scale, triples, pairs = project(blocks, None)
     terms = attend(triples, pairs)
     student_terms = call(
         functools.partial(terms_kernel, n_tp),
@@ -586,16 +631,18 @@
     )
     held_s = halve(student_terms)
     held = halve(terms)
-    other = {k ^ top_bit: tp_swap(held[k], top_bit) for k in sorted(held, reverse=True)}
+    other = {}
+    for k in (2, 0):
+        other[k ^ top_bit] = tp_swap(held[k], top_bit)
     velocity = tuple([low[k] for k in range(n_tp)] for low in map(spread_low, (held, other)))
-    _, _, triples, pairs = project(blocks, velocity, start_time)
+    _, _, triples, pairs = project(blocks, velocity)
     other_s = tp_swap(held_s[top_bit], top_bit)
     terms = attend(triples, pairs)
-    (student,) = call(
-        functools.partial(add_kernel, 1),
-        [whole((row_count, width))],
-        1000 * row_count,
-        held_s[0], other_s,
+    student, base = call(
+        base_kernel,
+        [whole((row_count, width)), whole((row_count, 2 * width))],
+        10 * row_count * width,
+        held[0], other[0], held_s[0], other_s,
     )
     held1 = halve(terms)
     other1 = tp_swap(held1[top_bit], top_bit)
@@ -603,11 +650,9 @@
         loss_kernel,
         [whole((row_count, width)), whole((8, 128), F32)],
         10 * row_count * width,
-        held[0], other[0], held1[0], other1, student, own_rows,
+        held1[0], other1, base, loss_weight,
     )
     part = part + tp_swap(part, 1)
-    for bit in bits_of(n_tp)[1:-1]:
-        part = part + tp_swap(part, bit)
 
     def both(value, seq_mask, tp_mask):
         return lax.ppermute(
@@ -623,8 +668,7 @@
     part = (part + both(part, 0, top_bit)) + (both(part, 1, 0) + both(part, 1, top_bit))
     low = n_seq // 4
     part = (part + seq_swap(part, low)) + (seq_swap(part, 2 * low) + seq_swap(part, 3 * low))
-    image_sum = part[0, : lengths.shape[0]]
-    loss = jnp.mean(image_sum / (lengths.astype(F32) * inner))
+    loss = part[0, 0]
     return (target, student, loss)
 
 
@@ -651,7 +695,7 @@
             latents.shape[1] % 128 == 0
             and q_gain.shape[0] == 128
             and n_seq == 2 * heads_here == 8
-            and n_tp in (2, 4)
+            and n_tp == 4
         )
         run = on_device_fused if fused else on_device
         return run(dict(mesh.shape), *arguments)

time: 120 us -> 114 us (0.950)
  waiting for transfers between devices: 48 us -> 43.7 us
  between operations: 2.61 us -> 0.86 us
    ppermute x41, waiting for transfers between devices: 44.9 us -> 40.2 us  [swap(): return lax.ppermute(value, axis, [(i, i ^ mask) for i in range(size)])]
    pallas_call x15 -> x21, Pallas kernels: 14.7 us -> 15.4 us  [call(): pl.pallas_call(body, out_shape=outs, in_specs=specs or [VM] * len(operand...]
  transfers between devices with their start and end apart: 44 -> 44, of which waited for: 24 -> 24; matrix products, arithmetic and copies ran while one was open for 0% -> 0% of each run, Pallas kernels for 8% -> 11%
where the time goes in v4:
time: 114 us
  starting transfers between devices  47.7 us (42%)
  waiting for transfers between devices  43.7 us (38%)
  Pallas kernels  19.8 us (17%)
  local copies, waits for them, and re-layouts  1.84 us (2%)
    ppermute x41, starting transfers between devices, swap(): return lax.ppermute(value, axis, [(i, i ^ mask) for i in range(size)])  44.2 us
    ppermute x41, waiting for transfers between devices, swap(): return lax.ppermute(value, axis, [(i, i ^ mask) for i in range(size)])  40.2 us
    pallas_call x21, Pallas kernels, call(): pl.pallas_call(body, out_shape=outs, in_specs=specs or [VM] * len(operand...  15.4 us
    pallas_call x1, Pallas kernels, setup(): pl.pallas_call(functools.partial(setup_kernel, plan, lengths.shape[0], co...  4.47 us
    ppermute x3, starting transfers between devices, both(): lax.ppermute(value, ('seq', 'tp'), [(s * n_tp + t, (s ^ seq_mask) * n_tp...  3.49 us
    ppermute x3, waiting for transfers between devices, both(): lax.ppermute(value, ('seq', 'tp'), [(s * n_tp + t, (s ^ seq_mask) * n_tp...  3.44 us
  transfers between devices with their start and end apart: 44, of which 24 were waited for; matrix products, arithmetic and copies ran while one was open for 0% of the time, Pallas kernels for 11%

profile of v4, /device:TPU:0, one launch (start us, length us, event | category | flops | bytes accessed | tf_op | source)
XLA Modules:
  0.0 113.9 jit_solution(14105465579366437551)
XLA Ops:
  0.6 3.0 %collective-permute-start.1 = (bf16[128,768]{1,0:T(8,128)(2,1)}, bf16[128,768]{1,0:T(8,128)(2,1)S(1)}, u32[]{:S(2)}, u32[]{:S(2)}) collective-permute-start(bf16[128,768]{1,0:T(8,128)(2,1)} %refs_2_.1), channel_id=1, source_target_pairs={{0,2},{1,3},{2,0},{3,1},{4,6},{5,7},{6,4},{7,5},{8,10},{9,11},{10,... | collective-permute-start | bytes 589832 | tf_op jit(solution)/shard_map/ppermute | solution.py:25
  3.7 5.1 %collective-permute-done.1.refs_8_ = bf16[128,768]{1,0:T(8,128)(2,1)S(1)} collective-permute-done((bf16[128,768]{1,0:T(8,128)(2,1)}, bf16[128,768]{1,0:T(8,128)(2,1)S(1)}, u32[]{:S(2)}, u32[]{:S(2)}) %collective-permute-start.1) | collective-permute-done | bytes 196640 | tf_op jit(solution)/shard_map/ppermute | solution.py:25
  10.1 4.5 %shard_map.130 = (bf16[128,768]{1,0:T(8,128)(2,1)S(1)}, bf16[3072,512]{1,0:T(8,128)(2,1)S(1)}, bf16[3072,512]{1,0:T(8,128)(2,1)S(1)}, bf16[3072,512]{1,0:T(8,128...) custom-call(s32[2]{0:T(128)S(1)} %copy-done.1, ...), custom_call_target="tpu_custom_call" | custom-call | flops 1929420800 | bytes 9647104 | tf_op jit(solution)/shard_map/pallas_call | solution.py:311
  15.6 1.6 %shard_map.132 = (bf16[128,1536]{1,0:T(8,128)(2,1)}, f32[128,1]{1,0:T(8,128)S(1)}, bf16[128,384]{1,0:T(8,128)(2,1)S(1)}, bf16[128,384]{1,0:T(8,128)(2,1)S(1)}, b...) custom-call(bf16[128,1536]{1,0:T(8,128)(2,1)S(1)} %get-tuple-element, ...), custom_call_target="tpu_custom_call" | custom-call | flops 603979776 | bytes 11024384 | tf_op jit(solution)/shard_map/pallas_call | solution.py:238
  17.3 3.8 %collective-permute-start.8 = (bf16[128,256]{1,0:T(8,128)(2,1)S(1)}, bf16[128,256]{1,0:T(8,128)(2,1)S(1)}, u32[]{:S(2)}, u32[]{:S(2)}) collective-permute-start(bf16[128,256]{1,0:T(8,128)(2,1)S(1)} %get-tuple-element.102), channel_id=1, source_target_pairs={{0,24},{4,28},{8,16},{12,20},{16,8},{20,12},{24,0},{28,4},{1,25},{... | collective-permute-start | bytes 196616 | tf_op jit(solution)/shard_map/ppermute | solution.py:25
  21.1 1.5 %collective-permute-start.3 = (bf16[128,384]{1,0:T(8,128)(2,1)S(1)}, bf16[128,384]{1,0:T(8,128)(2,1)S(1)}, u32[]{:S(2)}, u32[]{:S(2)}) collective-permute-start(bf16[128,384]{1,0:T(8,128)(2,1)S(1)} %get-tuple-element.95), channel_id=1, source_target_pairs={{0,4},{4,0},{8,12},{12,8},{16,20},{20,16},{24,28},{28,24},{1,5},{5... | collective-permute-start | bytes 294920 | tf_op jit(solution)/shard_map/ppermute | solution.py:25
  24.6 4.3 %collective-permute-start.6 = (bf16[128,256]{1,0:T(8,128)(2,1)S(1)}, bf16[128,256]{1,0:T(8,128)(2,1)S(1)}, u32[]{:S(2)}, u32[]{:S(2)}) collective-permute-start(bf16[128,256]{1,0:T(8,128)(2,1)S(1)} %get-tuple-element.98), channel_id=1, source_target_pairs={{0,28},{4,24},{8,20},{12,16},{16,12},{20,8},{24,4},{28,0},{1,29},{... | collective-permute-start | bytes 196616 | tf_op jit(solution)/shard_map/ppermute | solution.py:25
  29.3 2.0 %collective-permute-done.5.refs_3_ = bf16[128,384]{1,0:T(8,128)(2,1)S(1)} collective-permute-done((bf16[128,384]{1,0:T(8,128)(2,1)S(1)}, bf16[128,384]{1,0:T(8,128)(2,1)S(1)}, u32[]{:S(2)}, u32[]{:S(2)}) %collective-permute-start.5) | collective-permute-done | bytes 98336 | tf_op jit(solution)/shard_map/ppermute | solution.py:25
  33.6 1.8 %collective-permute-done.7.refs_5_ = bf16[128,256]{1,0:T(8,128)(2,1)S(1)} collective-permute-done((bf16[128,256]{1,0:T(8,128)(2,1)S(1)}, bf16[128,256]{1,0:T(8,128)(2,1)S(1)}, u32[]{:S(2)}, u32[]{:S(2)}) %collective-permute-start.7) | collective-permute-done | bytes 65568 | tf_op jit(solution)/shard_map/ppermute | solution.py:25
  36.8 1.5 %collective-permute-start.10 = (bf16[128,128]{1,0:T(8,128)(2,1)S(1)}, bf16[128,128]{1,0:T(8,128)(2,1)S(1)}, u32[]{:S(2)}, u32[]{:S(2)}) collective-permute-start(bf16[128,128]{1,0:T(8,128)(2,1)S(1)} %get-tuple-element.109), channel_id=1, source_target_pairs={{0,4},{4,0},{8,12},{12,8},{16,20},{20,16},{24,28},{28,24},{1,5},{5... | collective-permute-start | bytes 98312 | tf_op jit(solution)/shard_map/ppermute | solution.py:25
  38.2 2.1 %collective-permute-start.12 = (bf16[128,128]{1,0:T(8,128)(2,1)S(1)}, bf16[128,128]{1,0:T(8,128)(2,1)S(1)}, u32[]{:S(2)}, u32[]{:S(2)}) collective-permute-start(bf16[128,128]{1,0:T(8,128)(2,1)S(1)} %get-tuple-element.111), channel_id=1, source_target_pairs={{0,12},{4,8},{8,4},{12,0},{16,28},{20,24},{24,20},{28,16},{1,13},{... | collective-permute-start | bytes 98312 | tf_op jit(solution)/shard_map/ppermute | solution.py:25
  45.0 1.5 %collective-permute-start.16 = (bf16[128,768]{1,0:T(8,128)(2,1)S(1)}, bf16[128,768]{1,0:T(8,128)(2,1)S(1)}, u32[]{:S(2)}, u32[]{:S(2)}) collective-permute-start(bf16[128,768]{1,0:T(8,128)(2,1)S(1)} %shard_map.138.refs_10_), channel_id=1, source_target_pairs={{0,2},{1,3},{2,0},{3,1},{4,6},{5,7},{6,4},{7,5},{8,10},{9,11},{10,... | collective-permute-start | bytes 589832 | tf_op jit(solution)/shard_map/ppermute | solution.py:25
  47.3 5.6 %collective-permute-done.16.refs_4_.far0 = bf16[128,768]{1,0:T(8,128)(2,1)S(1)} collective-permute-done((bf16[128,768]{1,0:T(8,128)(2,1)S(1)}, bf16[128,768]{1,0:T(8,128)(2,1)S(1)}, u32[]{:S(2)}, u32[]{:S(2)}) %collective-permute-start.16) | collective-permute-done | bytes 196640 | tf_op jit(solution)/shard_map/ppermute | solution.py:25
  53.4 2.9 %collective-permute-done.19.refs_12_ = bf16[128,768]{1,0:T(8,128)(2,1)S(1)} collective-permute-done((bf16[128,768]{1,0:T(8,128)(2,1)S(1)}, bf16[128,768]{1,0:T(8,128)(2,1)S(1)}, u32[]{:S(2)}, u32[]{:S(2)}) %collective-permute-start.19) | collective-permute-done | bytes 196640 | tf_op jit(solution)/shard_map/ppermute | solution.py:25
  57.7 1.8 %shard_map.140 = (bf16[128,1536]{1,0:T(8,128)(2,1)}, f32[128,1]{1,0:T(8,128)}, bf16[128,384]{1,0:T(8,128)(2,1)S(1)}, bf16[128,384]{1,0:T(8,128)(2,1)S(1)}, bf16[...) custom-call(bf16[128,1536]{1,0:T(8,128)(2,1)S(1)} %get-tuple-element, ...), custom_call_target="tpu_custom_call" | custom-call | flops 603979776 | bytes 11810816 | tf_op jit(solution)/shard_map/pallas_call | solution.py:238
  59.5 2.3 %collective-permute-start.26 = (bf16[128,256]{1,0:T(8,128)(2,1)S(1)}, bf16[128,256]{1,0:T(8,128)(2,1)S(1)}, u32[]{:S(2)}, u32[]{:S(2)}) collective-permute-start(bf16[128,256]{1,0:T(8,128)(2,1)S(1)} %get-tuple-element.130), channel_id=1, source_target_pairs={{0,24},{4,28},{8,16},{12,20},{16,8},{20,12},{24,0},{28,4},{1,25},{... | collective-permute-start | bytes 196616 | tf_op jit(solution)/shard_map/ppermute | solution.py:25
  64.8 1.7 %collective-permute-start.23 = (bf16[128,384]{1,0:T(8,128)(2,1)S(1)}, bf16[128,384]{1,0:T(8,128)(2,1)S(1)}, u32[]{:S(2)}, u32[]{:S(2)}) collective-permute-start(bf16[128,384]{1,0:T(8,128)(2,1)S(1)} %get-tuple-element.127), channel_id=1, source_target_pairs={{0,12},{4,8},{8,4},{12,0},{16,28},{20,24},{24,20},{28,16},{1,13},{... | collective-permute-start | bytes 294920 | tf_op jit(solution)/shard_map/ppermute | solution.py:25
  66.4 2.6 %collective-permute-start.24 = (bf16[128,256]{1,0:T(8,128)(2,1)S(1)}, bf16[128,256]{1,0:T(8,128)(2,1)S(1)}, u32[]{:S(2)}, u32[]{:S(2)}) collective-permute-start(bf16[128,256]{1,0:T(8,128)(2,1)S(1)} %get-tuple-element.128), channel_id=1, source_target_pairs={{0,28},{4,24},{8,20},{12,16},{16,12},{20,8},{24,4},{28,0},{1,29},{... | collective-permute-start | bytes 196616 | tf_op jit(solution)/shard_map/ppermute | solution.py:25
  69.5 1.8 %collective-permute-start.25 = (bf16[128,256]{1,0:T(8,128)(2,1)S(1)}, bf16[128,256]{1,0:T(8,128)(2,1)S(1)}, u32[]{:S(2)}, u32[]{:S(2)}) collective-permute-start(bf16[128,256]{1,0:T(8,128)(2,1)S(1)} %get-tuple-element.129), channel_id=1, source_target_pairs={{0,20},{4,16},{8,28},{12,24},{16,4},{20,0},{24,12},{28,8},{1,21},{... | collective-permute-start | bytes 196616 | tf_op jit(solution)/shard_map/ppermute | solution.py:25
  72.7 1.4 %shard_map.141 = (f32[512,1]{1,0:T(8,128)S(1)}, f32[512,1]{1,0:T(8,128)S(1)}, f32[512,128]{1,0:T(8,128)S(1)}) custom-call(bf16[128,384]{1,0:T(8,128)(2,1)S(1)} %get-tuple-element.124.refs_0_, bf16[128,384]{1,0:T(8,128)(2,1)S(1)} %collective-permute-done.21.refs_1_, bf16[128,384]{1,0:T(8,128)(2,1)S(1)} %collective-permute-done.22.refs_2_, ...), custom_call_target="tpu_custom_call" | custom-call | flops 134217728 | bytes 530432 | tf_op jit(solution)/shard_map/pallas_call | solution.py:238
  74.1 2.8 %collective-permute-done.25.refs_5_ = bf16[128,256]{1,0:T(8,128)(2,1)S(1)} collective-permute-done((bf16[128,256]{1,0:T(8,128)(2,1)S(1)}, bf16[128,256]{1,0:T(8,128)(2,1)S(1)}, u32[]{:S(2)}, u32[]{:S(2)}) %collective-permute-start.25) | collective-permute-done | bytes 65568 | tf_op jit(solution)/shard_map/ppermute | solution.py:25
  79.4 2.4 %collective-permute-start.30 = (bf16[128,128]{1,0:T(8,128)(2,1)S(1)}, bf16[128,128]{1,0:T(8,128)(2,1)S(1)}, u32[]{:S(2)}, u32[]{:S(2)}) collective-permute-start(bf16[128,128]{1,0:T(8,128)(2,1)S(1)} %get-tuple-element.138), channel_id=1, source_target_pairs={{0,12},{4,8},{8,4},{12,0},{16,28},{20,24},{24,20},{28,16},{1,13},{... | collective-permute-start | bytes 98312 | tf_op jit(solution)/shard_map/ppermute | solution.py:25
  85.2 1.6 %collective-permute-start.36 = (bf16[128,768]{1,0:T(8,128)(2,1)S(1)}, bf16[128,768]{1,0:T(8,128)(2,1)S(1)}, u32[]{:S(2)}, u32[]{:S(2)}) collective-permute-start(bf16[128,768]{1,0:T(8,128)(2,1)S(1)} %shard_map.149), channel_id=1, source_target_pairs={{0,2},{1,3},{2,0},{3,1},{4,6},{5,7},{6,4},{7,5},{8,10},{9,11},{10,... | collective-permute-start | bytes 589832 | tf_op jit(solution)/shard_map/ppermute | solution.py:25
  88.0 5.1 %collective-permute-done.36.far_s = bf16[128,768]{1,0:T(8,128)(2,1)S(1)} collective-permute-done((bf16[128,768]{1,0:T(8,128)(2,1)S(1)}, bf16[128,768]{1,0:T(8,128)(2,1)S(1)}, u32[]{:S(2)}, u32[]{:S(2)}) %collective-permute-start.36) | collective-permute-done | bytes 196640 | tf_op jit(solution)/shard_map/ppermute | solution.py:25
  93.9 2.5 %collective-permute-done.33.far1 = bf16[128,768]{1,0:T(8,128)(2,1)S(1)} collective-permute-done((bf16[128,768]{1,0:T(8,128)(2,1)S(1)}, bf16[128,768]{1,0:T(8,128)(2,1)S(1)}, u32[]{:S(2)}, u32[]{:S(2)}) %collective-permute-start.33) | collective-permute-done | bytes 196640 | tf_op jit(solution)/shard_map/ppermute | solution.py:25
  98.5 1.5 %collective-permute-start.38 = (f32[8,128]{1,0:T(8,128)S(1)}, f32[8,128]{1,0:T(8,128)S(1)}, u32[]{:S(2)}, u32[]{:S(2)}) collective-permute-start(f32[8,128]{1,0:T(8,128)S(1)} %add.21), channel_id=1, source_target_pairs={{0,2},{1,3},{2,0},{3,1},{4,6},{5,7},{6,4},{7,5},{8,10},{9,11},{10,... | collective-permute-start | bytes 12296 | tf_op jit(solution)/shard_map/ppermute | solution.py:658
  102.1 1.5 %collective-permute-done.39 = f32[8,128]{1,0:T(8,128)S(1)} collective-permute-done((f32[8,128]{1,0:T(8,128)S(1)}, f32[8,128]{1,0:T(8,128)S(1)}, u32[]{:S(2)}, u32[]{:S(2)}) %collective-permute-start.39) | collective-permute-done | bytes 4128 | tf_op jit(solution)/shard_map/ppermute | solution.py:658
  103.6 1.8 %collective-permute-done.40 = f32[8,128]{1,0:T(8,128)S(1)} collective-permute-done((f32[8,128]{1,0:T(8,128)S(1)}, f32[8,128]{1,0:T(8,128)S(1)}, u32[]{:S(2)}, u32[]{:S(2)}) %collective-permute-start.40) | collective-permute-done | bytes 4128 | tf_op jit(solution)/shard_map/ppermute | solution.py:658
  105.4 2.0 %collective-permute-start.41 = (f32[8,128]{1,0:T(8,128)S(1)}, f32[8,128]{1,0:T(8,128)S(1)}, u32[]{:S(2)}, u32[]{:S(2)}) collective-permute-start(f32[8,128]{1,0:T(8,128)S(1)} %add_add_fusion.1), channel_id=1, source_target_pairs={{0,8},{4,12},{8,0},{12,4},{16,24},{20,28},{24,16},{28,20},{1,9},{5... | collective-permute-start | bytes 12296 | tf_op jit(solution)/shard_map/ppermute | solution.py:25
  108.0 1.9 %collective-permute-start.43 = (f32[8,128]{1,0:T(8,128)S(1)}, f32[8,128]{1,0:T(8,128)S(1)}, u32[]{:S(2)}, u32[]{:S(2)}) collective-permute-start(f32[8,128]{1,0:T(8,128)S(1)} %add_add_fusion.1), channel_id=1, source_target_pairs={{0,24},{4,28},{8,16},{12,20},{16,8},{20,12},{24,0},{28,4},{1,25},{... | collective-permute-start | bytes 12296 | tf_op jit(solution)/shard_map/ppermute | solution.py:25
  109.9 2.1 %collective-permute-done.42 = f32[8,128]{1,0:T(8,128)S(1)} collective-permute-done((f32[8,128]{1,0:T(8,128)S(1)}, f32[8,128]{1,0:T(8,128)S(1)}, u32[]{:S(2)}, u32[]{:S(2)}) %collective-permute-start.42) | collective-permute-done | bytes 4128 | tf_op jit(solution)/shard_map/ppermute | solution.py:25
  111.9 1.5 %collective-permute-done.43 = f32[8,128]{1,0:T(8,128)S(1)} collective-permute-done((f32[8,128]{1,0:T(8,128)S(1)}, f32[8,128]{1,0:T(8,128)S(1)}, u32[]{:S(2)}, u32[]{:S(2)}) %collective-permute-start.43) | collective-permute-done | bytes 4128 | tf_op jit(solution)/shard_map/ppermute | solution.py:25
  (93 shorter events, 33.7 us)
Async XLA Ops:
  0.6 8.1 %collective-permute-start.1 = (bf16[128,768]{1,0:T(8,128)(2,1)}, bf16[128,768]{1,0:T(8,128)(2,1)S(1)}, u32[]{:S(2)}, u32[]{:S(2)}) collective-permute-start(bf16[128,768]{1,0:T(8,128)(2,1)} %refs_2_.1), channel_id=1, source_target_pairs={{0,2},{1,3},{2,0},{3,1},{4,6},{5,7},{6,4},{7,5},{8,10},{9,11},{10,... | collective-permute-start | bytes 589832 | tf_op jit(solution)/shard_map/ppermute | solution.py:25
  3.7 10.9 %collective-permute-start = (bf16[128,768]{1,0:T(8,128)(2,1)}, bf16[128,768]{1,0:T(8,128)(2,1)S(1)}, u32[]{:S(2)}, u32[]{:S(2)}) collective-permute-start(bf16[128,768]{1,0:T(8,128)(2,1)} %refs_2_.1), channel_id=1, source_target_pairs={{0,1},{1,0},{2,3},{3,2},{4,5},{5,4},{6,7},{7,6},{8,9},{9,8},{10,11... | collective-permute-start | bytes 589832 | tf_op jit(solution)/shard_map/ppermute | solution.py:25
  8.8 6.8 %collective-permute-start.2 = (bf16[128,768]{1,0:T(8,128)(2,1)S(1)}, bf16[128,768]{1,0:T(8,128)(2,1)S(1)}, u32[]{:S(2)}, u32[]{:S(2)}) collective-permute-start(bf16[128,768]{1,0:T(8,128)(2,1)S(1)} %collective-permute-done.1.refs_8_), channel_id=1, source_target_pairs={{0,1},{1,0},{2,3},{3,2},{4,5},{5,4},{6,7},{7,6},{8,9},{9,8},{10,11... | collective-permute-start | bytes 589832 | tf_op jit(solution)/shard_map/ppermute | solution.py:25
  17.3 7.3 %collective-permute-start.8 = (bf16[128,256]{1,0:T(8,128)(2,1)S(1)}, bf16[128,256]{1,0:T(8,128)(2,1)S(1)}, u32[]{:S(2)}, u32[]{:S(2)}) collective-permute-start(bf16[128,256]{1,0:T(8,128)(2,1)S(1)} %get-tuple-element.102), channel_id=1, source_target_pairs={{0,24},{4,28},{8,16},{12,20},{16,8},{20,12},{24,0},{28,4},{1,25},{... | collective-permute-start | bytes 196616 | tf_op jit(solution)/shard_map/ppermute | solution.py:25
  21.1 7.8 %collective-permute-start.9 = (bf16[128,256]{1,0:T(8,128)(2,1)S(1)}, bf16[128,256]{1,0:T(8,128)(2,1)S(1)}, u32[]{:S(2)}, u32[]{:S(2)}) collective-permute-start(bf16[128,256]{1,0:T(8,128)(2,1)S(1)} %get-tuple-element.103), channel_id=1, source_target_pairs={{0,16},{4,20},{8,24},{12,28},{16,0},{20,4},{24,8},{28,12},{1,17},{... | collective-permute-start | bytes 196616 | tf_op jit(solution)/shard_map/ppermute | solution.py:25
  21.1 8.3 %collective-permute-start.3 = (bf16[128,384]{1,0:T(8,128)(2,1)S(1)}, bf16[128,384]{1,0:T(8,128)(2,1)S(1)}, u32[]{:S(2)}, u32[]{:S(2)}) collective-permute-start(bf16[128,384]{1,0:T(8,128)(2,1)S(1)} %get-tuple-element.95), channel_id=1, source_target_pairs={{0,4},{4,0},{8,12},{12,8},{16,20},{20,16},{24,28},{28,24},{1,5},{5... | collective-permute-start | bytes 294920 | tf_op jit(solution)/shard_map/ppermute | solution.py:25
  22.6 6.8 %collective-permute-start.4 = (bf16[128,384]{1,0:T(8,128)(2,1)S(1)}, bf16[128,384]{1,0:T(8,128)(2,1)S(1)}, u32[]{:S(2)}, u32[]{:S(2)}) collective-permute-start(bf16[128,384]{1,0:T(8,128)(2,1)S(1)} %get-tuple-element.96), channel_id=1, source_target_pairs={{0,8},{4,12},{8,0},{12,4},{16,24},{20,28},{24,16},{28,20},{1,9},{5... | collective-permute-start | bytes 294920 | tf_op jit(solution)/shard_map/ppermute | solution.py:25
  23.4 7.9 %collective-permute-start.5 = (bf16[128,384]{1,0:T(8,128)(2,1)S(1)}, bf16[128,384]{1,0:T(8,128)(2,1)S(1)}, u32[]{:S(2)}, u32[]{:S(2)}) collective-permute-start(bf16[128,384]{1,0:T(8,128)(2,1)S(1)} %get-tuple-element.97), channel_id=1, source_target_pairs={{0,12},{4,8},{8,4},{12,0},{16,28},{20,24},{24,20},{28,16},{1,13},{... | collective-permute-start | bytes 294920 | tf_op jit(solution)/shard_map/ppermute | solution.py:25
  24.6 9.0 %collective-permute-start.6 = (bf16[128,256]{1,0:T(8,128)(2,1)S(1)}, bf16[128,256]{1,0:T(8,128)(2,1)S(1)}, u32[]{:S(2)}, u32[]{:S(2)}) collective-permute-start(bf16[128,256]{1,0:T(8,128)(2,1)S(1)} %get-tuple-element.98), channel_id=1, source_target_pairs={{0,28},{4,24},{8,20},{12,16},{16,12},{20,8},{24,4},{28,0},{1,29},{... | collective-permute-start | bytes 196616 | tf_op jit(solution)/shard_map/ppermute | solution.py:25
  28.9 6.5 %collective-permute-start.7 = (bf16[128,256]{1,0:T(8,128)(2,1)S(1)}, bf16[128,256]{1,0:T(8,128)(2,1)S(1)}, u32[]{:S(2)}, u32[]{:S(2)}) collective-permute-start(bf16[128,256]{1,0:T(8,128)(2,1)S(1)} %get-tuple-element.99), channel_id=1, source_target_pairs={{0,20},{4,16},{8,28},{12,24},{16,4},{20,0},{24,12},{28,8},{1,21},{... | collective-permute-start | bytes 196616 | tf_op jit(solution)/shard_map/ppermute | solution.py:25
  36.8 4.0 %collective-permute-start.10 = (bf16[128,128]{1,0:T(8,128)(2,1)S(1)}, bf16[128,128]{1,0:T(8,128)(2,1)S(1)}, u32[]{:S(2)}, u32[]{:S(2)}) collective-permute-start(bf16[128,128]{1,0:T(8,128)(2,1)S(1)} %get-tuple-element.109), channel_id=1, source_target_pairs={{0,4},{4,0},{8,12},{12,8},{16,20},{20,16},{24,28},{28,24},{1,5},{5... | collective-permute-start | bytes 98312 | tf_op jit(solution)/shard_map/ppermute | solution.py:25
  38.2 4.8 %collective-permute-start.12 = (bf16[128,128]{1,0:T(8,128)(2,1)S(1)}, bf16[128,128]{1,0:T(8,128)(2,1)S(1)}, u32[]{:S(2)}, u32[]{:S(2)}) collective-permute-start(bf16[128,128]{1,0:T(8,128)(2,1)S(1)} %get-tuple-element.111), channel_id=1, source_target_pairs={{0,12},{4,8},{8,4},{12,0},{16,28},{20,24},{24,20},{28,16},{1,13},{... | collective-permute-start | bytes 98312 | tf_op jit(solution)/shard_map/ppermute | solution.py:25
  45.0 7.8 %collective-permute-start.16 = (bf16[128,768]{1,0:T(8,128)(2,1)S(1)}, bf16[128,768]{1,0:T(8,128)(2,1)S(1)}, u32[]{:S(2)}, u32[]{:S(2)}) collective-permute-start(bf16[128,768]{1,0:T(8,128)(2,1)S(1)} %shard_map.138.refs_10_), channel_id=1, source_target_pairs={{0,2},{1,3},{2,0},{3,1},{4,6},{5,7},{6,4},{7,5},{8,10},{9,11},{10,... | collective-permute-start | bytes 589832 | tf_op jit(solution)/shard_map/ppermute | solution.py:25
  46.6 9.6 %collective-permute-start.19 = (bf16[128,768]{1,0:T(8,128)(2,1)S(1)}, bf16[128,768]{1,0:T(8,128)(2,1)S(1)}, u32[]{:S(2)}, u32[]{:S(2)}) collective-permute-start(bf16[128,768]{1,0:T(8,128)(2,1)S(1)} %shard_map.136.refs_2_.near0), channel_id=1, source_target_pairs={{0,2},{1,3},{2,0},{3,1},{4,6},{5,7},{6,4},{7,5},{8,10},{9,11},{10,... | collective-permute-start | bytes 589832 | tf_op jit(solution)/shard_map/ppermute | solution.py:25
  47.2 9.0 %collective-permute-start.14 = (bf16[128,768]{1,0:T(8,128)(2,1)S(1)}, bf16[128,768]{1,0:T(8,128)(2,1)S(1)}, u32[]{:S(2)}, u32[]{:S(2)}) collective-permute-start(bf16[128,768]{1,0:T(8,128)(2,1)S(1)} %shard_map.136.refs_2_.near0), channel_id=1, source_target_pairs={{0,1},{1,0},{2,3},{3,2},{4,5},{5,4},{6,7},{7,6},{8,9},{9,8},{10,11... | collective-permute-start | bytes 589832 | tf_op jit(solution)/shard_map/ppermute | solution.py:25
  52.9 4.5 %collective-permute-start.18 = (bf16[128,768]{1,0:T(8,128)(2,1)S(1)}, bf16[128,768]{1,0:T(8,128)(2,1)S(1)}, u32[]{:S(2)}, u32[]{:S(2)}) collective-permute-start(bf16[128,768]{1,0:T(8,128)(2,1)S(1)} %shard_map.138.refs_10_), channel_id=1, source_target_pairs={{0,1},{1,0},{2,3},{3,2},{4,5},{5,4},{6,7},{7,6},{8,9},{9,8},{10,11... | collective-permute-start | bytes 589832 | tf_op jit(solution)/shard_map/ppermute | solution.py:25
  59.5 7.0 %collective-permute-start.26 = (bf16[128,256]{1,0:T(8,128)(2,1)S(1)}, bf16[128,256]{1,0:T(8,128)(2,1)S(1)}, u32[]{:S(2)}, u32[]{:S(2)}) collective-permute-start(bf16[128,256]{1,0:T(8,128)(2,1)S(1)} %get-tuple-element.130), channel_id=1, source_target_pairs={{0,24},{4,28},{8,16},{12,20},{16,8},{20,12},{24,0},{28,4},{1,25},{... | collective-permute-start | bytes 196616 | tf_op jit(solution)/shard_map/ppermute | solution.py:25
  61.7 7.7 %collective-permute-start.27 = (bf16[128,256]{1,0:T(8,128)(2,1)S(1)}, bf16[128,256]{1,0:T(8,128)(2,1)S(1)}, u32[]{:S(2)}, u32[]{:S(2)}) collective-permute-start(bf16[128,256]{1,0:T(8,128)(2,1)S(1)} %get-tuple-element.131), channel_id=1, source_target_pairs={{0,16},{4,20},{8,24},{12,28},{16,0},{20,4},{24,8},{28,12},{1,17},{... | collective-permute-start | bytes 196616 | tf_op jit(solution)/shard_map/ppermute | solution.py:25
  62.9 8.4 %collective-permute-start.21 = (bf16[128,384]{1,0:T(8,128)(2,1)S(1)}, bf16[128,384]{1,0:T(8,128)(2,1)S(1)}, u32[]{:S(2)}, u32[]{:S(2)}) collective-permute-start(bf16[128,384]{1,0:T(8,128)(2,1)S(1)} %get-tuple-element.125), channel_id=1, source_target_pairs={{0,4},{4,0},{8,12},{12,8},{16,20},{20,16},{24,28},{28,24},{1,5},{5... | collective-permute-start | bytes 294920 | tf_op jit(solution)/shard_map/ppermute | solution.py:25
  63.5 7.8 %collective-permute-start.22 = (bf16[128,384]{1,0:T(8,128)(2,1)S(1)}, bf16[128,384]{1,0:T(8,128)(2,1)S(1)}, u32[]{:S(2)}, u32[]{:S(2)}) collective-permute-start(bf16[128,384]{1,0:T(8,128)(2,1)S(1)} %get-tuple-element.126), channel_id=1, source_target_pairs={{0,8},{4,12},{8,0},{12,4},{16,24},{20,28},{24,16},{28,20},{1,9},{5... | collective-permute-start | bytes 294920 | tf_op jit(solution)/shard_map/ppermute | solution.py:25
  64.8 7.9 %collective-permute-start.23 = (bf16[128,384]{1,0:T(8,128)(2,1)S(1)}, bf16[128,384]{1,0:T(8,128)(2,1)S(1)}, u32[]{:S(2)}, u32[]{:S(2)}) collective-permute-start(bf16[128,384]{1,0:T(8,128)(2,1)S(1)} %get-tuple-element.127), channel_id=1, source_target_pairs={{0,12},{4,8},{8,4},{12,0},{16,28},{20,24},{24,20},{28,16},{1,13},{... | collective-permute-start | bytes 294920 | tf_op jit(solution)/shard_map/ppermute | solution.py:25
  66.4 7.7 %collective-permute-start.24 = (bf16[128,256]{1,0:T(8,128)(2,1)S(1)}, bf16[128,256]{1,0:T(8,128)(2,1)S(1)}, u32[]{:S(2)}, u32[]{:S(2)}) collective-permute-start(bf16[128,256]{1,0:T(8,128)(2,1)S(1)} %get-tuple-element.128), channel_id=1, source_target_pairs={{0,28},{4,24},{8,20},{12,16},{16,12},{20,8},{24,4},{28,0},{1,29},{... | collective-permute-start | bytes 196616 | tf_op jit(solution)/shard_map/ppermute | solution.py:25
  69.5 7.4 %collective-permute-start.25 = (bf16[128,256]{1,0:T(8,128)(2,1)S(1)}, bf16[128,256]{1,0:T(8,128)(2,1)S(1)}, u32[]{:S(2)}, u32[]{:S(2)}) collective-permute-start(bf16[128,256]{1,0:T(8,128)(2,1)S(1)} %get-tuple-element.129), channel_id=1, source_target_pairs={{0,20},{4,16},{8,28},{12,24},{16,4},{20,0},{24,12},{28,8},{1,21},{... | collective-permute-start | bytes 196616 | tf_op jit(solution)/shard_map/ppermute | solution.py:25
  78.3 4.5 %collective-permute-start.28 = (bf16[128,128]{1,0:T(8,128)(2,1)S(1)}, bf16[128,128]{1,0:T(8,128)(2,1)S(1)}, u32[]{:S(2)}, u32[]{:S(2)}) collective-permute-start(bf16[128,128]{1,0:T(8,128)(2,1)S(1)} %get-tuple-element.136), channel_id=1, source_target_pairs={{0,4},{4,0},{8,12},{12,8},{16,20},{20,16},{24,28},{28,24},{1,5},{5... | collective-permute-start | bytes 98312 | tf_op jit(solution)/shard_map/ppermute | solution.py:25
  79.4 4.8 %collective-permute-start.30 = (bf16[128,128]{1,0:T(8,128)(2,1)S(1)}, bf16[128,128]{1,0:T(8,128)(2,1)S(1)}, u32[]{:S(2)}, u32[]{:S(2)}) collective-permute-start(bf16[128,128]{1,0:T(8,128)(2,1)S(1)} %get-tuple-element.138), channel_id=1, source_target_pairs={{0,12},{4,8},{8,4},{12,0},{16,28},{20,24},{24,20},{28,16},{1,13},{... | collective-permute-start | bytes 98312 | tf_op jit(solution)/shard_map/ppermute | solution.py:25
  85.2 7.8 %collective-permute-start.36 = (bf16[128,768]{1,0:T(8,128)(2,1)S(1)}, bf16[128,768]{1,0:T(8,128)(2,1)S(1)}, u32[]{:S(2)}, u32[]{:S(2)}) collective-permute-start(bf16[128,768]{1,0:T(8,128)(2,1)S(1)} %shard_map.149), channel_id=1, source_target_pairs={{0,2},{1,3},{2,0},{3,1},{4,6},{5,7},{6,4},{7,5},{8,10},{9,11},{10,... | collective-permute-start | bytes 589832 | tf_op jit(solution)/shard_map/ppermute | solution.py:25
  87.2 6.6 %collective-permute-start.31 = (bf16[128,768]{1,0:T(8,128)(2,1)S(1)}, bf16[128,768]{1,0:T(8,128)(2,1)S(1)}, u32[]{:S(2)}, u32[]{:S(2)}) collective-permute-start(bf16[128,768]{1,0:T(8,128)(2,1)S(1)} %get-tuple-element.140), channel_id=1, source_target_pairs={{0,1},{1,0},{2,3},{3,2},{4,5},{5,4},{6,7},{7,6},{8,9},{9,8},{10,11... | collective-permute-start | bytes 589832 | tf_op jit(solution)/shard_map/ppermute | solution.py:25
  87.4 9.0 %collective-permute-start.33 = (bf16[128,768]{1,0:T(8,128)(2,1)S(1)}, bf16[128,768]{1,0:T(8,128)(2,1)S(1)}, u32[]{:S(2)}, u32[]{:S(2)}) collective-permute-start(bf16[128,768]{1,0:T(8,128)(2,1)S(1)} %shard_map.146), channel_id=1, source_target_pairs={{0,2},{1,3},{2,0},{3,1},{4,6},{5,7},{6,4},{7,5},{8,10},{9,11},{10,... | collective-permute-start | bytes 589832 | tf_op jit(solution)/shard_map/ppermute | solution.py:25
  100.9 4.5 %collective-permute-start.40 = (f32[8,128]{1,0:T(8,128)S(1)}, f32[8,128]{1,0:T(8,128)S(1)}, u32[]{:S(2)}, u32[]{:S(2)}) collective-permute-start(f32[8,128]{1,0:T(8,128)S(1)} %add.21), channel_id=1, source_target_pairs={{0,6},{1,7},{2,4},{3,5},{4,2},{5,3},{6,0},{7,1},{8,14},{9,15},{10,... | collective-permute-start | bytes 12296 | tf_op jit(solution)/shard_map/ppermute | solution.py:658
  105.4 4.5 %collective-permute-start.41 = (f32[8,128]{1,0:T(8,128)S(1)}, f32[8,128]{1,0:T(8,128)S(1)}, u32[]{:S(2)}, u32[]{:S(2)}) collective-permute-start(f32[8,128]{1,0:T(8,128)S(1)} %add_add_fusion.1), channel_id=1, source_target_pairs={{0,8},{4,12},{8,0},{12,4},{16,24},{20,28},{24,16},{28,20},{1,9},{5... | collective-permute-start | bytes 12296 | tf_op jit(solution)/shard_map/ppermute | solution.py:25
  107.4 4.5 %collective-permute-start.42 = (f32[8,128]{1,0:T(8,128)S(1)}, f32[8,128]{1,0:T(8,128)S(1)}, u32[]{:S(2)}, u32[]{:S(2)}) collective-permute-start(f32[8,128]{1,0:T(8,128)S(1)} %add_add_fusion.1), channel_id=1, source_target_pairs={{0,16},{4,20},{8,24},{12,28},{16,0},{20,4},{24,8},{28,12},{1,17},{... | collective-permute-start | bytes 12296 | tf_op jit(solution)/shard_map/ppermute | solution.py:25
  108.0 5.4 %collective-permute-start.43 = (f32[8,128]{1,0:T(8,128)S(1)}, f32[8,128]{1,0:T(8,128)S(1)}, u32[]{:S(2)}, u32[]{:S(2)}) collective-permute-start(f32[8,128]{1,0:T(8,128)S(1)} %add_add_fusion.1), channel_id=1, source_target_pairs={{0,24},{4,28},{8,16},{12,20},{16,8},{20,12},{24,0},{28,4},{1,25},{... | collective-permute-start | bytes 12296 | tf_op jit(solution)/shard_map/ppermute | solution.py:25
  (17 other events, 110.7 us)
